TPU v7x, 256 devices: a whole 4x4x8 slice. The times are simulated.
256 devices in a mesh: band: 64 (over x, y, z_hi, core), chan: 4 (over z_lo).
Axes of the slice: x: 4, y: 4, z: 8 (z_hi: 2, z_lo: 4; z = z_hi * 4 + z_lo), core: 2. Of those that a mesh axis runs over, the one named last changes fastest.
Arguments:
- cells_next: bfloat16 [131072, 1024], P('band', 'chan'), may hold values from -6 to 6
- node_embed: bfloat16 [16384, 1024], P('band', 'chan'), may hold values from -6 to 6
- enc_mix: bfloat16 [1024, 1024], P(None, 'chan'), may hold values from -0.1875 to 0.1875
- out_cotangent: bfloat16 [131072, 1024], P('band', 'chan'), may hold values from -16 to 16
- decoded_saved: bfloat16 [131072, 1024], P('band', 'chan'), may hold values from -6 to 6
- dec_proj: bfloat16 [1024, 1024], P(None, 'chan'), may hold values from -0.1875 to 0.1875
- tile_source: int32 [128, 16], replicated, may hold values from 0 to 1023, as said below
- tile_codes: int32 [128, 16, 128, 128], P('band'), may hold values from 0 to 65535
Outputs:
- hidden_nodes: bfloat16 [16384, 1024], P('band', 'chan')
- node_grad: bfloat16 [16384, 1024], P('band', 'chan')
- w_dec_grad: float32 [1024, 1024], P('band', 'chan')
Inputs may be any that keep to these rules, and one draw needn't show every extreme that they name: `tile_source`: each entry is a cell block; cell block c lies in band c // 16 and node block n in band n // 2. The cell blocks of a node block's tiles lie within 3 bands of its own. Of the 32 tiles of one band's node blocks, exactly 8 read that band itself and at most 8 read any other one band.
All inputs are finite; a program needn't handle non-finite values.
Results may differ from a plain program's by a relative error of at most 0.0049.
Values may be sent and summed in bfloat16 or wider, within the bound.
No kernel may reach another device: no remote copies, remote signals or barrier semaphores. Data moves between devices by JAX's collectives and lax.ppermute only.
A program may use at most 64 MiB of HBM per device.

v0:
```python
import functools

import jax
import jax.numpy as jnp
from jax import lax
from jax.experimental import pallas as pl
from jax.experimental.pallas import tpu as pltpu
from jax.sharding import PartitionSpec as P


BLK = 128
K = 16
CB_DEV = 16
NB_DEV = 2
CAP = 8
CHAN = 4
TILES = NB_DEV * K
PAIR_BLOCKS = 2 * CB_DEV
SIDE = 2 * CAP


def permute(x, move, bands):
    pairs = []
    for band in range(bands):
        for chan in range(CHAN):
            to_band, to_chan = move(band, chan)
            if 0 <= to_band < bands:
                pairs.append((band * CHAN + chan, to_band * CHAN + to_chan))
    return lax.ppermute(x, ("band", "chan"), pairs)


def far_step(band):
    return 2 if band % 2 == 0 else -2


def slot_table(tile_source, readers, offsets):
    bands = tile_source.shape[0] // NB_DEV
    rows = tile_source.reshape(bands, TILES)[jnp.clip(readers, 0, bands - 1)]
    hit = (rows // PAIR_BLOCKS - (readers // 2)[:, None]) == offsets[:, None]
    earlier = jnp.tril(jnp.ones((TILES, TILES), jnp.int32), -1)
    rank = jnp.sum(hit.astype(jnp.int32)[:, None, :] * earlier[None], axis=2)
    code = (jnp.arange(TILES, dtype=jnp.int32) * PAIR_BLOCKS)[None] + rows % PAIR_BLOCKS + 1
    chosen = hit[:, None, :] & (rank[:, None, :] == jnp.arange(SIDE, dtype=jnp.int32)[None, :, None])
    packed = jnp.sum(jnp.where(chosen, code[:, None, :], 0), axis=2) - 1
    tile = jnp.where(packed < 0, -1, packed // PAIR_BLOCKS)
    block = jnp.where(packed < 0, 0, packed % PAIR_BLOCKS)
    return tile, block


def pick_kernel(pick, codes, *refs):
    outs, sems = refs[:-1], refs[-1]
    places = [(out, i) for out in outs for i in range(out.shape[0])]
    copies = [
        pltpu.make_async_copy(codes.at[pick[slot]], out.at[i], sems.at[slot])
        for slot, (out, i) in enumerate(places)
    ]
    for copy in copies:
        copy.start()
    for copy in copies:
        copy.wait()


def pick_tiles(pick, codes, counts):
    return pl.pallas_call(
        pick_kernel,
        out_shape=[jax.ShapeDtypeStruct((count, BLK, BLK), codes.dtype) for count in counts],
        in_specs=[pl.BlockSpec(memory_space=pltpu.SMEM), pl.BlockSpec(memory_space=pl.ANY)],
        out_specs=[pl.BlockSpec(memory_space=pltpu.VMEM)] * len(counts),
        scratch_shapes=[pltpu.SemaphoreType.DMA((sum(counts),))],
        cost_estimate=pl.CostEstimate(flops=10**8, bytes_accessed=2 * sum(counts) * BLK * BLK * 4, transcendentals=0),
        name="pick_tiles",
    )(pick, codes)


def products_kernel(groups, n_codes, *refs):
    meta = refs[0]
    codes = refs[1 : 1 + n_codes]
    cells_own, cells_sib, cot_own, cot_sib = refs[1 + n_codes : 5 + n_codes]
    outs = refs[5 + n_codes : 5 + n_codes + len(groups)]
    code_buf, cell_buf, cot_buf, total, sems = refs[5 + n_codes + len(groups) :]
    for parts in groups:
        for operand, first, count in parts:
            source = codes[operand]

            def begin(i, carry, first=first, source=source):
                slot = first + i
                pltpu.make_async_copy(source.at[meta[3, slot]], code_buf.at[slot], sems.at[0, slot]).start()
                local = meta[2, slot]

                @pl.when(meta[1, slot] == 1)
                def _():
                    pltpu.make_async_copy(cells_own.at[local], cell_buf.at[slot], sems.at[1, slot]).start()
                    pltpu.make_async_copy(cot_own.at[local], cot_buf.at[slot], sems.at[2, slot]).start()

                @pl.when(meta[1, slot] != 1)
                def _():
                    pltpu.make_async_copy(cells_sib.at[local], cell_buf.at[slot], sems.at[1, slot]).start()
                    pltpu.make_async_copy(cot_sib.at[local], cot_buf.at[slot], sems.at[2, slot]).start()

                return carry

            lax.fori_loop(0, count, begin, 0)

    for out, parts in zip(outs, groups):
        total[...] = jnp.zeros_like(total)
        first = parts[0][1]
        slots = sum(count for _, _, count in parts)

        def step(i, carry, first=first):
            enc_rows, dec_rows = [[], []], [[], []]
            base = first + i * 4
            for inner in range(4):
                slot = base + inner
                pltpu.make_async_copy(codes[0].at[0], code_buf.at[slot], sems.at[0, slot]).wait()
                pltpu.make_async_copy(cells_own.at[0], cell_buf.at[slot], sems.at[1, slot]).wait()
                pltpu.make_async_copy(cot_own.at[0], cot_buf.at[slot], sems.at[2, slot]).wait()
                words = code_buf[slot]
                enc = ((words & 255) - 128).astype(jnp.float32)
                dec = ((words >> 8) - 128).astype(jnp.float32)
                for node in range(NB_DEV):
                    keep = (meta[0, slot] == node).astype(jnp.float32)
                    enc_rows[node].append((enc * keep).astype(jnp.bfloat16))
                    dec_rows[node].append((dec * keep).astype(jnp.bfloat16))
            wide = [
                jnp.concatenate([jnp.concatenate(line, axis=1) for line in both], axis=0)
                for both in (enc_rows, dec_rows)
            ]
            cells = cell_buf[pl.ds(base, 4)].reshape(4 * BLK, -1)
            cots = cot_buf[pl.ds(base, 4)].reshape(4 * BLK, -1)
            total[0] += jnp.dot(wide[0], cells, preferred_element_type=jnp.float32)
            total[1] += jnp.dot(wide[1], cots, preferred_element_type=jnp.float32)
            return carry

        lax.fori_loop(0, slots // 4, step, 0)
        out[...] = total[...].astype(out.dtype)


def tile_products(meta, codes, blocks, groups, dtypes):
    slots = meta.shape[1]
    channels = blocks[0].shape[-1]
    flops = slots * 4 * BLK * BLK * channels
    moved = slots * (BLK * BLK * 4 + 2 * BLK * channels * 2)
    return pl.pallas_call(
        functools.partial(products_kernel, groups, len(codes)),
        out_shape=[jax.ShapeDtypeStruct((2, NB_DEV * BLK, channels), dtype) for dtype in dtypes],
        in_specs=[pl.BlockSpec(memory_space=pltpu.SMEM)]
        + [pl.BlockSpec(memory_space=pl.ANY)] * (len(codes) + 4),
        out_specs=[pl.BlockSpec(memory_space=pltpu.VMEM)] * len(dtypes),
        scratch_shapes=[
            pltpu.VMEM((slots, BLK, BLK), jnp.int32),
            pltpu.VMEM((slots, BLK, channels), jnp.bfloat16),
            pltpu.VMEM((slots, BLK, channels), jnp.bfloat16),
            pltpu.VMEM((2, NB_DEV * BLK, channels), jnp.float32),
            pltpu.SemaphoreType.DMA((3, slots)),
        ],
        cost_estimate=pl.CostEstimate(flops=flops, bytes_accessed=moved, transcendentals=0),
        name="tile_products",
    )(meta, *codes, *blocks)


def project_kernel(chan_ref, p0, p1, p2, p3, enc_mix, dec_proj, node_embed, hidden, node_grad):
    chan = chan_ref[0]
    mixed = None
    for back, piece in enumerate((p0, p1, p2, p3)):
        rows = pl.ds(pl.multiple_of(((chan + CHAN - back) % CHAN) * 256, 256), 256)
        left = jnp.dot(piece[0], enc_mix[rows, :], preferred_element_type=jnp.float32)
        right = jnp.dot(piece[1], dec_proj[rows, :], preferred_element_type=jnp.float32)
        mixed, grad = (left, right) if mixed is None else (mixed + left, grad + right)
    hidden[...] = (node_embed[...].astype(jnp.float32) + mixed / (1.0 + jnp.exp(-mixed))).astype(hidden.dtype)
    node_grad[...] = grad.astype(node_grad.dtype)


def project(chan, pieces, enc_mix, dec_proj, node_embed):
    rows, channels = node_embed.shape
    vmem = pl.BlockSpec(memory_space=pltpu.VMEM)
    return pl.pallas_call(
        project_kernel,
        out_shape=[jax.ShapeDtypeStruct((rows, channels), jnp.bfloat16)] * 2,
        in_specs=[pl.BlockSpec(memory_space=pltpu.SMEM)] + [vmem] * 7,
        out_specs=[vmem] * 2,
        cost_estimate=pl.CostEstimate(
            flops=4 * rows * CHAN * channels * channels,
            bytes_accessed=4 * CHAN * rows * channels * 4,
            transcendentals=rows * channels,
        ),
        name="project",
    )(chan.reshape(1), *pieces, enc_mix, dec_proj, node_embed)


def near_step(band):
    return 1 - 2 * (band // 2 % 2)


def one_device(
    cells_next, node_embed, enc_mix, out_cotangent, decoded_saved, dec_proj, tile_source, tile_codes
):
    bands = lax.axis_size("band")
    band = lax.axis_index("band")
    chan = lax.axis_index("chan")
    core = band % 2
    tile_scale = (3.0 / (K * BLK)) ** 0.5 / 128.0
    channels = cells_next.shape[1]
    go = functools.partial(permute, bands=bands)
    codes = tile_codes.reshape(TILES, BLK, BLK)
    cells = cells_next.reshape(CB_DEV, BLK, channels)
    cotangent = out_cotangent.reshape(CB_DEV, BLK, channels)
    quarter = SIDE // CHAN

    cells_sib = go(cells, lambda b, c: (b ^ 1, c))
    cotangent_sib = go(cotangent, lambda b, c: (b ^ 1, c))

    near = near_step(band)
    far = far_step_traced(core)
    readers = band + jnp.array([0, 0, 0, 0, 2, -2, 0], jnp.int32) * near + jnp.array([0] * 6 + [2], jnp.int32) * far
    offsets = (
        jnp.array([1, -1, 0, 0, -1, 1, 0], jnp.int32) * near + jnp.array([0, 0, -1, 0, 0, 0, -1], jnp.int32) * far
    )
    tile, block = slot_table(tile_source, readers, offsets)

    wanted = lax.dynamic_slice_in_dim(tile[:2], (CHAN - 1 - chan) * quarter, quarter, 1)
    pick = jnp.maximum(jnp.concatenate([wanted.reshape(-1), tile[2, :CAP]]), 0)
    keep_codes, give_codes, far_codes = pick_tiles(pick, codes, (quarter, quarter, CAP))
    give_codes = go(give_codes, lambda b, c: (b - 2 * near_step(b), CHAN - 1 - c))
    keep_codes = go(keep_codes, lambda b, c: (b ^ 2, CHAN - 1 - c))
    far_codes = go(far_codes, lambda b, c: (b - 2 * far_step(b), c))

    def over_chan(x):
        return [x] + [go(x, lambda b, c, by=by: (b, (c + by) % CHAN)) for by in range(1, CHAN)]

    give_codes = over_chan(give_codes)
    keep_codes = over_chan(keep_codes)

    cot_pair = go(out_cotangent, lambda b, c: (b, c ^ 1))
    dec_pair = go(decoded_saved, lambda b, c: (b, c ^ 2))

    def meta_of(row, index):
        node = jnp.where(tile[row] < 0, NB_DEV, tile[row] // K)
        own = (block[row] // CB_DEV == core).astype(jnp.int32)
        return jnp.stack([node, own, block[row] % CB_DEV, index])

    def pieces_meta(row):
        meta = meta_of(row, jnp.arange(SIDE, dtype=jnp.int32) % quarter)
        double = jnp.concatenate([meta, meta], axis=1)
        parts = [
            lax.dynamic_slice_in_dim(double, (chan + CHAN - i) * quarter, quarter, 1) for i in range(CHAN)
        ]
        return jnp.concatenate(parts, axis=1)

    blocks = (cells, cells_sib, cotangent, cotangent_sib)
    piece_group = [[(i, i * quarter, quarter) for i in range(CHAN)]]
    near_meta = jnp.concatenate(
        [meta_of(6, jnp.arange(SIDE, dtype=jnp.int32))[:, :CAP], meta_of(3, jnp.maximum(tile[3], 0))], axis=1
    )
    far_part, own_part = tile_products(
        near_meta, [far_codes, codes], blocks, [[(0, 0, CAP)], [(1, CAP, SIDE)]], [jnp.bfloat16, jnp.float32]
    )
    got_far = go(far_part, lambda b, c: (b + 2 * far_step(b), c))
    (give_part,) = tile_products(pieces_meta(5), give_codes, blocks, piece_group, [jnp.bfloat16])
    got_give = go(give_part, lambda b, c: (b - 4 * near_step(b), c))
    (keep_part,) = tile_products(pieces_meta(4), keep_codes, blocks, piece_group, [jnp.float32])
    crossing = (keep_part + got_give.astype(jnp.float32)).astype(jnp.bfloat16)
    got_keep = go(crossing, lambda b, c: (b ^ 2, c))
    summed = own_part + got_keep.astype(jnp.float32) + got_far.astype(jnp.float32)
    aggregates = (summed * tile_scale).astype(jnp.bfloat16)
    pieces = over_chan(aggregates)
    hidden_nodes, node_grad = project(chan, pieces, enc_mix, dec_proj, node_embed)

    w_dec_grad = projection_gradient(go, out_cotangent, decoded_saved, cot_pair, dec_pair, bands)
    return (hidden_nodes, node_grad, w_dec_grad)


def far_step_traced(core):
    return 2 - 4 * core


def projection_gradient(go, cot, dec, cot_pair, dec_pair, bands):
    band, chan = lax.axis_index("band"), lax.axis_index("chan")
    along = bands // 16
    x, y, zh, core = band // (4 * along), band // along % 4, band // 2 % 2, band % 2
    channels = cot.shape[1]
    cells_total = cot.shape[0] * bands
    rows = channels // 16

    def outer(left, right):
        return lax.dot_general(left, right, (((0,), (0,)), ((), ())), preferred_element_type=jnp.float32)

    whole = jnp.stack([outer(cot, dec), outer(cot_pair, dec), outer(cot, dec_pair), outer(cot_pair, dec_pair)])
    halves = whole.reshape(4, 8, 2, rows, channels)
    own = lax.dynamic_index_in_dim(halves, core, 2, keepdims=False)
    other = lax.dynamic_index_in_dim(halves, 1 - core, 2, keepdims=False).astype(jnp.bfloat16)
    own = own + go(other, lambda b, c: (b ^ 1, c)).astype(jnp.float32)

    def take(i):
        return lax.dynamic_index_in_dim(own, i, 0, keepdims=False)

    share = take(x ^ chan)
    for by in range(1, 4):
        sent = take(((x + by) % 4) ^ chan).astype(jnp.bfloat16)
        share = share + go(sent, lambda b, c: ((b + by * 4 * along) % bands, c)).astype(jnp.float32)

    own = share.reshape(4, 2, rows, channels)
    share = take(y)
    for by in range(1, 4):
        sent = take((y + by) % 4)
        share = share + go(sent, lambda b, c: (b // 16 * 16 + (b % 16 + by * 4) % 16, c))

    def home(b, c):
        at_x, rest = b // 16, b % 16
        return (2 * (c // 2) + at_x % 2) * 16 + rest, c % 2 + 2 * (at_x // 2)

    def home_across(b, c):
        return home(b ^ 2, c)

    own = share
    return (go(take(zh), home) + go(take(1 - zh), home_across)) * cells_total ** (-0.5)


def solution(mesh):
    in_specs = (
        P("band", "chan"),
        P("band", "chan"),
        P(None, "chan"),
        P("band", "chan"),
        P("band", "chan"),
        P(None, "chan"),
        P(),
        P("band", None, None, None),
    )
    out_specs = (P("band", "chan"), P("band", "chan"), P("band", "chan"))
    return jax.shard_map(one_device, mesh=mesh, in_specs=in_specs, out_specs=out_specs, check_vma=False)
```

profile of v0, /device:TPU:5, one launch (start us, length us, event | category | flops | bytes accessed | tf_op | source)
XLA Modules:
  0.0 184.1 jit_solution(4346517982416274309)
XLA Ops:
  0.7 1.7 collective-permute-start.17
  2.4 3.0 %collective-permute-start.18 = (bf16[2048,256]{1,0:T(8,128)(2,1)}, bf16[2048,256]{1,0:T(8,128)(2,1)}, u32[]{:S(2)}, u32[]{:S(2)}) collective-permute-start(bf16[2048,256]{1,0:T(8,128)(2,1)} %param.16), channel_id=1, source_target_pairs={{0,2},{1,3},{2,0},{3,1},{4,6},{5,7},{6,4},{7,5},{8,10},{9,11},{10,... | collective-permute-start | bytes 3145736 | tf_op jit(solution)/shard_map/ppermute | solution.py:29
  9.6 3.4 %pick_tiles.1 = (s32[4,128,128]{2,1,0:T(8,128)}, s32[4,128,128]{2,1,0:T(8,128)}, s32[8,128,128]{2,1,0:T(8,128)}) custom-call(s32[16]{0:T(128)} %add_maximum_fusion.pick, s32[32,128,128]{2,1,0:T(8,128)} %bitcast.60), custom_call_target="tpu_custom_call" | custom-call | flops 100000000 | bytes 2097152 | tf_op jit(solution)/shard_map/pick_tiles/pallas_call | solution.py:64
  13.0 6.8 %collective-permute-start.7 = (s32[4,128,128]{2,1,0:T(8,128)}, s32[4,128,128]{2,1,0:T(8,128)S(1)}, u32[]{:S(2)}, u32[]{:S(2)}) collective-permute-start(s32[4,128,128]{2,1,0:T(8,128)} %get-tuple-element.13), channel_id=1, source_target_pairs={{8,19},{9,18},{10,17},{11,16},{12,23},{13,22},{14,21},{15,20},{16,... | collective-permute-start | bytes 786440 | tf_op jit(solution)/shard_map/ppermute | solution.py:29
  19.9 1.6 collective-permute-start.1
  23.3 1.7 fusion.28
  25.0 22.7 %collective-permute-done.17 = bf16[2048,256]{1,0:T(8,128)(2,1)} collective-permute-done((bf16[2048,256]{1,0:T(8,128)(2,1)}, bf16[2048,256]{1,0:T(8,128)(2,1)}, u32[]{:S(2)}, u32[]{:S(2)}) %collective-permute-start.17) | collective-permute-done | bytes 1048608 | tf_op jit(solution)/shard_map/ppermute | solution.py:29
  47.7 4.9 %collective-permute-start.3 = (s32[4,128,128]{2,1,0:T(8,128)S(1)}, s32[4,128,128]{2,1,0:T(8,128)}, u32[]{:S(2)}, u32[]{:S(2)}) collective-permute-start(s32[4,128,128]{2,1,0:T(8,128)S(1)} %copy-done.16), channel_id=1, source_target_pairs={{0,11},{1,10},{2,9},{3,8},{4,15},{5,14},{6,13},{7,12},{8,3},{9,2},... | collective-permute-start | bytes 786440 | tf_op jit(solution)/shard_map/ppermute | solution.py:29
  52.6 1.7 fusion.29
  54.3 3.2 %collective-permute-start = (s32[8,128,128]{2,1,0:T(8,128)}, s32[8,128,128]{2,1,0:T(8,128)}, u32[]{:S(2)}, u32[]{:S(2)}) collective-permute-start(s32[8,128,128]{2,1,0:T(8,128)} %get-tuple-element.10), channel_id=1, source_target_pairs={{4,20},{5,21},{6,22},{7,23},{12,28},{13,29},{14,30},{15,31},{16,0}... | collective-permute-start | bytes 1572872 | tf_op jit(solution)/shard_map/ppermute | solution.py:29
  57.6 2.2 %collective-permute-start.10 = (s32[4,128,128]{2,1,0:T(8,128)S(1)}, s32[4,128,128]{2,1,0:T(8,128)S(1)}, u32[]{:S(2)}, u32[]{:S(2)}) collective-permute-start(s32[4,128,128]{2,1,0:T(8,128)S(1)} %collective-permute-done.7.refs_1_), channel_id=1, source_target_pairs={{0,3},{1,0},{2,1},{3,2},{4,7},{5,4},{6,5},{7,6},{8,11},{9,8},{10,9... | collective-permute-start | bytes 786440 | tf_op jit(solution)/shard_map/ppermute | solution.py:29
  59.8 2.0 %fusion.31 = f32[256,256]{1,0:T(8,128)S(1)} fusion(bf16[2048,256]{1,0:T(8,128)(2,1)} %collective-permute-done.17, bf16[2048,256]{1,0:T(8,128)(2,1)} %collective-permute-done.18), kind=kOutput, calls=%fused_computation.135 | convolution fusion | flops 268435456 | bytes 2359296 | tf_op jit(solution)/shard_map/dot_general | solution.py:285
  61.8 7.8 %collective-permute-done.3.refs_1_ = s32[4,128,128]{2,1,0:T(8,128)} collective-permute-done((s32[4,128,128]{2,1,0:T(8,128)S(1)}, s32[4,128,128]{2,1,0:T(8,128)}, u32[]{:S(2)}, u32[]{:S(2)}) %collective-permute-start.3) | collective-permute-done | bytes 262176 | tf_op jit(solution)/shard_map/ppermute | solution.py:29
  69.6 2.4 %collective-permute-start.9 = (s32[4,128,128]{2,1,0:T(8,128)S(1)}, s32[4,128,128]{2,1,0:T(8,128)S(1)}, u32[]{:S(2)}, u32[]{:S(2)}) collective-permute-start(s32[4,128,128]{2,1,0:T(8,128)S(1)} %collective-permute-done.7.refs_1_), channel_id=1, source_target_pairs={{0,2},{1,3},{2,0},{3,1},{4,6},{5,7},{6,4},{7,5},{8,10},{9,11},{10,... | collective-permute-start | bytes 786440 | tf_op jit(solution)/shard_map/ppermute | solution.py:29
  72.0 1.7 fusion.30
  74.7 3.6 %collective-permute-done.8.refs_2_ = s32[4,128,128]{2,1,0:T(8,128)S(1)} collective-permute-done((s32[4,128,128]{2,1,0:T(8,128)S(1)}, s32[4,128,128]{2,1,0:T(8,128)S(1)}, u32[]{:S(2)}, u32[]{:S(2)}) %collective-permute-start.8) | collective-permute-done | bytes 262176 | tf_op jit(solution)/shard_map/ppermute | solution.py:29
  78.3 22.2 %collective-permute-done.9.refs_3_ = s32[4,128,128]{2,1,0:T(8,128)S(1)} collective-permute-done((s32[4,128,128]{2,1,0:T(8,128)S(1)}, s32[4,128,128]{2,1,0:T(8,128)S(1)}, u32[]{:S(2)}, u32[]{:S(2)}) %collective-permute-start.9) | collective-permute-done | bytes 262176 | tf_op jit(solution)/shard_map/ppermute | solution.py:29
  102.7 4.8 %tile_products.5 = bf16[2,256,256]{2,1,0:T(8,128)(2,1)} custom-call(s32[4,16]{1,0:T(4,128)} %pad_add_fusion.6.refs_0_, s32[4,128,128]{2,1,0:T(8,128)} %copy-done.8, s32[4,128,128]{2,1,0:T(8,128)} %copy-done.10, s32[4,128,128]{2,1,0:T(8,128)} %copy-done.11, s32[4,128,128]{2,1,0:T(8,128)} %copy-done.9, bf16[16,128,256]{2,1,0:T(8,128)(2,1)} %bitcast.56, ...), custom_call_target="tpu_custom_call" | custom-call | flops 268435456 | bytes 3145728 | tf_op jit(solution)/shard_map/tile_products/pallas_call | solution.py:143
  107.5 5.4 %collective-permute-start.11 = (bf16[2,256,256]{2,1,0:T(8,128)(2,1)}, bf16[2,256,256]{2,1,0:T(8,128)(2,1)S(1)}, u32[]{:S(2)}, u32[]{:S(2)}) collective-permute-start(bf16[2,256,256]{2,1,0:T(8,128)(2,1)} %tile_products.5), channel_id=1, source_target_pairs={{8,24},{9,25},{10,26},{11,27},{12,28},{13,29},{14,30},{15,31},{16,... | collective-permute-start | bytes 786440 | tf_op jit(solution)/shard_map/ppermute | solution.py:29
  112.9 5.8 %tile_products.3 = (bf16[2,256,256]{2,1,0:T(8,128)(2,1)}, f32[2,256,256]{2,1,0:T(8,128)}) custom-call(s32[4,24]{1,0:T(4,128)} %add_add_fusion.refs_0_, s32[8,128,128]{2,1,0:T(8,128)} %collective-permute-done.refs_1_, s32[32,128,128]{2,1,0:T(8,128)} %bitcast.61, bf16[16,128,256]{2,1,0:T(8,128)(2,1)} %bitcast.57, bf16[16,128,256]{2,1,0:T(8,128)(2,1)} %copy-done.2, ...), custom_call_target="tpu_custom_call" | custom-call | flops 402653184 | bytes 4718592 | tf_op jit(solution)/shard_map/tile_products/pallas_call | solution.py:143
  118.7 2.4 %collective-permute-start.13 = (bf16[2,256,256]{2,1,0:T(8,128)(2,1)}, bf16[2,256,256]{2,1,0:T(8,128)(2,1)S(1)}, u32[]{:S(2)}, u32[]{:S(2)}) collective-permute-start(bf16[2,256,256]{2,1,0:T(8,128)(2,1)} %get-tuple-element.14), channel_id=1, source_target_pairs={{0,16},{1,17},{2,18},{3,19},{8,24},{9,25},{10,26},{11,27},{16,32},... | collective-permute-start | bytes 786440 | tf_op jit(solution)/shard_map/ppermute | solution.py:29
  121.9 5.0 %tile_products.4 = f32[2,256,256]{2,1,0:T(8,128)} custom-call(s32[4,16]{1,0:T(4,128)} %pad_add_fusion.5.refs_0_, s32[4,128,128]{2,1,0:T(8,128)} %collective-permute-done.3.refs_1_, s32[4,128,128]{2,1,0:T(8,128)} %collective-permute-done.4.refs_2_, s32[4,128,128]{2,1,0:T(8,128)} %collective-permute-done.5.refs_3_, s32[4,128,128]{2,1,0:T(8,128)} %copy-done.15, ...), custom_call_target="tpu_custom_call" | custom-call | flops 268435456 | bytes 3145728 | tf_op jit(solution)/shard_map/tile_products/pallas_call | solution.py:143
  130.7 2.4 %collective-permute-start.12 = (bf16[2,256,256]{2,1,0:T(8,128)(2,1)S(1)}, bf16[2,256,256]{2,1,0:T(8,128)(2,1)S(1)}, u32[]{:S(2)}, u32[]{:S(2)}) collective-permute-start(bf16[2,256,256]{2,1,0:T(8,128)(2,1)S(1)} %add_convert_fusion), channel_id=1, source_target_pairs={{0,8},{1,9},{2,10},{3,11},{4,12},{5,13},{6,14},{7,15},{8,0},{9,1},... | collective-permute-start | bytes 786440 | tf_op jit(solution)/shard_map/ppermute | solution.py:29
  133.2 2.4 %collective-permute-start.23 = (f32[2,16,256]{2,1,0:T(8,128)S(1)}, f32[2,16,256]{2,1,0:T(8,128)S(1)}, u32[]{:S(2)}, u32[]{:S(2)}) collective-permute-start(f32[2,16,256]{2,1,0:T(8,128)S(1)} %get-tuple-element.32), channel_id=1, source_target_pairs={{0,16},{1,17},{2,18},{3,19},{4,20},{5,21},{6,22},{7,23},{8,24},{9,... | collective-permute-start | bytes 98312 | tf_op jit(solution)/shard_map/ppermute | solution.py:29
  135.9 2.3 %collective-permute-start.25 = (f32[2,16,256]{2,1,0:T(8,128)S(1)}, f32[2,16,256]{2,1,0:T(8,128)S(1)}, u32[]{:S(2)}, u32[]{:S(2)}) collective-permute-start(f32[2,16,256]{2,1,0:T(8,128)S(1)} %get-tuple-element.33), channel_id=1, source_target_pairs={{0,48},{1,49},{2,50},{3,51},{4,52},{5,53},{6,54},{7,55},{8,56},{9,... | collective-permute-start | bytes 98312 | tf_op jit(solution)/shard_map/ppermute | solution.py:29
  138.1 2.1 %collective-permute-done.24 = f32[2,16,256]{2,1,0:T(8,128)S(1)} collective-permute-done((f32[2,16,256]{2,1,0:T(8,128)S(1)}, f32[2,16,256]{2,1,0:T(8,128)S(1)}, u32[]{:S(2)}, u32[]{:S(2)}) %collective-permute-start.24) | collective-permute-done | bytes 32800 | tf_op jit(solution)/shard_map/ppermute | solution.py:29
  140.6 1.6 collective-permute-start.14
  142.1 10.0 %collective-permute-start.15 = (bf16[2,256,256]{2,1,0:T(8,128)(2,1)S(1)}, bf16[2,256,256]{2,1,0:T(8,128)(2,1)S(1)}, u32[]{:S(2)}, u32[]{:S(2)}) collective-permute-start(bf16[2,256,256]{2,1,0:T(8,128)(2,1)S(1)} %multiply_convert_fusion.p0), channel_id=1, source_target_pairs={{0,2},{1,3},{2,0},{3,1},{4,6},{5,7},{6,4},{7,5},{8,10},{9,11},{10,... | collective-permute-start | bytes 786440 | tf_op jit(solution)/shard_map/ppermute | solution.py:29
  153.2 5.4 %collective-permute-start.26 = (f32[16,256]{1,0:T(8,128)S(1)}, f32[16,256]{1,0:T(8,128)S(1)}, u32[]{:S(2)}, u32[]{:S(2)}) collective-permute-start(f32[16,256]{1,0:T(8,128)S(1)} %get-tuple-element.36), channel_id=1, source_target_pairs={{0,0},{1,1},{2,128},{3,129},{4,4},{5,5},{6,132},{7,133},{8,8},{9,9... | collective-permute-start | bytes 49160 | tf_op jit(solution)/shard_map/ppermute | solution.py:29
  158.6 1.7 collective-permute-start.27
  160.2 19.6 %collective-permute-done.26 = f32[16,256]{1,0:T(8,128)S(1)} collective-permute-done((f32[16,256]{1,0:T(8,128)S(1)}, f32[16,256]{1,0:T(8,128)S(1)}, u32[]{:S(2)}, u32[]{:S(2)}) %collective-permute-start.26) | collective-permute-done | bytes 16416 | tf_op jit(solution)/shard_map/ppermute | solution.py:29
  181.4 2.7 %project.1 = (bf16[256,256]{1,0:T(8,128)(2,1)}, bf16[256,256]{1,0:T(8,128)(2,1)}) custom-call(s32[1]{0:T(128)} %bitcast.chan_ref, bf16[2,256,256]{2,1,0:T(8,128)(2,1)} %copy-done.6, bf16[2,256,256]{2,1,0:T(8,128)(2,1)} %copy-done.12, bf16[2,256,256]{2,1,0:T(8,128)(2,1)} %copy-done.13, bf16[2,256,256]{2,1,0:T(8,128)(2,1)} %copy-done.14, ...), custom_call_target="tpu_custom_call" | custom-call | flops 268435456 | bytes 4194304 | tf_op jit(solution)/shard_map/project/pallas_call | solution.py:176
  (112 shorter events, 16.8 us)
Async XLA Ops:
  0.7 47.0 %collective-permute-start.17 = (bf16[2048,256]{1,0:T(8,128)(2,1)}, bf16[2048,256]{1,0:T(8,128)(2,1)}, u32[]{:S(2)}, u32[]{:S(2)}) collective-permute-start(bf16[2048,256]{1,0:T(8,128)(2,1)} %param.15), channel_id=1, source_target_pairs={{0,1},{1,0},{2,3},{3,2},{4,5},{5,4},{6,7},{7,6},{8,9},{9,8},{10,11... | collective-permute-start | bytes 3145736 | tf_op jit(solution)/shard_map/ppermute | solution.py:29
  2.4 55.2 %collective-permute-start.18 = (bf16[2048,256]{1,0:T(8,128)(2,1)}, bf16[2048,256]{1,0:T(8,128)(2,1)}, u32[]{:S(2)}, u32[]{:S(2)}) collective-permute-start(bf16[2048,256]{1,0:T(8,128)(2,1)} %param.16), channel_id=1, source_target_pairs={{0,2},{1,3},{2,0},{3,1},{4,6},{5,7},{6,4},{7,5},{8,10},{9,11},{10,... | collective-permute-start | bytes 3145736 | tf_op jit(solution)/shard_map/ppermute | solution.py:29
  13.0 41.3 %collective-permute-start.7 = (s32[4,128,128]{2,1,0:T(8,128)}, s32[4,128,128]{2,1,0:T(8,128)S(1)}, u32[]{:S(2)}, u32[]{:S(2)}) collective-permute-start(s32[4,128,128]{2,1,0:T(8,128)} %get-tuple-element.13), channel_id=1, source_target_pairs={{8,19},{9,18},{10,17},{11,16},{12,23},{13,22},{14,21},{15,20},{16,... | collective-permute-start | bytes 786440 | tf_op jit(solution)/shard_map/ppermute | solution.py:29
  19.9 80.6 %collective-permute-start.1 = (bf16[16,128,256]{2,1,0:T(8,128)(2,1)S(1)}, bf16[16,128,256]{2,1,0:T(8,128)(2,1)S(1)}, u32[]{:S(2)}, u32[]{:S(2)}) collective-permute-start(bf16[16,128,256]{2,1,0:T(8,128)(2,1)S(1)} %bitcast.59), channel_id=1, source_target_pairs={{0,4},{1,5},{2,6},{3,7},{4,0},{5,1},{6,2},{7,3},{8,12},{9,13},{10,... | collective-permute-start | bytes 3145736 | tf_op jit(solution)/shard_map/ppermute | solution.py:29
  21.4 79.2 %collective-permute-start.2 = (bf16[16,128,256]{2,1,0:T(8,128)(2,1)S(1)}, bf16[16,128,256]{2,1,0:T(8,128)(2,1)}, u32[]{:S(2)}, u32[]{:S(2)}) collective-permute-start(bf16[16,128,256]{2,1,0:T(8,128)(2,1)S(1)} %bitcast.55), channel_id=1, source_target_pairs={{0,4},{1,5},{2,6},{3,7},{4,0},{5,1},{6,2},{7,3},{8,12},{9,13},{10,... | collective-permute-start | bytes 3145736 | tf_op jit(solution)/shard_map/ppermute | solution.py:29
  22.5 25.2 %copy-start.16 = (s32[4,128,128]{2,1,0:T(8,128)S(1)}, s32[4,128,128]{2,1,0:T(8,128)}, u32[]{:S(2)}) copy-start(s32[4,128,128]{2,1,0:T(8,128)} %get-tuple-element.12) | copy-start | bytes 786436
  22.5 30.1 %copy-start.3 = (bf16[2048,256]{1,0:T(8,128)(2,1)S(1)}, bf16[2048,256]{1,0:T(8,128)(2,1)}, u32[]{:S(2)}) copy-start(bf16[2048,256]{1,0:T(8,128)(2,1)} %param.16) | copy-start | bytes 3145732
  47.7 21.9 %collective-permute-start.3 = (s32[4,128,128]{2,1,0:T(8,128)S(1)}, s32[4,128,128]{2,1,0:T(8,128)}, u32[]{:S(2)}, u32[]{:S(2)}) collective-permute-start(s32[4,128,128]{2,1,0:T(8,128)S(1)} %copy-done.16), channel_id=1, source_target_pairs={{0,11},{1,10},{2,9},{3,8},{4,15},{5,14},{6,13},{7,12},{8,3},{9,2},... | collective-permute-start | bytes 786440 | tf_op jit(solution)/shard_map/ppermute | solution.py:29
  54.3 53.1 %collective-permute-start = (s32[8,128,128]{2,1,0:T(8,128)}, s32[8,128,128]{2,1,0:T(8,128)}, u32[]{:S(2)}, u32[]{:S(2)}) collective-permute-start(s32[8,128,128]{2,1,0:T(8,128)} %get-tuple-element.10), channel_id=1, source_target_pairs={{4,20},{5,21},{6,22},{7,23},{12,28},{13,29},{14,30},{15,31},{16,0}... | collective-permute-start | bytes 1572872 | tf_op jit(solution)/shard_map/ppermute | solution.py:29
  57.6 12.0 %collective-permute-start.10 = (s32[4,128,128]{2,1,0:T(8,128)S(1)}, s32[4,128,128]{2,1,0:T(8,128)S(1)}, u32[]{:S(2)}, u32[]{:S(2)}) collective-permute-start(s32[4,128,128]{2,1,0:T(8,128)S(1)} %collective-permute-done.7.refs_1_), channel_id=1, source_target_pairs={{0,3},{1,0},{2,1},{3,2},{4,7},{5,4},{6,5},{7,6},{8,11},{9,8},{10,9... | collective-permute-start | bytes 786440 | tf_op jit(solution)/shard_map/ppermute | solution.py:29
  69.6 8.7 %collective-permute-start.8 = (s32[4,128,128]{2,1,0:T(8,128)S(1)}, s32[4,128,128]{2,1,0:T(8,128)S(1)}, u32[]{:S(2)}, u32[]{:S(2)}) collective-permute-start(s32[4,128,128]{2,1,0:T(8,128)S(1)} %collective-permute-done.7.refs_1_), channel_id=1, source_target_pairs={{0,1},{1,2},{2,3},{3,0},{4,5},{5,6},{6,7},{7,4},{8,9},{9,10},{10,1... | collective-permute-start | bytes 786440 | tf_op jit(solution)/shard_map/ppermute | solution.py:29
  69.6 30.9 %collective-permute-start.9 = (s32[4,128,128]{2,1,0:T(8,128)S(1)}, s32[4,128,128]{2,1,0:T(8,128)S(1)}, u32[]{:S(2)}, u32[]{:S(2)}) collective-permute-start(s32[4,128,128]{2,1,0:T(8,128)S(1)} %collective-permute-done.7.refs_1_), channel_id=1, source_target_pairs={{0,2},{1,3},{2,0},{3,1},{4,6},{5,7},{6,4},{7,5},{8,10},{9,11},{10,... | collective-permute-start | bytes 786440 | tf_op jit(solution)/shard_map/ppermute | solution.py:29
  73.9 26.7 %copy-start.4 = (f32[4,8,2,16,256]{4,3,2,1,0:T(8,128)}, f32[4,8,2,16,256]{4,3,2,1,0:T(8,128)S(1)}, u32[]{:S(2)}) copy-start(f32[4,8,2,16,256]{4,3,2,1,0:T(8,128)S(1)} %pad_maximum_fusion) | copy-start | bytes 3145732
  78.3 40.5 %collective-permute-start.4 = (s32[4,128,128]{2,1,0:T(8,128)}, s32[4,128,128]{2,1,0:T(8,128)}, u32[]{:S(2)}, u32[]{:S(2)}) collective-permute-start(s32[4,128,128]{2,1,0:T(8,128)} %collective-permute-done.3.refs_1_), channel_id=1, source_target_pairs={{0,1},{1,2},{2,3},{3,0},{4,5},{5,6},{6,7},{7,4},{8,9},{9,10},{10,1... | collective-permute-start | bytes 786440 | tf_op jit(solution)/shard_map/ppermute | solution.py:29
  100.5 20.7 %collective-permute-start.5 = (s32[4,128,128]{2,1,0:T(8,128)}, s32[4,128,128]{2,1,0:T(8,128)}, u32[]{:S(2)}, u32[]{:S(2)}) collective-permute-start(s32[4,128,128]{2,1,0:T(8,128)} %collective-permute-done.3.refs_1_), channel_id=1, source_target_pairs={{0,2},{1,3},{2,0},{3,1},{4,6},{5,7},{6,4},{7,5},{8,10},{9,11},{10,... | collective-permute-start | bytes 786440 | tf_op jit(solution)/shard_map/ppermute | solution.py:29
  100.5 20.7 %collective-permute-start.6 = (s32[4,128,128]{2,1,0:T(8,128)}, s32[4,128,128]{2,1,0:T(8,128)S(1)}, u32[]{:S(2)}, u32[]{:S(2)}) collective-permute-start(s32[4,128,128]{2,1,0:T(8,128)} %collective-permute-done.3.refs_1_), channel_id=1, source_target_pairs={{0,3},{1,0},{2,1},{3,2},{4,7},{5,4},{6,5},{7,6},{8,11},{9,8},{10,9... | collective-permute-start | bytes 786440 | tf_op jit(solution)/shard_map/ppermute | solution.py:29
  100.6 26.3 %collective-permute-start.19 = (bf16[4,8,16,256]{3,2,1,0:T(8,128)(2,1)}, bf16[4,8,16,256]{3,2,1,0:T(8,128)(2,1)S(1)}, u32[]{:S(2)}, u32[]{:S(2)}) collective-permute-start(bf16[4,8,16,256]{3,2,1,0:T(8,128)(2,1)} %fusion), channel_id=1, source_target_pairs={{0,4},{1,5},{2,6},{3,7},{4,0},{5,1},{6,2},{7,3},{8,12},{9,13},{10,... | collective-permute-start | bytes 786440 | tf_op jit(solution)/shard_map/ppermute | solution.py:29
  107.5 22.2 %collective-permute-start.11 = (bf16[2,256,256]{2,1,0:T(8,128)(2,1)}, bf16[2,256,256]{2,1,0:T(8,128)(2,1)S(1)}, u32[]{:S(2)}, u32[]{:S(2)}) collective-permute-start(bf16[2,256,256]{2,1,0:T(8,128)(2,1)} %tile_products.5), channel_id=1, source_target_pairs={{8,24},{9,25},{10,26},{11,27},{12,28},{13,29},{14,30},{15,31},{16,... | collective-permute-start | bytes 786440 | tf_op jit(solution)/shard_map/ppermute | solution.py:29
  118.7 21.5 %collective-permute-start.13 = (bf16[2,256,256]{2,1,0:T(8,128)(2,1)}, bf16[2,256,256]{2,1,0:T(8,128)(2,1)S(1)}, u32[]{:S(2)}, u32[]{:S(2)}) collective-permute-start(bf16[2,256,256]{2,1,0:T(8,128)(2,1)} %get-tuple-element.14), channel_id=1, source_target_pairs={{0,16},{1,17},{2,18},{3,19},{8,24},{9,25},{10,26},{11,27},{16,32},... | collective-permute-start | bytes 786440 | tf_op jit(solution)/shard_map/ppermute | solution.py:29
  127.0 6.1 %collective-permute-start.20 = (bf16[8,16,256]{2,1,0:T(8,128)(2,1)S(1)}, bf16[8,16,256]{2,1,0:T(8,128)(2,1)S(1)}, u32[]{:S(2)}, u32[]{:S(2)}) collective-permute-start(bf16[8,16,256]{2,1,0:T(8,128)(2,1)S(1)} %get-tuple-element.29), channel_id=1, source_target_pairs={{0,64},{1,65},{2,66},{3,67},{4,68},{5,69},{6,70},{7,71},{8,72},{9,... | collective-permute-start | bytes 196616 | tf_op jit(solution)/shard_map/ppermute | solution.py:29
  128.3 4.8 %collective-permute-start.21 = (bf16[8,16,256]{2,1,0:T(8,128)(2,1)S(1)}, bf16[8,16,256]{2,1,0:T(8,128)(2,1)S(1)}, u32[]{:S(2)}, u32[]{:S(2)}) collective-permute-start(bf16[8,16,256]{2,1,0:T(8,128)(2,1)S(1)} %get-tuple-element.31), channel_id=1, source_target_pairs={{0,128},{1,129},{2,130},{3,131},{4,132},{5,133},{6,134},{7,135},{8... | collective-permute-start | bytes 196616 | tf_op jit(solution)/shard_map/ppermute | solution.py:29
  128.5 4.6 %collective-permute-start.22 = (bf16[8,16,256]{2,1,0:T(8,128)(2,1)S(1)}, bf16[8,16,256]{2,1,0:T(8,128)(2,1)S(1)}, u32[]{:S(2)}, u32[]{:S(2)}) collective-permute-start(bf16[8,16,256]{2,1,0:T(8,128)(2,1)S(1)} %get-tuple-element.30), channel_id=1, source_target_pairs={{0,192},{1,193},{2,194},{3,195},{4,196},{5,197},{6,198},{7,199},{8... | collective-permute-start | bytes 196616 | tf_op jit(solution)/shard_map/ppermute | solution.py:29
  130.7 9.7 %collective-permute-start.12 = (bf16[2,256,256]{2,1,0:T(8,128)(2,1)S(1)}, bf16[2,256,256]{2,1,0:T(8,128)(2,1)S(1)}, u32[]{:S(2)}, u32[]{:S(2)}) collective-permute-start(bf16[2,256,256]{2,1,0:T(8,128)(2,1)S(1)} %add_convert_fusion), channel_id=1, source_target_pairs={{0,8},{1,9},{2,10},{3,11},{4,12},{5,13},{6,14},{7,15},{8,0},{9,1},... | collective-permute-start | bytes 786440 | tf_op jit(solution)/shard_map/ppermute | solution.py:29
  133.2 4.9 %collective-permute-start.23 = (f32[2,16,256]{2,1,0:T(8,128)S(1)}, f32[2,16,256]{2,1,0:T(8,128)S(1)}, u32[]{:S(2)}, u32[]{:S(2)}) collective-permute-start(f32[2,16,256]{2,1,0:T(8,128)S(1)} %get-tuple-element.32), channel_id=1, source_target_pairs={{0,16},{1,17},{2,18},{3,19},{4,20},{5,21},{6,22},{7,23},{8,24},{9,... | collective-permute-start | bytes 98312 | tf_op jit(solution)/shard_map/ppermute | solution.py:29
  135.6 4.6 %collective-permute-start.24 = (f32[2,16,256]{2,1,0:T(8,128)S(1)}, f32[2,16,256]{2,1,0:T(8,128)S(1)}, u32[]{:S(2)}, u32[]{:S(2)}) collective-permute-start(f32[2,16,256]{2,1,0:T(8,128)S(1)} %get-tuple-element.34), channel_id=1, source_target_pairs={{0,32},{1,33},{2,34},{3,35},{4,36},{5,37},{6,38},{7,39},{8,40},{9,... | collective-permute-start | bytes 98312 | tf_op jit(solution)/shard_map/ppermute | solution.py:29
  135.9 4.3 %collective-permute-start.25 = (f32[2,16,256]{2,1,0:T(8,128)S(1)}, f32[2,16,256]{2,1,0:T(8,128)S(1)}, u32[]{:S(2)}, u32[]{:S(2)}) collective-permute-start(f32[2,16,256]{2,1,0:T(8,128)S(1)} %get-tuple-element.33), channel_id=1, source_target_pairs={{0,48},{1,49},{2,50},{3,51},{4,52},{5,53},{6,54},{7,55},{8,56},{9,... | collective-permute-start | bytes 98312 | tf_op jit(solution)/shard_map/ppermute | solution.py:29
  140.6 40.0 %copy-start.6 = (bf16[2,256,256]{2,1,0:T(8,128)(2,1)}, bf16[2,256,256]{2,1,0:T(8,128)(2,1)S(1)}, u32[]{:S(2)}) copy-start(bf16[2,256,256]{2,1,0:T(8,128)(2,1)S(1)} %multiply_convert_fusion.p0) | copy-start | bytes 786436
  140.6 39.9 %collective-permute-start.14 = (bf16[2,256,256]{2,1,0:T(8,128)(2,1)S(1)}, bf16[2,256,256]{2,1,0:T(8,128)(2,1)S(1)}, u32[]{:S(2)}, u32[]{:S(2)}) collective-permute-start(bf16[2,256,256]{2,1,0:T(8,128)(2,1)S(1)} %multiply_convert_fusion.p0), channel_id=1, source_target_pairs={{0,1},{1,2},{2,3},{3,0},{4,5},{5,6},{6,7},{7,4},{8,9},{9,10},{10,1... | collective-permute-start | bytes 786440 | tf_op jit(solution)/shard_map/ppermute | solution.py:29
  142.1 38.4 %collective-permute-start.15 = (bf16[2,256,256]{2,1,0:T(8,128)(2,1)S(1)}, bf16[2,256,256]{2,1,0:T(8,128)(2,1)S(1)}, u32[]{:S(2)}, u32[]{:S(2)}) collective-permute-start(bf16[2,256,256]{2,1,0:T(8,128)(2,1)S(1)} %multiply_convert_fusion.p0), channel_id=1, source_target_pairs={{0,2},{1,3},{2,0},{3,1},{4,6},{5,7},{6,4},{7,5},{8,10},{9,11},{10,... | collective-permute-start | bytes 786440 | tf_op jit(solution)/shard_map/ppermute | solution.py:29
  152.1 28.4 %collective-permute-start.16 = (bf16[2,256,256]{2,1,0:T(8,128)(2,1)S(1)}, bf16[2,256,256]{2,1,0:T(8,128)(2,1)S(1)}, u32[]{:S(2)}, u32[]{:S(2)}) collective-permute-start(bf16[2,256,256]{2,1,0:T(8,128)(2,1)S(1)} %multiply_convert_fusion.p0), channel_id=1, source_target_pairs={{0,3},{1,0},{2,1},{3,2},{4,7},{5,4},{6,5},{7,6},{8,11},{9,8},{10,9... | collective-permute-start | bytes 786440 | tf_op jit(solution)/shard_map/ppermute | solution.py:29
  153.2 26.7 %collective-permute-start.26 = (f32[16,256]{1,0:T(8,128)S(1)}, f32[16,256]{1,0:T(8,128)S(1)}, u32[]{:S(2)}, u32[]{:S(2)}) collective-permute-start(f32[16,256]{1,0:T(8,128)S(1)} %get-tuple-element.36), channel_id=1, source_target_pairs={{0,0},{1,1},{2,128},{3,129},{4,4},{5,5},{6,132},{7,133},{8,8},{9,9... | collective-permute-start | bytes 49160 | tf_op jit(solution)/shard_map/ppermute | solution.py:29
  158.6 21.3 %collective-permute-start.27 = (f32[16,256]{1,0:T(8,128)S(1)}, f32[16,256]{1,0:T(8,128)S(1)}, u32[]{:S(2)}, u32[]{:S(2)}) collective-permute-start(f32[16,256]{1,0:T(8,128)S(1)} %get-tuple-element.35), channel_id=1, source_target_pairs={{0,8},{1,9},{2,136},{3,137},{4,12},{5,13},{6,140},{7,141},{8,0},{9... | collective-permute-start | bytes 49160 | tf_op jit(solution)/shard_map/ppermute | solution.py:29
  (13 other events, 115.9 us)
where the time goes:
time: 185 us; the launch traced here: 184 us
  waiting for transfers between devices  78.3 us (42%)
  starting transfers between devices  64.9 us (35%)
  Pallas kernels  21.7 us (12%)
  matrix products  7.09 us (4%)
  other arithmetic  6.81 us (4%)
  local copies, waits for them, and re-layouts  4.25 us (2%)
    ppermute x28, waiting for transfers between devices, permute(): return lax.ppermute(x, ('band', 'chan'), pairs)  78.3 us
    ppermute x28, starting transfers between devices, permute(): return lax.ppermute(x, ('band', 'chan'), pairs)  64.9 us
    pallas_call x3, Pallas kernels, tile_products(): pl.pallas_call(functools.partial(products_kernel, groups, len(codes)), ou...  15.6 us
    dot_general x4, matrix products, outer(): lax.dot_general(left, right, (((0,), (0,)), ((), ())), preferred_element_...  7.09 us
  transfers between devices with their start and end apart: 28, of which 7 were waited for; matrix products, arithmetic and copies ran while one was open for 9% of the time, Pallas kernels for 10%

commit v1 on v0

--- a/solution.py
+++ b/solution.py
@@ -230,8 +230,10 @@
     give_codes = over_chan(give_codes)
     keep_codes = over_chan(keep_codes)
 
+    half = decoded_saved.shape[0] // 2
+    dec_first = go(decoded_saved[:half], lambda b, c: (b, c ^ 2))
     cot_pair = go(out_cotangent, lambda b, c: (b, c ^ 1))
-    dec_pair = go(decoded_saved, lambda b, c: (b, c ^ 2))
+    dec_second = go(decoded_saved[half:], lambda b, c: (b, c ^ 2))
 
     def meta_of(row, index):
         node = jnp.where(tile[row] < 0, NB_DEV, tile[row] // K)
@@ -265,7 +267,7 @@
     pieces = over_chan(aggregates)
     hidden_nodes, node_grad = project(chan, pieces, enc_mix, dec_proj, node_embed)
 
-    w_dec_grad = projection_gradient(go, out_cotangent, decoded_saved, cot_pair, dec_pair, bands)
+    w_dec_grad = projection_gradient(go, out_cotangent, decoded_saved, cot_pair, (dec_first, dec_second), bands)
     return (hidden_nodes, node_grad, w_dec_grad)
 
 
@@ -284,7 +286,12 @@
     def outer(left, right):
         return lax.dot_general(left, right, (((0,), (0,)), ((), ())), preferred_element_type=jnp.float32)
 
-    whole = jnp.stack([outer(cot, dec), outer(cot_pair, dec), outer(cot, dec_pair), outer(cot_pair, dec_pair)])
+    def outer_halves(left):
+        half = left.shape[0] // 2
+        return outer(left[:half], dec_pair[0]) + outer(left[half:], dec_pair[1])
+
+    first = outer(cot, dec)
+    whole = jnp.stack([first, outer(cot_pair, dec), outer_halves(cot), outer_halves(cot_pair)])
     halves = whole.reshape(4, 8, 2, rows, channels)
     own = lax.dynamic_index_in_dim(halves, core, 2, keepdims=False)
     other = lax.dynamic_index_in_dim(halves, 1 - core, 2, keepdims=False).astype(jnp.bfloat16)

time: 185 us -> 188 us (1.016)
  local copies, waits for them, and re-layouts: 4.25 us -> 7.08 us
  matrix products: 7.09 us -> 9.25 us
    slice x0 -> x1, local copies, waits for them, and re-layouts: none -> 2.39 us  [one_device(): dec_first = go(decoded_saved[:half], lambda b, c: (b, c ^ 2))]
    dot_general x4 -> x6, matrix products: 7.09 us -> 9.25 us  [outer(): lax.dot_general(left, right, (((0,), (0,)), ((), ())), preferred_element_...]
    ppermute x28 -> x29, starting transfers between devices: 64.9 us -> 64.1 us  [permute(): return lax.ppermute(x, ('band', 'chan'), pairs)]
    ppermute x28 -> x29, waiting for transfers between devices: 78.3 us -> 78 us  [permute(): return lax.ppermute(x, ('band', 'chan'), pairs)]
  transfers between devices with their start and end apart: 28 -> 29, of which waited for: 7 -> 9; matrix products, arithmetic and copies ran while one was open for 9% -> 9% of each run, Pallas kernels for 10% -> 10%
where the time goes in v1:
time: 188 us; the launch traced here: 187 us
  waiting for transfers between devices  78 us (41%)
  starting transfers between devices  64.1 us (34%)
  Pallas kernels  21.6 us (11%)
  matrix products  9.25 us (5%)
  local copies, waits for them, and re-layouts  7.08 us (4%)
  other arithmetic  5.45 us (3%)
    ppermute x29, waiting for transfers between devices, permute(): return lax.ppermute(x, ('band', 'chan'), pairs)  78 us
    ppermute x29, starting transfers between devices, permute(): return lax.ppermute(x, ('band', 'chan'), pairs)  64.1 us
    pallas_call x3, Pallas kernels, tile_products(): pl.pallas_call(functools.partial(products_kernel, groups, len(codes)), ou...  15.5 us
    dot_general x6, matrix products, outer(): lax.dot_general(left, right, (((0,), (0,)), ((), ())), preferred_element_...  9.25 us
  transfers between devices with their start and end apart: 29, of which 9 were waited for; matrix products, arithmetic and copies ran while one was open for 9% of the time, Pallas kernels for 10%

profile of v1, /device:TPU:5, one launch (start us, length us, event | category | flops | bytes accessed | tf_op | source)
XLA Modules:
  0.0 186.7 jit_solution(16051299893433330711)
XLA Ops:
  0.7 2.4 %fusion.34 = (bf16[1024,256]{1,0:T(8,128)(2,1)}, bf16[1024,256]{1,0:T(8,128)(2,1)}) fusion(bf16[2048,256]{1,0:T(8,128)(2,1)} %param.16), kind=kLoop, calls=%fused_computation.140 | loop fusion | bytes 2097152 | tf_op jit(solution)/shard_map/slice | solution.py:234
  3.1 3.0 %collective-permute-start.19 = (bf16[1024,256]{1,0:T(8,128)(2,1)}, bf16[1024,256]{1,0:T(8,128)(2,1)}, u32[]{:S(2)}, u32[]{:S(2)}) collective-permute-start(bf16[1024,256]{1,0:T(8,128)(2,1)} %get-tuple-element.30), channel_id=1, source_target_pairs={{0,2},{1,3},{2,0},{3,1},{4,6},{5,7},{6,4},{7,5},{8,10},{9,11},{10,... | collective-permute-start | bytes 1572872 | tf_op jit(solution)/shard_map/ppermute | solution.py:29
  6.1 1.6 collective-permute-start.17
  10.0 3.4 %pick_tiles.1 = (s32[4,128,128]{2,1,0:T(8,128)}, s32[4,128,128]{2,1,0:T(8,128)}, s32[8,128,128]{2,1,0:T(8,128)}) custom-call(s32[16]{0:T(128)} %add_maximum_fusion.pick, s32[32,128,128]{2,1,0:T(8,128)} %bitcast.60), custom_call_target="tpu_custom_call" | custom-call | flops 100000000 | bytes 2097152 | tf_op jit(solution)/shard_map/pick_tiles/pallas_call | solution.py:64
  13.4 8.0 %collective-permute-start.7 = (s32[4,128,128]{2,1,0:T(8,128)}, s32[4,128,128]{2,1,0:T(8,128)S(1)}, u32[]{:S(2)}, u32[]{:S(2)}) collective-permute-start(s32[4,128,128]{2,1,0:T(8,128)} %get-tuple-element.13), channel_id=1, source_target_pairs={{8,19},{9,18},{10,17},{11,16},{12,23},{13,22},{14,21},{15,20},{16,... | collective-permute-start | bytes 786440 | tf_op jit(solution)/shard_map/ppermute | solution.py:29
  21.4 1.9 collective-permute-start.1
  25.0 1.7 fusion.35
  26.7 2.6 %collective-permute-done.19 = bf16[1024,256]{1,0:T(8,128)(2,1)} collective-permute-done((bf16[1024,256]{1,0:T(8,128)(2,1)}, bf16[1024,256]{1,0:T(8,128)(2,1)}, u32[]{:S(2)}, u32[]{:S(2)}) %collective-permute-start.19) | collective-permute-done | bytes 524320 | tf_op jit(solution)/shard_map/ppermute | solution.py:29
  29.3 2.2 %collective-permute-start.2 = (bf16[16,128,256]{2,1,0:T(8,128)(2,1)S(1)}, bf16[16,128,256]{2,1,0:T(8,128)(2,1)S(1)}, u32[]{:S(2)}, u32[]{:S(2)}) collective-permute-start(bf16[16,128,256]{2,1,0:T(8,128)(2,1)S(1)} %bitcast.55), channel_id=1, source_target_pairs={{0,4},{1,5},{2,6},{3,7},{4,0},{5,1},{6,2},{7,3},{8,12},{9,13},{10,... | collective-permute-start | bytes 3145736 | tf_op jit(solution)/shard_map/ppermute | solution.py:29
  32.9 17.9 %collective-permute-done.18 = bf16[1024,256]{1,0:T(8,128)(2,1)} collective-permute-done((bf16[1024,256]{1,0:T(8,128)(2,1)}, bf16[1024,256]{1,0:T(8,128)(2,1)}, u32[]{:S(2)}, u32[]{:S(2)}) %collective-permute-start.18) | collective-permute-done | bytes 524320 | tf_op jit(solution)/shard_map/ppermute | solution.py:29
  50.8 9.3 %collective-permute-start.3 = (s32[4,128,128]{2,1,0:T(8,128)S(1)}, s32[4,128,128]{2,1,0:T(8,128)}, u32[]{:S(2)}, u32[]{:S(2)}) collective-permute-start(s32[4,128,128]{2,1,0:T(8,128)S(1)} %copy-done.22), channel_id=1, source_target_pairs={{0,11},{1,10},{2,9},{3,8},{4,15},{5,14},{6,13},{7,12},{8,3},{9,2},... | collective-permute-start | bytes 786440 | tf_op jit(solution)/shard_map/ppermute | solution.py:29
  61.5 3.2 %collective-permute-start = (s32[8,128,128]{2,1,0:T(8,128)}, s32[8,128,128]{2,1,0:T(8,128)}, u32[]{:S(2)}, u32[]{:S(2)}) collective-permute-start(s32[8,128,128]{2,1,0:T(8,128)} %get-tuple-element.10), channel_id=1, source_target_pairs={{4,20},{5,21},{6,22},{7,23},{12,28},{13,29},{14,30},{15,31},{16,0}... | collective-permute-start | bytes 1572872 | tf_op jit(solution)/shard_map/ppermute | solution.py:29
  64.8 1.7 fusion.36
  68.0 6.0 %collective-permute-done.3.refs_1_ = s32[4,128,128]{2,1,0:T(8,128)} collective-permute-done((s32[4,128,128]{2,1,0:T(8,128)S(1)}, s32[4,128,128]{2,1,0:T(8,128)}, u32[]{:S(2)}, u32[]{:S(2)}) %collective-permute-start.3) | collective-permute-done | bytes 262176 | tf_op jit(solution)/shard_map/ppermute | solution.py:29
  77.2 6.0 %collective-permute-done.8.refs_2_ = s32[4,128,128]{2,1,0:T(8,128)S(1)} collective-permute-done((s32[4,128,128]{2,1,0:T(8,128)S(1)}, s32[4,128,128]{2,1,0:T(8,128)S(1)}, u32[]{:S(2)}, u32[]{:S(2)}) %collective-permute-start.8) | collective-permute-done | bytes 262176 | tf_op jit(solution)/shard_map/ppermute | solution.py:29
  83.2 21.7 %collective-permute-done.9.refs_3_ = s32[4,128,128]{2,1,0:T(8,128)S(1)} collective-permute-done((s32[4,128,128]{2,1,0:T(8,128)S(1)}, s32[4,128,128]{2,1,0:T(8,128)S(1)}, u32[]{:S(2)}, u32[]{:S(2)}) %collective-permute-start.9) | collective-permute-done | bytes 262176 | tf_op jit(solution)/shard_map/ppermute | solution.py:29
  108.1 4.8 %tile_products.5 = bf16[2,256,256]{2,1,0:T(8,128)(2,1)} custom-call(s32[4,16]{1,0:T(4,128)} %pad_add_fusion.6.refs_0_, s32[4,128,128]{2,1,0:T(8,128)} %copy-done.9, s32[4,128,128]{2,1,0:T(8,128)} %copy-done.11, s32[4,128,128]{2,1,0:T(8,128)} %copy-done.12, s32[4,128,128]{2,1,0:T(8,128)} %copy-done.10, bf16[16,128,256]{2,1,0:T(8,128)(2,1)} %bitcast.56, ...), custom_call_target="tpu_custom_call" | custom-call | flops 268435456 | bytes 3145728 | tf_op jit(solution)/shard_map/tile_products/pallas_call | solution.py:143
  112.9 4.8 %collective-permute-start.11 = (bf16[2,256,256]{2,1,0:T(8,128)(2,1)}, bf16[2,256,256]{2,1,0:T(8,128)(2,1)S(1)}, u32[]{:S(2)}, u32[]{:S(2)}) collective-permute-start(bf16[2,256,256]{2,1,0:T(8,128)(2,1)} %tile_products.5), channel_id=1, source_target_pairs={{8,24},{9,25},{10,26},{11,27},{12,28},{13,29},{14,30},{15,31},{16,... | collective-permute-start | bytes 786440 | tf_op jit(solution)/shard_map/ppermute | solution.py:29
  117.7 5.9 %tile_products.3 = (bf16[2,256,256]{2,1,0:T(8,128)(2,1)}, f32[2,256,256]{2,1,0:T(8,128)}) custom-call(s32[4,24]{1,0:T(4,128)} %add_add_fusion.refs_0_, s32[8,128,128]{2,1,0:T(8,128)} %collective-permute-done.refs_1_, s32[32,128,128]{2,1,0:T(8,128)} %bitcast.61, bf16[16,128,256]{2,1,0:T(8,128)(2,1)} %bitcast.57, bf16[16,128,256]{2,1,0:T(8,128)(2,1)} %copy-done.2, ...), custom_call_target="tpu_custom_call" | custom-call | flops 402653184 | bytes 4718592 | tf_op jit(solution)/shard_map/tile_products/pallas_call | solution.py:143
  123.6 2.5 %collective-permute-start.13 = (bf16[2,256,256]{2,1,0:T(8,128)(2,1)}, bf16[2,256,256]{2,1,0:T(8,128)(2,1)S(1)}, u32[]{:S(2)}, u32[]{:S(2)}) collective-permute-start(bf16[2,256,256]{2,1,0:T(8,128)(2,1)} %get-tuple-element.14), channel_id=1, source_target_pairs={{0,16},{1,17},{2,18},{3,19},{8,24},{9,25},{10,26},{11,27},{16,32},... | collective-permute-start | bytes 786440 | tf_op jit(solution)/shard_map/ppermute | solution.py:29
  126.8 4.8 %tile_products.4 = f32[2,256,256]{2,1,0:T(8,128)} custom-call(s32[4,16]{1,0:T(4,128)} %pad_add_fusion.5.refs_0_, s32[4,128,128]{2,1,0:T(8,128)} %collective-permute-done.3.refs_1_, s32[4,128,128]{2,1,0:T(8,128)} %collective-permute-done.4.refs_2_, s32[4,128,128]{2,1,0:T(8,128)} %collective-permute-done.5.refs_3_, s32[4,128,128]{2,1,0:T(8,128)} %copy-done.16, ...), custom_call_target="tpu_custom_call" | custom-call | flops 268435456 | bytes 3145728 | tf_op jit(solution)/shard_map/tile_products/pallas_call | solution.py:143
  131.8 1.6 collective-permute-start.21
  138.1 2.2 %collective-permute-start.24 = (f32[2,16,256]{2,1,0:T(8,128)S(1)}, f32[2,16,256]{2,1,0:T(8,128)S(1)}, u32[]{:S(2)}, u32[]{:S(2)}) collective-permute-start(f32[2,16,256]{2,1,0:T(8,128)S(1)} %get-tuple-element.34), channel_id=1, source_target_pairs={{0,16},{1,17},{2,18},{3,19},{4,20},{5,21},{6,22},{7,23},{8,24},{9,... | collective-permute-start | bytes 98312 | tf_op jit(solution)/shard_map/ppermute | solution.py:29
  140.3 2.5 %collective-permute-start.26 = (f32[2,16,256]{2,1,0:T(8,128)S(1)}, f32[2,16,256]{2,1,0:T(8,128)S(1)}, u32[]{:S(2)}, u32[]{:S(2)}) collective-permute-start(f32[2,16,256]{2,1,0:T(8,128)S(1)} %get-tuple-element.35), channel_id=1, source_target_pairs={{0,48},{1,49},{2,50},{3,51},{4,52},{5,53},{6,54},{7,55},{8,56},{9,... | collective-permute-start | bytes 98312 | tf_op jit(solution)/shard_map/ppermute | solution.py:29
  142.8 2.1 %collective-permute-done.25 = f32[2,16,256]{2,1,0:T(8,128)S(1)} collective-permute-done((f32[2,16,256]{2,1,0:T(8,128)S(1)}, f32[2,16,256]{2,1,0:T(8,128)S(1)}, u32[]{:S(2)}, u32[]{:S(2)}) %collective-permute-start.25) | collective-permute-done | bytes 32800 | tf_op jit(solution)/shard_map/ppermute | solution.py:29
  144.9 1.7 collective-permute-done.12
  147.7 8.3 %collective-permute-start.15 = (bf16[2,256,256]{2,1,0:T(8,128)(2,1)S(1)}, bf16[2,256,256]{2,1,0:T(8,128)(2,1)S(1)}, u32[]{:S(2)}, u32[]{:S(2)}) collective-permute-start(bf16[2,256,256]{2,1,0:T(8,128)(2,1)S(1)} %multiply_convert_fusion.p0), channel_id=1, source_target_pairs={{0,2},{1,3},{2,0},{3,1},{4,6},{5,7},{6,4},{7,5},{8,10},{9,11},{10,... | collective-permute-start | bytes 786440 | tf_op jit(solution)/shard_map/ppermute | solution.py:29
  156.0 2.3 %collective-permute-start.16 = (bf16[2,256,256]{2,1,0:T(8,128)(2,1)S(1)}, bf16[2,256,256]{2,1,0:T(8,128)(2,1)S(1)}, u32[]{:S(2)}, u32[]{:S(2)}) collective-permute-start(bf16[2,256,256]{2,1,0:T(8,128)(2,1)S(1)} %multiply_convert_fusion.p0), channel_id=1, source_target_pairs={{0,3},{1,0},{2,1},{3,2},{4,7},{5,4},{6,5},{7,6},{8,11},{9,8},{10,9... | collective-permute-start | bytes 786440 | tf_op jit(solution)/shard_map/ppermute | solution.py:29
  158.3 3.0 %collective-permute-start.27 = (f32[16,256]{1,0:T(8,128)S(1)}, f32[16,256]{1,0:T(8,128)S(1)}, u32[]{:S(2)}, u32[]{:S(2)}) collective-permute-start(f32[16,256]{1,0:T(8,128)S(1)} %get-tuple-element.38), channel_id=1, source_target_pairs={{0,0},{1,1},{2,128},{3,129},{4,4},{5,5},{6,132},{7,133},{8,8},{9,9... | collective-permute-start | bytes 49160 | tf_op jit(solution)/shard_map/ppermute | solution.py:29
  161.3 2.6 %collective-permute-start.28 = (f32[16,256]{1,0:T(8,128)S(1)}, f32[16,256]{1,0:T(8,128)S(1)}, u32[]{:S(2)}, u32[]{:S(2)}) collective-permute-start(f32[16,256]{1,0:T(8,128)S(1)} %get-tuple-element.37), channel_id=1, source_target_pairs={{0,8},{1,9},{2,136},{3,137},{4,12},{5,13},{6,140},{7,141},{8,0},{9... | collective-permute-start | bytes 49160 | tf_op jit(solution)/shard_map/ppermute | solution.py:29
  163.8 18.6 %collective-permute-done.27 = f32[16,256]{1,0:T(8,128)S(1)} collective-permute-done((f32[16,256]{1,0:T(8,128)S(1)}, f32[16,256]{1,0:T(8,128)S(1)}, u32[]{:S(2)}, u32[]{:S(2)}) %collective-permute-start.27) | collective-permute-done | bytes 16416 | tf_op jit(solution)/shard_map/ppermute | solution.py:29
  184.1 2.7 %project.1 = (bf16[256,256]{1,0:T(8,128)(2,1)}, bf16[256,256]{1,0:T(8,128)(2,1)}) custom-call(s32[1]{0:T(128)} %bitcast.chan_ref, bf16[2,256,256]{2,1,0:T(8,128)(2,1)} %copy-done.7, bf16[2,256,256]{2,1,0:T(8,128)(2,1)} %copy-done.13, bf16[2,256,256]{2,1,0:T(8,128)(2,1)} %copy-done.14, bf16[2,256,256]{2,1,0:T(8,128)(2,1)} %copy-done.15, ...), custom_call_target="tpu_custom_call" | custom-call | flops 268435456 | bytes 4194304 | tf_op jit(solution)/shard_map/project/pallas_call | solution.py:176
  (129 shorter events, 22.7 us)
Async XLA Ops:
  3.1 26.2 %collective-permute-start.19 = (bf16[1024,256]{1,0:T(8,128)(2,1)}, bf16[1024,256]{1,0:T(8,128)(2,1)}, u32[]{:S(2)}, u32[]{:S(2)}) collective-permute-start(bf16[1024,256]{1,0:T(8,128)(2,1)} %get-tuple-element.30), channel_id=1, source_target_pairs={{0,2},{1,3},{2,0},{3,1},{4,6},{5,7},{6,4},{7,5},{8,10},{9,11},{10,... | collective-permute-start | bytes 1572872 | tf_op jit(solution)/shard_map/ppermute | solution.py:29
  6.1 58.6 %collective-permute-start.17 = (bf16[2048,256]{1,0:T(8,128)(2,1)S(1)}, bf16[2048,256]{1,0:T(8,128)(2,1)}, u32[]{:S(2)}, u32[]{:S(2)}) collective-permute-start(bf16[2048,256]{1,0:T(8,128)(2,1)S(1)} %copy-done), channel_id=1, source_target_pairs={{0,1},{1,0},{2,3},{3,2},{4,5},{5,4},{6,7},{7,6},{8,9},{9,8},{10,11... | collective-permute-start | bytes 3145736 | tf_op jit(solution)/shard_map/ppermute | solution.py:29
  7.7 43.0 %collective-permute-start.18 = (bf16[1024,256]{1,0:T(8,128)(2,1)}, bf16[1024,256]{1,0:T(8,128)(2,1)}, u32[]{:S(2)}, u32[]{:S(2)}) collective-permute-start(bf16[1024,256]{1,0:T(8,128)(2,1)} %get-tuple-element.29), channel_id=1, source_target_pairs={{0,2},{1,3},{2,0},{3,1},{4,6},{5,7},{6,4},{7,5},{8,10},{9,11},{10,... | collective-permute-start | bytes 1572872 | tf_op jit(solution)/shard_map/ppermute | solution.py:29
  13.4 48.0 %collective-permute-start.7 = (s32[4,128,128]{2,1,0:T(8,128)}, s32[4,128,128]{2,1,0:T(8,128)S(1)}, u32[]{:S(2)}, u32[]{:S(2)}) collective-permute-start(s32[4,128,128]{2,1,0:T(8,128)} %get-tuple-element.13), channel_id=1, source_target_pairs={{8,19},{9,18},{10,17},{11,16},{12,23},{13,22},{14,21},{15,20},{16,... | collective-permute-start | bytes 786440 | tf_op jit(solution)/shard_map/ppermute | solution.py:29
  21.4 83.5 %collective-permute-start.1 = (bf16[16,128,256]{2,1,0:T(8,128)(2,1)S(1)}, bf16[16,128,256]{2,1,0:T(8,128)(2,1)S(1)}, u32[]{:S(2)}, u32[]{:S(2)}) collective-permute-start(bf16[16,128,256]{2,1,0:T(8,128)(2,1)S(1)} %bitcast.59), channel_id=1, source_target_pairs={{0,4},{1,5},{2,6},{3,7},{4,0},{5,1},{6,2},{7,3},{8,12},{9,13},{10,... | collective-permute-start | bytes 3145736 | tf_op jit(solution)/shard_map/ppermute | solution.py:29
  26.7 38.0 %copy-start.4 = (bf16[2048,256]{1,0:T(8,128)(2,1)S(1)}, bf16[2048,256]{1,0:T(8,128)(2,1)}, u32[]{:S(2)}) copy-start(bf16[2048,256]{1,0:T(8,128)(2,1)} %param.16) | copy-start | bytes 3145732
  29.3 75.7 %collective-permute-start.2 = (bf16[16,128,256]{2,1,0:T(8,128)(2,1)S(1)}, bf16[16,128,256]{2,1,0:T(8,128)(2,1)S(1)}, u32[]{:S(2)}, u32[]{:S(2)}) collective-permute-start(bf16[16,128,256]{2,1,0:T(8,128)(2,1)S(1)} %bitcast.55), channel_id=1, source_target_pairs={{0,4},{1,5},{2,6},{3,7},{4,0},{5,1},{6,2},{7,3},{8,12},{9,13},{10,... | collective-permute-start | bytes 3145736 | tf_op jit(solution)/shard_map/ppermute | solution.py:29
  50.8 23.2 %collective-permute-start.3 = (s32[4,128,128]{2,1,0:T(8,128)S(1)}, s32[4,128,128]{2,1,0:T(8,128)}, u32[]{:S(2)}, u32[]{:S(2)}) collective-permute-start(s32[4,128,128]{2,1,0:T(8,128)S(1)} %copy-done.22), channel_id=1, source_target_pairs={{0,11},{1,10},{2,9},{3,8},{4,15},{5,14},{6,13},{7,12},{8,3},{9,2},... | collective-permute-start | bytes 786440 | tf_op jit(solution)/shard_map/ppermute | solution.py:29
  61.5 51.5 %collective-permute-start = (s32[8,128,128]{2,1,0:T(8,128)}, s32[8,128,128]{2,1,0:T(8,128)}, u32[]{:S(2)}, u32[]{:S(2)}) collective-permute-start(s32[8,128,128]{2,1,0:T(8,128)} %get-tuple-element.10), channel_id=1, source_target_pairs={{4,20},{5,21},{6,22},{7,23},{12,28},{13,29},{14,30},{15,31},{16,0}... | collective-permute-start | bytes 1572872 | tf_op jit(solution)/shard_map/ppermute | solution.py:29
  64.7 9.3 %collective-permute-start.10 = (s32[4,128,128]{2,1,0:T(8,128)S(1)}, s32[4,128,128]{2,1,0:T(8,128)S(1)}, u32[]{:S(2)}, u32[]{:S(2)}) collective-permute-start(s32[4,128,128]{2,1,0:T(8,128)S(1)} %collective-permute-done.7.refs_1_), channel_id=1, source_target_pairs={{0,3},{1,0},{2,1},{3,2},{4,7},{5,4},{6,5},{7,6},{8,11},{9,8},{10,9... | collective-permute-start | bytes 786440 | tf_op jit(solution)/shard_map/ppermute | solution.py:29
  74.0 9.2 %collective-permute-start.8 = (s32[4,128,128]{2,1,0:T(8,128)S(1)}, s32[4,128,128]{2,1,0:T(8,128)S(1)}, u32[]{:S(2)}, u32[]{:S(2)}) collective-permute-start(s32[4,128,128]{2,1,0:T(8,128)S(1)} %collective-permute-done.7.refs_1_), channel_id=1, source_target_pairs={{0,1},{1,2},{2,3},{3,0},{4,5},{5,6},{6,7},{7,4},{8,9},{9,10},{10,1... | collective-permute-start | bytes 786440 | tf_op jit(solution)/shard_map/ppermute | solution.py:29
  74.0 30.9 %collective-permute-start.9 = (s32[4,128,128]{2,1,0:T(8,128)S(1)}, s32[4,128,128]{2,1,0:T(8,128)S(1)}, u32[]{:S(2)}, u32[]{:S(2)}) collective-permute-start(s32[4,128,128]{2,1,0:T(8,128)S(1)} %collective-permute-done.7.refs_1_), channel_id=1, source_target_pairs={{0,2},{1,3},{2,0},{3,1},{4,6},{5,7},{6,4},{7,5},{8,10},{9,11},{10,... | collective-permute-start | bytes 786440 | tf_op jit(solution)/shard_map/ppermute | solution.py:29
  76.4 31.0 %copy-start.5 = (f32[4,8,2,16,256]{4,3,2,1,0:T(8,128)}, f32[4,8,2,16,256]{4,3,2,1,0:T(8,128)S(1)}, u32[]{:S(2)}) copy-start(f32[4,8,2,16,256]{4,3,2,1,0:T(8,128)S(1)} %pad_maximum_fusion) | copy-start | bytes 3145732
  83.2 40.3 %collective-permute-start.4 = (s32[4,128,128]{2,1,0:T(8,128)}, s32[4,128,128]{2,1,0:T(8,128)}, u32[]{:S(2)}, u32[]{:S(2)}) collective-permute-start(s32[4,128,128]{2,1,0:T(8,128)} %collective-permute-done.3.refs_1_), channel_id=1, source_target_pairs={{0,1},{1,2},{2,3},{3,0},{4,5},{5,6},{6,7},{7,4},{8,9},{9,10},{10,1... | collective-permute-start | bytes 786440 | tf_op jit(solution)/shard_map/ppermute | solution.py:29
  104.9 21.2 %collective-permute-start.5 = (s32[4,128,128]{2,1,0:T(8,128)}, s32[4,128,128]{2,1,0:T(8,128)}, u32[]{:S(2)}, u32[]{:S(2)}) collective-permute-start(s32[4,128,128]{2,1,0:T(8,128)} %collective-permute-done.3.refs_1_), channel_id=1, source_target_pairs={{0,2},{1,3},{2,0},{3,1},{4,6},{5,7},{6,4},{7,5},{8,10},{9,11},{10,... | collective-permute-start | bytes 786440 | tf_op jit(solution)/shard_map/ppermute | solution.py:29
  104.9 21.2 %collective-permute-start.6 = (s32[4,128,128]{2,1,0:T(8,128)}, s32[4,128,128]{2,1,0:T(8,128)S(1)}, u32[]{:S(2)}, u32[]{:S(2)}) collective-permute-start(s32[4,128,128]{2,1,0:T(8,128)} %collective-permute-done.3.refs_1_), channel_id=1, source_target_pairs={{0,3},{1,0},{2,1},{3,2},{4,7},{5,4},{6,5},{7,6},{8,11},{9,8},{10,9... | collective-permute-start | bytes 786440 | tf_op jit(solution)/shard_map/ppermute | solution.py:29
  106.1 25.6 %collective-permute-start.20 = (bf16[4,8,16,256]{3,2,1,0:T(8,128)(2,1)}, bf16[4,8,16,256]{3,2,1,0:T(8,128)(2,1)S(1)}, u32[]{:S(2)}, u32[]{:S(2)}) collective-permute-start(bf16[4,8,16,256]{3,2,1,0:T(8,128)(2,1)} %fusion.6), channel_id=1, source_target_pairs={{0,4},{1,5},{2,6},{3,7},{4,0},{5,1},{6,2},{7,3},{8,12},{9,13},{10,... | collective-permute-start | bytes 786440 | tf_op jit(solution)/shard_map/ppermute | solution.py:29
  112.9 21.8 %collective-permute-start.11 = (bf16[2,256,256]{2,1,0:T(8,128)(2,1)}, bf16[2,256,256]{2,1,0:T(8,128)(2,1)S(1)}, u32[]{:S(2)}, u32[]{:S(2)}) collective-permute-start(bf16[2,256,256]{2,1,0:T(8,128)(2,1)} %tile_products.5), channel_id=1, source_target_pairs={{8,24},{9,25},{10,26},{11,27},{12,28},{13,29},{14,30},{15,31},{16,... | collective-permute-start | bytes 786440 | tf_op jit(solution)/shard_map/ppermute | solution.py:29
  123.6 21.3 %collective-permute-start.13 = (bf16[2,256,256]{2,1,0:T(8,128)(2,1)}, bf16[2,256,256]{2,1,0:T(8,128)(2,1)S(1)}, u32[]{:S(2)}, u32[]{:S(2)}) collective-permute-start(bf16[2,256,256]{2,1,0:T(8,128)(2,1)} %get-tuple-element.14), channel_id=1, source_target_pairs={{0,16},{1,17},{2,18},{3,19},{8,24},{9,25},{10,26},{11,27},{16,32},... | collective-permute-start | bytes 786440 | tf_op jit(solution)/shard_map/ppermute | solution.py:29
  131.8 4.9 %collective-permute-start.21 = (bf16[8,16,256]{2,1,0:T(8,128)(2,1)S(1)}, bf16[8,16,256]{2,1,0:T(8,128)(2,1)S(1)}, u32[]{:S(2)}, u32[]{:S(2)}) collective-permute-start(bf16[8,16,256]{2,1,0:T(8,128)(2,1)S(1)} %get-tuple-element.31), channel_id=1, source_target_pairs={{0,64},{1,65},{2,66},{3,67},{4,68},{5,69},{6,70},{7,71},{8,72},{9,... | collective-permute-start | bytes 196616 | tf_op jit(solution)/shard_map/ppermute | solution.py:29
  133.4 4.6 %collective-permute-start.22 = (bf16[8,16,256]{2,1,0:T(8,128)(2,1)S(1)}, bf16[8,16,256]{2,1,0:T(8,128)(2,1)S(1)}, u32[]{:S(2)}, u32[]{:S(2)}) collective-permute-start(bf16[8,16,256]{2,1,0:T(8,128)(2,1)S(1)} %get-tuple-element.33), channel_id=1, source_target_pairs={{0,128},{1,129},{2,130},{3,131},{4,132},{5,133},{6,134},{7,135},{8... | collective-permute-start | bytes 196616 | tf_op jit(solution)/shard_map/ppermute | solution.py:29
  133.4 4.6 %collective-permute-start.23 = (bf16[8,16,256]{2,1,0:T(8,128)(2,1)S(1)}, bf16[8,16,256]{2,1,0:T(8,128)(2,1)S(1)}, u32[]{:S(2)}, u32[]{:S(2)}) collective-permute-start(bf16[8,16,256]{2,1,0:T(8,128)(2,1)S(1)} %get-tuple-element.32), channel_id=1, source_target_pairs={{0,192},{1,193},{2,194},{3,195},{4,196},{5,197},{6,198},{7,199},{8... | collective-permute-start | bytes 196616 | tf_op jit(solution)/shard_map/ppermute | solution.py:29
  135.8 10.8 %collective-permute-start.12 = (bf16[2,256,256]{2,1,0:T(8,128)(2,1)S(1)}, bf16[2,256,256]{2,1,0:T(8,128)(2,1)S(1)}, u32[]{:S(2)}, u32[]{:S(2)}) collective-permute-start(bf16[2,256,256]{2,1,0:T(8,128)(2,1)S(1)} %add_convert_fusion), channel_id=1, source_target_pairs={{0,8},{1,9},{2,10},{3,11},{4,12},{5,13},{6,14},{7,15},{8,0},{9,1},... | collective-permute-start | bytes 786440 | tf_op jit(solution)/shard_map/ppermute | solution.py:29
  138.1 4.7 %collective-permute-start.24 = (f32[2,16,256]{2,1,0:T(8,128)S(1)}, f32[2,16,256]{2,1,0:T(8,128)S(1)}, u32[]{:S(2)}, u32[]{:S(2)}) collective-permute-start(f32[2,16,256]{2,1,0:T(8,128)S(1)} %get-tuple-element.34), channel_id=1, source_target_pairs={{0,16},{1,17},{2,18},{3,19},{4,20},{5,21},{6,22},{7,23},{8,24},{9,... | collective-permute-start | bytes 98312 | tf_op jit(solution)/shard_map/ppermute | solution.py:29
  140.3 4.6 %collective-permute-start.25 = (f32[2,16,256]{2,1,0:T(8,128)S(1)}, f32[2,16,256]{2,1,0:T(8,128)S(1)}, u32[]{:S(2)}, u32[]{:S(2)}) collective-permute-start(f32[2,16,256]{2,1,0:T(8,128)S(1)} %get-tuple-element.36), channel_id=1, source_target_pairs={{0,32},{1,33},{2,34},{3,35},{4,36},{5,37},{6,38},{7,39},{8,40},{9,... | collective-permute-start | bytes 98312 | tf_op jit(solution)/shard_map/ppermute | solution.py:29
  140.3 4.6 %collective-permute-start.26 = (f32[2,16,256]{2,1,0:T(8,128)S(1)}, f32[2,16,256]{2,1,0:T(8,128)S(1)}, u32[]{:S(2)}, u32[]{:S(2)}) collective-permute-start(f32[2,16,256]{2,1,0:T(8,128)S(1)} %get-tuple-element.35), channel_id=1, source_target_pairs={{0,48},{1,49},{2,50},{3,51},{4,52},{5,53},{6,54},{7,55},{8,56},{9,... | collective-permute-start | bytes 98312 | tf_op jit(solution)/shard_map/ppermute | solution.py:29
  146.7 36.4 %copy-start.7 = (bf16[2,256,256]{2,1,0:T(8,128)(2,1)}, bf16[2,256,256]{2,1,0:T(8,128)(2,1)S(1)}, u32[]{:S(2)}) copy-start(bf16[2,256,256]{2,1,0:T(8,128)(2,1)S(1)} %multiply_convert_fusion.p0) | copy-start | bytes 786436
  146.7 36.4 %collective-permute-start.14 = (bf16[2,256,256]{2,1,0:T(8,128)(2,1)S(1)}, bf16[2,256,256]{2,1,0:T(8,128)(2,1)S(1)}, u32[]{:S(2)}, u32[]{:S(2)}) collective-permute-start(bf16[2,256,256]{2,1,0:T(8,128)(2,1)S(1)} %multiply_convert_fusion.p0), channel_id=1, source_target_pairs={{0,1},{1,2},{2,3},{3,0},{4,5},{5,6},{6,7},{7,4},{8,9},{9,10},{10,1... | collective-permute-start | bytes 786440 | tf_op jit(solution)/shard_map/ppermute | solution.py:29
  147.7 35.4 %collective-permute-start.15 = (bf16[2,256,256]{2,1,0:T(8,128)(2,1)S(1)}, bf16[2,256,256]{2,1,0:T(8,128)(2,1)S(1)}, u32[]{:S(2)}, u32[]{:S(2)}) collective-permute-start(bf16[2,256,256]{2,1,0:T(8,128)(2,1)S(1)} %multiply_convert_fusion.p0), channel_id=1, source_target_pairs={{0,2},{1,3},{2,0},{3,1},{4,6},{5,7},{6,4},{7,5},{8,10},{9,11},{10,... | collective-permute-start | bytes 786440 | tf_op jit(solution)/shard_map/ppermute | solution.py:29
  156.0 27.1 %collective-permute-start.16 = (bf16[2,256,256]{2,1,0:T(8,128)(2,1)S(1)}, bf16[2,256,256]{2,1,0:T(8,128)(2,1)S(1)}, u32[]{:S(2)}, u32[]{:S(2)}) collective-permute-start(bf16[2,256,256]{2,1,0:T(8,128)(2,1)S(1)} %multiply_convert_fusion.p0), channel_id=1, source_target_pairs={{0,3},{1,0},{2,1},{3,2},{4,7},{5,4},{6,5},{7,6},{8,11},{9,8},{10,9... | collective-permute-start | bytes 786440 | tf_op jit(solution)/shard_map/ppermute | solution.py:29
  158.3 24.2 %collective-permute-start.27 = (f32[16,256]{1,0:T(8,128)S(1)}, f32[16,256]{1,0:T(8,128)S(1)}, u32[]{:S(2)}, u32[]{:S(2)}) collective-permute-start(f32[16,256]{1,0:T(8,128)S(1)} %get-tuple-element.38), channel_id=1, source_target_pairs={{0,0},{1,1},{2,128},{3,129},{4,4},{5,5},{6,132},{7,133},{8,8},{9,9... | collective-permute-start | bytes 49160 | tf_op jit(solution)/shard_map/ppermute | solution.py:29
  161.3 21.2 %collective-permute-start.28 = (f32[16,256]{1,0:T(8,128)S(1)}, f32[16,256]{1,0:T(8,128)S(1)}, u32[]{:S(2)}, u32[]{:S(2)}) collective-permute-start(f32[16,256]{1,0:T(8,128)S(1)} %get-tuple-element.37), channel_id=1, source_target_pairs={{0,8},{1,9},{2,136},{3,137},{4,12},{5,13},{6,140},{7,141},{8,0},{9... | collective-permute-start | bytes 49160 | tf_op jit(solution)/shard_map/ppermute | solution.py:29
  (20 other events, 162.4 us)

commit v2 on v0

--- a/solution.py
+++ b/solution.py
@@ -47,29 +47,52 @@
     return tile, block
 
 
-def pick_kernel(pick, codes, *refs):
-    outs, sems = refs[:-1], refs[-1]
-    places = [(out, i) for out in outs for i in range(out.shape[0])]
-    copies = [
-        pltpu.make_async_copy(codes.at[pick[slot]], out.at[i], sems.at[slot])
-        for slot, (out, i) in enumerate(places)
-    ]
-    for copy in copies:
-        copy.start()
+def pick_kernel(place, rows, codes, give_out, keep_out, far_out, listed, sems):
+    band, chan = place[0], place[1]
+    chip = band // 2
+    near = 1 - 2 * (chip % 2)
+    far = 2 - 4 * (band % 2)
+    first = (CHAN - 1 - chan) * (SIDE // CHAN)
+    for i in range(3 * SIDE):
+        listed[i] = 0
+
+    def sort(tile, counts):
+        offset = rows[tile // K, tile % K] // PAIR_BLOCKS - chip
+        after = []
+        for kind, (wanted, count) in enumerate(zip((-near, near, -far), counts)):
+            hit = offset == wanted
+
+            @pl.when(hit & (count < SIDE))
+            def _(kind=kind, count=count):
+                listed[kind * SIDE + count] = tile
+
+            after.append(count + hit.astype(jnp.int32))
+        return tuple(after)
+
+    zero = jnp.int32(0)
+    lax.fori_loop(0, TILES, sort, (zero, zero, zero))
+    copies = []
+    for kind, (out, start) in enumerate(((give_out, first), (keep_out, first), (far_out, 0))):
+        for i in range(out.shape[0]):
+            tile = listed[kind * SIDE + start + i]
+            copies.append(pltpu.make_async_copy(codes.at[tile], out.at[i], sems.at[len(copies)]))
+            copies[-1].start()
     for copy in copies:
         copy.wait()
 
 
-def pick_tiles(pick, codes, counts):
+def pick_tiles(place, rows, codes):
+    counts = (SIDE // CHAN, SIDE // CHAN, CAP)
+    smem = pl.BlockSpec(memory_space=pltpu.SMEM)
     return pl.pallas_call(
         pick_kernel,
         out_shape=[jax.ShapeDtypeStruct((count, BLK, BLK), codes.dtype) for count in counts],
-        in_specs=[pl.BlockSpec(memory_space=pltpu.SMEM), pl.BlockSpec(memory_space=pl.ANY)],
-        out_specs=[pl.BlockSpec(memory_space=pltpu.VMEM)] * len(counts),
-        scratch_shapes=[pltpu.SemaphoreType.DMA((sum(counts),))],
+        in_specs=[smem, smem, pl.BlockSpec(memory_space=pl.ANY)],
+        out_specs=[pl.BlockSpec(memory_space=pltpu.VMEM)] * 3,
+        scratch_shapes=[pltpu.SMEM((3 * SIDE,), jnp.int32), pltpu.SemaphoreType.DMA((sum(counts),))],
         cost_estimate=pl.CostEstimate(flops=10**8, bytes_accessed=2 * sum(counts) * BLK * BLK * 4, transcendentals=0),
         name="pick_tiles",
-    )(pick, codes)
+    )(place, rows, codes)
 
 
 def products_kernel(groups, n_codes, *refs):
@@ -209,17 +232,9 @@
     cells_sib = go(cells, lambda b, c: (b ^ 1, c))
     cotangent_sib = go(cotangent, lambda b, c: (b ^ 1, c))
 
-    near = near_step(band)
-    far = far_step_traced(core)
-    readers = band + jnp.array([0, 0, 0, 0, 2, -2, 0], jnp.int32) * near + jnp.array([0] * 6 + [2], jnp.int32) * far
-    offsets = (
-        jnp.array([1, -1, 0, 0, -1, 1, 0], jnp.int32) * near + jnp.array([0, 0, -1, 0, 0, 0, -1], jnp.int32) * far
-    )
-    tile, block = slot_table(tile_source, readers, offsets)
-
-    wanted = lax.dynamic_slice_in_dim(tile[:2], (CHAN - 1 - chan) * quarter, quarter, 1)
-    pick = jnp.maximum(jnp.concatenate([wanted.reshape(-1), tile[2, :CAP]]), 0)
-    keep_codes, give_codes, far_codes = pick_tiles(pick, codes, (quarter, quarter, CAP))
+    rows = lax.dynamic_slice_in_dim(tile_source, band * NB_DEV, NB_DEV, 0)
+    place = jnp.stack([band, chan]).astype(jnp.int32)
+    give_codes, keep_codes, far_codes = pick_tiles(place, rows, codes)
     give_codes = go(give_codes, lambda b, c: (b - 2 * near_step(b), CHAN - 1 - c))
     keep_codes = go(keep_codes, lambda b, c: (b ^ 2, CHAN - 1 - c))
     far_codes = go(far_codes, lambda b, c: (b - 2 * far_step(b), c))
@@ -230,8 +245,14 @@
     give_codes = over_chan(give_codes)
     keep_codes = over_chan(keep_codes)
 
+    dec_pair = go(decoded_saved, lambda b, c: (b, c ^ 2))
     cot_pair = go(out_cotangent, lambda b, c: (b, c ^ 1))
-    dec_pair = go(decoded_saved, lambda b, c: (b, c ^ 2))
+
+    near = near_step(band)
+    far = far_step_traced(core)
+    readers = band + jnp.array([2, -2, 0, 0], jnp.int32) * near + jnp.array([0, 0, 2, 0], jnp.int32) * far
+    offsets = jnp.array([-1, 1, 0, 0], jnp.int32) * near + jnp.array([0, 0, -1, 0], jnp.int32) * far
+    tile, block = slot_table(tile_source, readers, offsets)
 
     def meta_of(row, index):
         node = jnp.where(tile[row] < 0, NB_DEV, tile[row] // K)
@@ -249,15 +270,15 @@
     blocks = (cells, cells_sib, cotangent, cotangent_sib)
     piece_group = [[(i, i * quarter, quarter) for i in range(CHAN)]]
     near_meta = jnp.concatenate(
-        [meta_of(6, jnp.arange(SIDE, dtype=jnp.int32))[:, :CAP], meta_of(3, jnp.maximum(tile[3], 0))], axis=1
+        [meta_of(2, jnp.arange(SIDE, dtype=jnp.int32))[:, :CAP], meta_of(3, jnp.maximum(tile[3], 0))], axis=1
     )
     far_part, own_part = tile_products(
         near_meta, [far_codes, codes], blocks, [[(0, 0, CAP)], [(1, CAP, SIDE)]], [jnp.bfloat16, jnp.float32]
     )
     got_far = go(far_part, lambda b, c: (b + 2 * far_step(b), c))
-    (give_part,) = tile_products(pieces_meta(5), give_codes, blocks, piece_group, [jnp.bfloat16])
+    (give_part,) = tile_products(pieces_meta(1), give_codes, blocks, piece_group, [jnp.bfloat16])
     got_give = go(give_part, lambda b, c: (b - 4 * near_step(b), c))
-    (keep_part,) = tile_products(pieces_meta(4), keep_codes, blocks, piece_group, [jnp.float32])
+    (keep_part,) = tile_products(pieces_meta(0), keep_codes, blocks, piece_group, [jnp.float32])
     crossing = (keep_part + got_give.astype(jnp.float32)).astype(jnp.bfloat16)
     got_keep = go(crossing, lambda b, c: (b ^ 2, c))
     summed = own_part + got_keep.astype(jnp.float32) + got_far.astype(jnp.float32)
@@ -284,7 +305,10 @@
     def outer(left, right):
         return lax.dot_general(left, right, (((0,), (0,)), ((), ())), preferred_element_type=jnp.float32)
 
-    whole = jnp.stack([outer(cot, dec), outer(cot_pair, dec), outer(cot, dec_pair), outer(cot_pair, dec_pair)])
+    first = outer(cot, dec)
+    third = outer(cot, dec_pair)
+    second, fourth = outer(cot_pair, dec), outer(cot_pair, dec_pair)
+    whole = jnp.stack([first, second, third, fourth])
     halves = whole.reshape(4, 8, 2, rows, channels)
     own = lax.dynamic_index_in_dim(halves, core, 2, keepdims=False)
     other = lax.dynamic_index_in_dim(halves, 1 - core, 2, keepdims=False).astype(jnp.bfloat16)

time: 185 us -> 185 us (level)
  transfers between devices with their start and end apart: 28 -> 28, of which waited for: 7 -> 6; matrix products, arithmetic and copies ran while one was open for 9% -> 8% of each run, Pallas kernels for 10% -> 11%
where the time goes in v2:
time: 185 us; the launch traced here: 184 us
  waiting for transfers between devices  78.1 us (42%)
  starting transfers between devices  65 us (35%)
  Pallas kernels  22.3 us (12%)
  matrix products  7.09 us (4%)
  local copies, waits for them, and re-layouts  5.34 us (3%)
  other arithmetic  5.33 us (3%)
    ppermute x28, waiting for transfers between devices, permute(): return lax.ppermute(x, ('band', 'chan'), pairs)  78.1 us
    ppermute x28, starting transfers between devices, permute(): return lax.ppermute(x, ('band', 'chan'), pairs)  65 us
    pallas_call x3, Pallas kernels, tile_products(): pl.pallas_call(functools.partial(products_kernel, groups, len(codes)), ou...  15.3 us
    dot_general x4, matrix products, outer(): lax.dot_general(left, right, (((0,), (0,)), ((), ())), preferred_element_...  7.09 us
    pallas_call x1, Pallas kernels, pick_tiles(): pl.pallas_call(pick_kernel, out_shape=[jax.ShapeDtypeStruct((count, BLK,...  4.33 us
  transfers between devices with their start and end apart: 28, of which 6 were waited for; matrix products, arithmetic and copies ran while one was open for 8% of the time, Pallas kernels for 11%

profile of v2, /device:TPU:5, one launch (start us, length us, event | category | flops | bytes accessed | tf_op | source)
XLA Modules:
  0.0 184.4 jit_solution(107952532455930853)
XLA Ops:
  0.7 1.7 collective-permute-start.17
  2.4 3.0 %collective-permute-start.18 = (bf16[2048,256]{1,0:T(8,128)(2,1)}, bf16[2048,256]{1,0:T(8,128)(2,1)}, u32[]{:S(2)}, u32[]{:S(2)}) collective-permute-start(bf16[2048,256]{1,0:T(8,128)(2,1)} %param.16), channel_id=1, source_target_pairs={{0,2},{1,3},{2,0},{3,1},{4,6},{5,7},{6,4},{7,5},{8,10},{9,11},{10,... | collective-permute-start | bytes 3145736 | tf_op jit(solution)/shard_map/ppermute | solution.py:29
  7.4 4.3 %pick_tiles.1 = (s32[4,128,128]{2,1,0:T(8,128)}, s32[4,128,128]{2,1,0:T(8,128)}, s32[8,128,128]{2,1,0:T(8,128)}) custom-call(s32[2]{0:T(128)} %pad_add_fusion.7.place, s32[2,16]{1,0:T(2,128)} %constant_dynamic-slice_fusion.8.rows, s32[32,128,128]{2,1,0:T(8,128)} %bitcast.59), custom_call_target="tpu_custom_call" | custom-call | flops 100000000 | bytes 2097152 | tf_op jit(solution)/shard_map/pick_tiles/pallas_call | solution.py:87
  11.7 6.8 %collective-permute-start.7 = (s32[4,128,128]{2,1,0:T(8,128)}, s32[4,128,128]{2,1,0:T(8,128)S(1)}, u32[]{:S(2)}, u32[]{:S(2)}) collective-permute-start(s32[4,128,128]{2,1,0:T(8,128)} %get-tuple-element.13), channel_id=1, source_target_pairs={{8,19},{9,18},{10,17},{11,16},{12,23},{13,22},{14,21},{15,20},{16,... | collective-permute-start | bytes 786440 | tf_op jit(solution)/shard_map/ppermute | solution.py:29
  18.6 1.6 collective-permute-start.1
  23.2 1.7 fusion.26
  24.9 22.9 %collective-permute-done.17 = bf16[2048,256]{1,0:T(8,128)(2,1)} collective-permute-done((bf16[2048,256]{1,0:T(8,128)(2,1)}, bf16[2048,256]{1,0:T(8,128)(2,1)}, u32[]{:S(2)}, u32[]{:S(2)}) %collective-permute-start.17) | collective-permute-done | bytes 1048608 | tf_op jit(solution)/shard_map/ppermute | solution.py:29
  47.8 4.9 %collective-permute-start.3 = (s32[4,128,128]{2,1,0:T(8,128)S(1)}, s32[4,128,128]{2,1,0:T(8,128)}, u32[]{:S(2)}, u32[]{:S(2)}) collective-permute-start(s32[4,128,128]{2,1,0:T(8,128)S(1)} %copy-done.20), channel_id=1, source_target_pairs={{0,11},{1,10},{2,9},{3,8},{4,15},{5,14},{6,13},{7,12},{8,3},{9,2},... | collective-permute-start | bytes 786440 | tf_op jit(solution)/shard_map/ppermute | solution.py:29
  52.7 1.7 fusion.27
  54.4 3.2 %collective-permute-start = (s32[8,128,128]{2,1,0:T(8,128)}, s32[8,128,128]{2,1,0:T(8,128)}, u32[]{:S(2)}, u32[]{:S(2)}) collective-permute-start(s32[8,128,128]{2,1,0:T(8,128)} %get-tuple-element.10), channel_id=1, source_target_pairs={{4,20},{5,21},{6,22},{7,23},{12,28},{13,29},{14,30},{15,31},{16,0}... | collective-permute-start | bytes 1572872 | tf_op jit(solution)/shard_map/ppermute | solution.py:29
  57.6 2.2 %collective-permute-start.10 = (s32[4,128,128]{2,1,0:T(8,128)S(1)}, s32[4,128,128]{2,1,0:T(8,128)S(1)}, u32[]{:S(2)}, u32[]{:S(2)}) collective-permute-start(s32[4,128,128]{2,1,0:T(8,128)S(1)} %collective-permute-done.7.refs_1_), channel_id=1, source_target_pairs={{0,3},{1,0},{2,1},{3,2},{4,7},{5,4},{6,5},{7,6},{8,11},{9,8},{10,9... | collective-permute-start | bytes 786440 | tf_op jit(solution)/shard_map/ppermute | solution.py:29
  59.9 2.0 %fusion.29 = f32[256,256]{1,0:T(8,128)S(1)} fusion(bf16[2048,256]{1,0:T(8,128)(2,1)} %collective-permute-done.17, bf16[2048,256]{1,0:T(8,128)(2,1)} %collective-permute-done.18), kind=kOutput, calls=%fused_computation.134 | convolution fusion | flops 268435456 | bytes 2359296 | tf_op jit(solution)/shard_map/dot_general | solution.py:306
  61.9 7.8 %collective-permute-done.3.refs_1_ = s32[4,128,128]{2,1,0:T(8,128)} collective-permute-done((s32[4,128,128]{2,1,0:T(8,128)S(1)}, s32[4,128,128]{2,1,0:T(8,128)}, u32[]{:S(2)}, u32[]{:S(2)}) %collective-permute-start.3) | collective-permute-done | bytes 262176 | tf_op jit(solution)/shard_map/ppermute | solution.py:29
  69.6 2.4 %collective-permute-start.9 = (s32[4,128,128]{2,1,0:T(8,128)S(1)}, s32[4,128,128]{2,1,0:T(8,128)S(1)}, u32[]{:S(2)}, u32[]{:S(2)}) collective-permute-start(s32[4,128,128]{2,1,0:T(8,128)S(1)} %collective-permute-done.7.refs_1_), channel_id=1, source_target_pairs={{0,2},{1,3},{2,0},{3,1},{4,6},{5,7},{6,4},{7,5},{8,10},{9,11},{10,... | collective-permute-start | bytes 786440 | tf_op jit(solution)/shard_map/ppermute | solution.py:29
  72.1 1.7 fusion.28
  74.8 3.5 %collective-permute-done.8.refs_2_ = s32[4,128,128]{2,1,0:T(8,128)S(1)} collective-permute-done((s32[4,128,128]{2,1,0:T(8,128)S(1)}, s32[4,128,128]{2,1,0:T(8,128)S(1)}, u32[]{:S(2)}, u32[]{:S(2)}) %collective-permute-start.8) | collective-permute-done | bytes 262176 | tf_op jit(solution)/shard_map/ppermute | solution.py:29
  78.3 22.2 %collective-permute-done.9.refs_3_ = s32[4,128,128]{2,1,0:T(8,128)S(1)} collective-permute-done((s32[4,128,128]{2,1,0:T(8,128)S(1)}, s32[4,128,128]{2,1,0:T(8,128)S(1)}, u32[]{:S(2)}, u32[]{:S(2)}) %collective-permute-start.9) | collective-permute-done | bytes 262176 | tf_op jit(solution)/shard_map/ppermute | solution.py:29
  102.7 4.8 %tile_products.5 = bf16[2,256,256]{2,1,0:T(8,128)(2,1)} custom-call(s32[4,16]{1,0:T(4,128)} %pad_add_fusion.6.refs_0_, s32[4,128,128]{2,1,0:T(8,128)} %copy-done.8, s32[4,128,128]{2,1,0:T(8,128)} %copy-done.10, s32[4,128,128]{2,1,0:T(8,128)} %copy-done.11, s32[4,128,128]{2,1,0:T(8,128)} %copy-done.9, bf16[16,128,256]{2,1,0:T(8,128)(2,1)} %bitcast.55, ...), custom_call_target="tpu_custom_call" | custom-call | flops 268435456 | bytes 3145728 | tf_op jit(solution)/shard_map/tile_products/pallas_call | solution.py:166
  107.5 5.4 %collective-permute-start.11 = (bf16[2,256,256]{2,1,0:T(8,128)(2,1)}, bf16[2,256,256]{2,1,0:T(8,128)(2,1)S(1)}, u32[]{:S(2)}, u32[]{:S(2)}) collective-permute-start(bf16[2,256,256]{2,1,0:T(8,128)(2,1)} %tile_products.5), channel_id=1, source_target_pairs={{8,24},{9,25},{10,26},{11,27},{12,28},{13,29},{14,30},{15,31},{16,... | collective-permute-start | bytes 786440 | tf_op jit(solution)/shard_map/ppermute | solution.py:29
  112.9 5.8 %tile_products.3 = (bf16[2,256,256]{2,1,0:T(8,128)(2,1)}, f32[2,256,256]{2,1,0:T(8,128)}) custom-call(s32[4,24]{1,0:T(4,128)} %add_add_fusion.refs_0_, s32[8,128,128]{2,1,0:T(8,128)} %collective-permute-done.refs_1_, s32[32,128,128]{2,1,0:T(8,128)} %bitcast.60, bf16[16,128,256]{2,1,0:T(8,128)(2,1)} %bitcast.56, bf16[16,128,256]{2,1,0:T(8,128)(2,1)} %copy-done.2, ...), custom_call_target="tpu_custom_call" | custom-call | flops 402653184 | bytes 4718592 | tf_op jit(solution)/shard_map/tile_products/pallas_call | solution.py:166
  118.7 2.5 %collective-permute-start.13 = (bf16[2,256,256]{2,1,0:T(8,128)(2,1)}, bf16[2,256,256]{2,1,0:T(8,128)(2,1)S(1)}, u32[]{:S(2)}, u32[]{:S(2)}) collective-permute-start(bf16[2,256,256]{2,1,0:T(8,128)(2,1)} %get-tuple-element.14), channel_id=1, source_target_pairs={{0,16},{1,17},{2,18},{3,19},{8,24},{9,25},{10,26},{11,27},{16,32},... | collective-permute-start | bytes 786440 | tf_op jit(solution)/shard_map/ppermute | solution.py:29
  121.9 4.8 %tile_products.4 = f32[2,256,256]{2,1,0:T(8,128)} custom-call(s32[4,16]{1,0:T(4,128)} %pad_add_fusion.5.refs_0_, s32[4,128,128]{2,1,0:T(8,128)} %collective-permute-done.3.refs_1_, s32[4,128,128]{2,1,0:T(8,128)} %collective-permute-done.4.refs_2_, s32[4,128,128]{2,1,0:T(8,128)} %collective-permute-done.5.refs_3_, s32[4,128,128]{2,1,0:T(8,128)} %copy-done.15, ...), custom_call_target="tpu_custom_call" | custom-call | flops 268435456 | bytes 3145728 | tf_op jit(solution)/shard_map/tile_products/pallas_call | solution.py:166
  130.5 2.3 %collective-permute-start.12 = (bf16[2,256,256]{2,1,0:T(8,128)(2,1)S(1)}, bf16[2,256,256]{2,1,0:T(8,128)(2,1)S(1)}, u32[]{:S(2)}, u32[]{:S(2)}) collective-permute-start(bf16[2,256,256]{2,1,0:T(8,128)(2,1)S(1)} %add_convert_fusion), channel_id=1, source_target_pairs={{0,8},{1,9},{2,10},{3,11},{4,12},{5,13},{6,14},{7,15},{8,0},{9,1},... | collective-permute-start | bytes 786440 | tf_op jit(solution)/shard_map/ppermute | solution.py:29
  132.9 2.8 %collective-permute-start.23 = (f32[2,16,256]{2,1,0:T(8,128)S(1)}, f32[2,16,256]{2,1,0:T(8,128)S(1)}, u32[]{:S(2)}, u32[]{:S(2)}) collective-permute-start(f32[2,16,256]{2,1,0:T(8,128)S(1)} %get-tuple-element.32), channel_id=1, source_target_pairs={{0,16},{1,17},{2,18},{3,19},{4,20},{5,21},{6,22},{7,23},{8,24},{9,... | collective-permute-start | bytes 98312 | tf_op jit(solution)/shard_map/ppermute | solution.py:29
  135.7 2.5 %collective-permute-start.25 = (f32[2,16,256]{2,1,0:T(8,128)S(1)}, f32[2,16,256]{2,1,0:T(8,128)S(1)}, u32[]{:S(2)}, u32[]{:S(2)}) collective-permute-start(f32[2,16,256]{2,1,0:T(8,128)S(1)} %get-tuple-element.33), channel_id=1, source_target_pairs={{0,48},{1,49},{2,50},{3,51},{4,52},{5,53},{6,54},{7,55},{8,56},{9,... | collective-permute-start | bytes 98312 | tf_op jit(solution)/shard_map/ppermute | solution.py:29
  138.2 2.1 %collective-permute-done.24 = f32[2,16,256]{2,1,0:T(8,128)S(1)} collective-permute-done((f32[2,16,256]{2,1,0:T(8,128)S(1)}, f32[2,16,256]{2,1,0:T(8,128)S(1)}, u32[]{:S(2)}, u32[]{:S(2)}) %collective-permute-start.24) | collective-permute-done | bytes 32800 | tf_op jit(solution)/shard_map/ppermute | solution.py:29
  140.4 1.5 collective-permute-start.14
  141.9 10.1 %collective-permute-start.15 = (bf16[2,256,256]{2,1,0:T(8,128)(2,1)S(1)}, bf16[2,256,256]{2,1,0:T(8,128)(2,1)S(1)}, u32[]{:S(2)}, u32[]{:S(2)}) collective-permute-start(bf16[2,256,256]{2,1,0:T(8,128)(2,1)S(1)} %multiply_convert_fusion.p0), channel_id=1, source_target_pairs={{0,2},{1,3},{2,0},{3,1},{4,6},{5,7},{6,4},{7,5},{8,10},{9,11},{10,... | collective-permute-start | bytes 786440 | tf_op jit(solution)/shard_map/ppermute | solution.py:29
  153.0 5.2 %collective-permute-start.26 = (f32[16,256]{1,0:T(8,128)S(1)}, f32[16,256]{1,0:T(8,128)S(1)}, u32[]{:S(2)}, u32[]{:S(2)}) collective-permute-start(f32[16,256]{1,0:T(8,128)S(1)} %get-tuple-element.36), channel_id=1, source_target_pairs={{0,0},{1,1},{2,128},{3,129},{4,4},{5,5},{6,132},{7,133},{8,8},{9,9... | collective-permute-start | bytes 49160 | tf_op jit(solution)/shard_map/ppermute | solution.py:29
  158.2 1.7 collective-permute-start.27
  159.9 19.6 %collective-permute-done.26 = f32[16,256]{1,0:T(8,128)S(1)} collective-permute-done((f32[16,256]{1,0:T(8,128)S(1)}, f32[16,256]{1,0:T(8,128)S(1)}, u32[]{:S(2)}, u32[]{:S(2)}) %collective-permute-start.26) | collective-permute-done | bytes 16416 | tf_op jit(solution)/shard_map/ppermute | solution.py:29
  181.7 2.7 %project.1 = (bf16[256,256]{1,0:T(8,128)(2,1)}, bf16[256,256]{1,0:T(8,128)(2,1)}) custom-call(s32[1]{0:T(128)} %bitcast.chan_ref, bf16[2,256,256]{2,1,0:T(8,128)(2,1)} %copy-done.6, bf16[2,256,256]{2,1,0:T(8,128)(2,1)} %copy-done.12, bf16[2,256,256]{2,1,0:T(8,128)(2,1)} %copy-done.13, bf16[2,256,256]{2,1,0:T(8,128)(2,1)} %copy-done.14, ...), custom_call_target="tpu_custom_call" | custom-call | flops 268435456 | bytes 4194304 | tf_op jit(solution)/shard_map/project/pallas_call | solution.py:199
  (117 shorter events, 15.7 us)
Async XLA Ops:
  0.7 47.0 %collective-permute-start.17 = (bf16[2048,256]{1,0:T(8,128)(2,1)}, bf16[2048,256]{1,0:T(8,128)(2,1)}, u32[]{:S(2)}, u32[]{:S(2)}) collective-permute-start(bf16[2048,256]{1,0:T(8,128)(2,1)} %param.15), channel_id=1, source_target_pairs={{0,1},{1,0},{2,3},{3,2},{4,5},{5,4},{6,7},{7,6},{8,9},{9,8},{10,11... | collective-permute-start | bytes 3145736 | tf_op jit(solution)/shard_map/ppermute | solution.py:29
  2.4 55.2 %collective-permute-start.18 = (bf16[2048,256]{1,0:T(8,128)(2,1)}, bf16[2048,256]{1,0:T(8,128)(2,1)}, u32[]{:S(2)}, u32[]{:S(2)}) collective-permute-start(bf16[2048,256]{1,0:T(8,128)(2,1)} %param.16), channel_id=1, source_target_pairs={{0,2},{1,3},{2,0},{3,1},{4,6},{5,7},{6,4},{7,5},{8,10},{9,11},{10,... | collective-permute-start | bytes 3145736 | tf_op jit(solution)/shard_map/ppermute | solution.py:29
  11.7 42.7 %collective-permute-start.7 = (s32[4,128,128]{2,1,0:T(8,128)}, s32[4,128,128]{2,1,0:T(8,128)S(1)}, u32[]{:S(2)}, u32[]{:S(2)}) collective-permute-start(s32[4,128,128]{2,1,0:T(8,128)} %get-tuple-element.13), channel_id=1, source_target_pairs={{8,19},{9,18},{10,17},{11,16},{12,23},{13,22},{14,21},{15,20},{16,... | collective-permute-start | bytes 786440 | tf_op jit(solution)/shard_map/ppermute | solution.py:29
  18.6 82.0 %collective-permute-start.1 = (bf16[16,128,256]{2,1,0:T(8,128)(2,1)S(1)}, bf16[16,128,256]{2,1,0:T(8,128)(2,1)S(1)}, u32[]{:S(2)}, u32[]{:S(2)}) collective-permute-start(bf16[16,128,256]{2,1,0:T(8,128)(2,1)S(1)} %bitcast.58), channel_id=1, source_target_pairs={{0,4},{1,5},{2,6},{3,7},{4,0},{5,1},{6,2},{7,3},{8,12},{9,13},{10,... | collective-permute-start | bytes 3145736 | tf_op jit(solution)/shard_map/ppermute | solution.py:29
  20.1 80.5 %collective-permute-start.2 = (bf16[16,128,256]{2,1,0:T(8,128)(2,1)S(1)}, bf16[16,128,256]{2,1,0:T(8,128)(2,1)}, u32[]{:S(2)}, u32[]{:S(2)}) collective-permute-start(bf16[16,128,256]{2,1,0:T(8,128)(2,1)S(1)} %bitcast.54), channel_id=1, source_target_pairs={{0,4},{1,5},{2,6},{3,7},{4,0},{5,1},{6,2},{7,3},{8,12},{9,13},{10,... | collective-permute-start | bytes 3145736 | tf_op jit(solution)/shard_map/ppermute | solution.py:29
  22.4 25.3 %copy-start.20 = (s32[4,128,128]{2,1,0:T(8,128)S(1)}, s32[4,128,128]{2,1,0:T(8,128)}, u32[]{:S(2)}) copy-start(s32[4,128,128]{2,1,0:T(8,128)} %get-tuple-element.12) | copy-start | bytes 786436
  22.4 30.2 %copy-start.3 = (bf16[2048,256]{1,0:T(8,128)(2,1)S(1)}, bf16[2048,256]{1,0:T(8,128)(2,1)}, u32[]{:S(2)}) copy-start(bf16[2048,256]{1,0:T(8,128)(2,1)} %param.16) | copy-start | bytes 3145732
  47.8 21.9 %collective-permute-start.3 = (s32[4,128,128]{2,1,0:T(8,128)S(1)}, s32[4,128,128]{2,1,0:T(8,128)}, u32[]{:S(2)}, u32[]{:S(2)}) collective-permute-start(s32[4,128,128]{2,1,0:T(8,128)S(1)} %copy-done.20), channel_id=1, source_target_pairs={{0,11},{1,10},{2,9},{3,8},{4,15},{5,14},{6,13},{7,12},{8,3},{9,2},... | collective-permute-start | bytes 786440 | tf_op jit(solution)/shard_map/ppermute | solution.py:29
  54.4 53.1 %collective-permute-start = (s32[8,128,128]{2,1,0:T(8,128)}, s32[8,128,128]{2,1,0:T(8,128)}, u32[]{:S(2)}, u32[]{:S(2)}) collective-permute-start(s32[8,128,128]{2,1,0:T(8,128)} %get-tuple-element.10), channel_id=1, source_target_pairs={{4,20},{5,21},{6,22},{7,23},{12,28},{13,29},{14,30},{15,31},{16,0}... | collective-permute-start | bytes 1572872 | tf_op jit(solution)/shard_map/ppermute | solution.py:29
  57.6 12.0 %collective-permute-start.10 = (s32[4,128,128]{2,1,0:T(8,128)S(1)}, s32[4,128,128]{2,1,0:T(8,128)S(1)}, u32[]{:S(2)}, u32[]{:S(2)}) collective-permute-start(s32[4,128,128]{2,1,0:T(8,128)S(1)} %collective-permute-done.7.refs_1_), channel_id=1, source_target_pairs={{0,3},{1,0},{2,1},{3,2},{4,7},{5,4},{6,5},{7,6},{8,11},{9,8},{10,9... | collective-permute-start | bytes 786440 | tf_op jit(solution)/shard_map/ppermute | solution.py:29
  69.6 8.7 %collective-permute-start.8 = (s32[4,128,128]{2,1,0:T(8,128)S(1)}, s32[4,128,128]{2,1,0:T(8,128)S(1)}, u32[]{:S(2)}, u32[]{:S(2)}) collective-permute-start(s32[4,128,128]{2,1,0:T(8,128)S(1)} %collective-permute-done.7.refs_1_), channel_id=1, source_target_pairs={{0,1},{1,2},{2,3},{3,0},{4,5},{5,6},{6,7},{7,4},{8,9},{9,10},{10,1... | collective-permute-start | bytes 786440 | tf_op jit(solution)/shard_map/ppermute | solution.py:29
  69.6 30.9 %collective-permute-start.9 = (s32[4,128,128]{2,1,0:T(8,128)S(1)}, s32[4,128,128]{2,1,0:T(8,128)S(1)}, u32[]{:S(2)}, u32[]{:S(2)}) collective-permute-start(s32[4,128,128]{2,1,0:T(8,128)S(1)} %collective-permute-done.7.refs_1_), channel_id=1, source_target_pairs={{0,2},{1,3},{2,0},{3,1},{4,6},{5,7},{6,4},{7,5},{8,10},{9,11},{10,... | collective-permute-start | bytes 786440 | tf_op jit(solution)/shard_map/ppermute | solution.py:29
  73.9 26.7 %copy-start.4 = (f32[4,8,2,16,256]{4,3,2,1,0:T(8,128)}, f32[4,8,2,16,256]{4,3,2,1,0:T(8,128)S(1)}, u32[]{:S(2)}) copy-start(f32[4,8,2,16,256]{4,3,2,1,0:T(8,128)S(1)} %pad_maximum_fusion) | copy-start | bytes 3145732
  78.3 40.4 %collective-permute-start.4 = (s32[4,128,128]{2,1,0:T(8,128)}, s32[4,128,128]{2,1,0:T(8,128)}, u32[]{:S(2)}, u32[]{:S(2)}) collective-permute-start(s32[4,128,128]{2,1,0:T(8,128)} %collective-permute-done.3.refs_1_), channel_id=1, source_target_pairs={{0,1},{1,2},{2,3},{3,0},{4,5},{5,6},{6,7},{7,4},{8,9},{9,10},{10,1... | collective-permute-start | bytes 786440 | tf_op jit(solution)/shard_map/ppermute | solution.py:29
  100.5 20.7 %collective-permute-start.5 = (s32[4,128,128]{2,1,0:T(8,128)}, s32[4,128,128]{2,1,0:T(8,128)}, u32[]{:S(2)}, u32[]{:S(2)}) collective-permute-start(s32[4,128,128]{2,1,0:T(8,128)} %collective-permute-done.3.refs_1_), channel_id=1, source_target_pairs={{0,2},{1,3},{2,0},{3,1},{4,6},{5,7},{6,4},{7,5},{8,10},{9,11},{10,... | collective-permute-start | bytes 786440 | tf_op jit(solution)/shard_map/ppermute | solution.py:29
  100.5 20.7 %collective-permute-start.6 = (s32[4,128,128]{2,1,0:T(8,128)}, s32[4,128,128]{2,1,0:T(8,128)S(1)}, u32[]{:S(2)}, u32[]{:S(2)}) collective-permute-start(s32[4,128,128]{2,1,0:T(8,128)} %collective-permute-done.3.refs_1_), channel_id=1, source_target_pairs={{0,3},{1,0},{2,1},{3,2},{4,7},{5,4},{6,5},{7,6},{8,11},{9,8},{10,9... | collective-permute-start | bytes 786440 | tf_op jit(solution)/shard_map/ppermute | solution.py:29
  100.7 26.1 %collective-permute-start.19 = (bf16[4,8,16,256]{3,2,1,0:T(8,128)(2,1)}, bf16[4,8,16,256]{3,2,1,0:T(8,128)(2,1)S(1)}, u32[]{:S(2)}, u32[]{:S(2)}) collective-permute-start(bf16[4,8,16,256]{3,2,1,0:T(8,128)(2,1)} %fusion), channel_id=1, source_target_pairs={{0,4},{1,5},{2,6},{3,7},{4,0},{5,1},{6,2},{7,3},{8,12},{9,13},{10,... | collective-permute-start | bytes 786440 | tf_op jit(solution)/shard_map/ppermute | solution.py:29
  107.5 21.9 %collective-permute-start.11 = (bf16[2,256,256]{2,1,0:T(8,128)(2,1)}, bf16[2,256,256]{2,1,0:T(8,128)(2,1)S(1)}, u32[]{:S(2)}, u32[]{:S(2)}) collective-permute-start(bf16[2,256,256]{2,1,0:T(8,128)(2,1)} %tile_products.5), channel_id=1, source_target_pairs={{8,24},{9,25},{10,26},{11,27},{12,28},{13,29},{14,30},{15,31},{16,... | collective-permute-start | bytes 786440 | tf_op jit(solution)/shard_map/ppermute | solution.py:29
  118.7 21.6 %collective-permute-start.13 = (bf16[2,256,256]{2,1,0:T(8,128)(2,1)}, bf16[2,256,256]{2,1,0:T(8,128)(2,1)S(1)}, u32[]{:S(2)}, u32[]{:S(2)}) collective-permute-start(bf16[2,256,256]{2,1,0:T(8,128)(2,1)} %get-tuple-element.14), channel_id=1, source_target_pairs={{0,16},{1,17},{2,18},{3,19},{8,24},{9,25},{10,26},{11,27},{16,32},... | collective-permute-start | bytes 786440 | tf_op jit(solution)/shard_map/ppermute | solution.py:29
  126.9 5.9 %collective-permute-start.20 = (bf16[8,16,256]{2,1,0:T(8,128)(2,1)S(1)}, bf16[8,16,256]{2,1,0:T(8,128)(2,1)S(1)}, u32[]{:S(2)}, u32[]{:S(2)}) collective-permute-start(bf16[8,16,256]{2,1,0:T(8,128)(2,1)S(1)} %get-tuple-element.29), channel_id=1, source_target_pairs={{0,64},{1,65},{2,66},{3,67},{4,68},{5,69},{6,70},{7,71},{8,72},{9,... | collective-permute-start | bytes 196616 | tf_op jit(solution)/shard_map/ppermute | solution.py:29
  128.1 4.7 %collective-permute-start.21 = (bf16[8,16,256]{2,1,0:T(8,128)(2,1)S(1)}, bf16[8,16,256]{2,1,0:T(8,128)(2,1)S(1)}, u32[]{:S(2)}, u32[]{:S(2)}) collective-permute-start(bf16[8,16,256]{2,1,0:T(8,128)(2,1)S(1)} %get-tuple-element.31), channel_id=1, source_target_pairs={{0,128},{1,129},{2,130},{3,131},{4,132},{5,133},{6,134},{7,135},{8... | collective-permute-start | bytes 196616 | tf_op jit(solution)/shard_map/ppermute | solution.py:29
  128.3 4.5 %collective-permute-start.22 = (bf16[8,16,256]{2,1,0:T(8,128)(2,1)S(1)}, bf16[8,16,256]{2,1,0:T(8,128)(2,1)S(1)}, u32[]{:S(2)}, u32[]{:S(2)}) collective-permute-start(bf16[8,16,256]{2,1,0:T(8,128)(2,1)S(1)} %get-tuple-element.30), channel_id=1, source_target_pairs={{0,192},{1,193},{2,194},{3,195},{4,196},{5,197},{6,198},{7,199},{8... | collective-permute-start | bytes 196616 | tf_op jit(solution)/shard_map/ppermute | solution.py:29
  130.5 9.8 %collective-permute-start.12 = (bf16[2,256,256]{2,1,0:T(8,128)(2,1)S(1)}, bf16[2,256,256]{2,1,0:T(8,128)(2,1)S(1)}, u32[]{:S(2)}, u32[]{:S(2)}) collective-permute-start(bf16[2,256,256]{2,1,0:T(8,128)(2,1)S(1)} %add_convert_fusion), channel_id=1, source_target_pairs={{0,8},{1,9},{2,10},{3,11},{4,12},{5,13},{6,14},{7,15},{8,0},{9,1},... | collective-permute-start | bytes 786440 | tf_op jit(solution)/shard_map/ppermute | solution.py:29
  132.9 5.3 %collective-permute-start.23 = (f32[2,16,256]{2,1,0:T(8,128)S(1)}, f32[2,16,256]{2,1,0:T(8,128)S(1)}, u32[]{:S(2)}, u32[]{:S(2)}) collective-permute-start(f32[2,16,256]{2,1,0:T(8,128)S(1)} %get-tuple-element.32), channel_id=1, source_target_pairs={{0,16},{1,17},{2,18},{3,19},{4,20},{5,21},{6,22},{7,23},{8,24},{9,... | collective-permute-start | bytes 98312 | tf_op jit(solution)/shard_map/ppermute | solution.py:29
  135.7 4.6 %collective-permute-start.24 = (f32[2,16,256]{2,1,0:T(8,128)S(1)}, f32[2,16,256]{2,1,0:T(8,128)S(1)}, u32[]{:S(2)}, u32[]{:S(2)}) collective-permute-start(f32[2,16,256]{2,1,0:T(8,128)S(1)} %get-tuple-element.34), channel_id=1, source_target_pairs={{0,32},{1,33},{2,34},{3,35},{4,36},{5,37},{6,38},{7,39},{8,40},{9,... | collective-permute-start | bytes 98312 | tf_op jit(solution)/shard_map/ppermute | solution.py:29
  135.7 4.6 %collective-permute-start.25 = (f32[2,16,256]{2,1,0:T(8,128)S(1)}, f32[2,16,256]{2,1,0:T(8,128)S(1)}, u32[]{:S(2)}, u32[]{:S(2)}) collective-permute-start(f32[2,16,256]{2,1,0:T(8,128)S(1)} %get-tuple-element.33), channel_id=1, source_target_pairs={{0,48},{1,49},{2,50},{3,51},{4,52},{5,53},{6,54},{7,55},{8,56},{9,... | collective-permute-start | bytes 98312 | tf_op jit(solution)/shard_map/ppermute | solution.py:29
  140.4 39.8 %copy-start.6 = (bf16[2,256,256]{2,1,0:T(8,128)(2,1)}, bf16[2,256,256]{2,1,0:T(8,128)(2,1)S(1)}, u32[]{:S(2)}) copy-start(bf16[2,256,256]{2,1,0:T(8,128)(2,1)S(1)} %multiply_convert_fusion.p0) | copy-start | bytes 786436
  140.4 39.7 %collective-permute-start.14 = (bf16[2,256,256]{2,1,0:T(8,128)(2,1)S(1)}, bf16[2,256,256]{2,1,0:T(8,128)(2,1)S(1)}, u32[]{:S(2)}, u32[]{:S(2)}) collective-permute-start(bf16[2,256,256]{2,1,0:T(8,128)(2,1)S(1)} %multiply_convert_fusion.p0), channel_id=1, source_target_pairs={{0,1},{1,2},{2,3},{3,0},{4,5},{5,6},{6,7},{7,4},{8,9},{9,10},{10,1... | collective-permute-start | bytes 786440 | tf_op jit(solution)/shard_map/ppermute | solution.py:29
  141.9 38.2 %collective-permute-start.15 = (bf16[2,256,256]{2,1,0:T(8,128)(2,1)S(1)}, bf16[2,256,256]{2,1,0:T(8,128)(2,1)S(1)}, u32[]{:S(2)}, u32[]{:S(2)}) collective-permute-start(bf16[2,256,256]{2,1,0:T(8,128)(2,1)S(1)} %multiply_convert_fusion.p0), channel_id=1, source_target_pairs={{0,2},{1,3},{2,0},{3,1},{4,6},{5,7},{6,4},{7,5},{8,10},{9,11},{10,... | collective-permute-start | bytes 786440 | tf_op jit(solution)/shard_map/ppermute | solution.py:29
  152.0 28.1 %collective-permute-start.16 = (bf16[2,256,256]{2,1,0:T(8,128)(2,1)S(1)}, bf16[2,256,256]{2,1,0:T(8,128)(2,1)S(1)}, u32[]{:S(2)}, u32[]{:S(2)}) collective-permute-start(bf16[2,256,256]{2,1,0:T(8,128)(2,1)S(1)} %multiply_convert_fusion.p0), channel_id=1, source_target_pairs={{0,3},{1,0},{2,1},{3,2},{4,7},{5,4},{6,5},{7,6},{8,11},{9,8},{10,9... | collective-permute-start | bytes 786440 | tf_op jit(solution)/shard_map/ppermute | solution.py:29
  153.0 26.5 %collective-permute-start.26 = (f32[16,256]{1,0:T(8,128)S(1)}, f32[16,256]{1,0:T(8,128)S(1)}, u32[]{:S(2)}, u32[]{:S(2)}) collective-permute-start(f32[16,256]{1,0:T(8,128)S(1)} %get-tuple-element.36), channel_id=1, source_target_pairs={{0,0},{1,1},{2,128},{3,129},{4,4},{5,5},{6,132},{7,133},{8,8},{9,9... | collective-permute-start | bytes 49160 | tf_op jit(solution)/shard_map/ppermute | solution.py:29
  158.2 21.3 %collective-permute-start.27 = (f32[16,256]{1,0:T(8,128)S(1)}, f32[16,256]{1,0:T(8,128)S(1)}, u32[]{:S(2)}, u32[]{:S(2)}) collective-permute-start(f32[16,256]{1,0:T(8,128)S(1)} %get-tuple-element.35), channel_id=1, source_target_pairs={{0,8},{1,9},{2,136},{3,137},{4,12},{5,13},{6,140},{7,141},{8,0},{9... | collective-permute-start | bytes 49160 | tf_op jit(solution)/shard_map/ppermute | solution.py:29
  (17 other events, 192.0 us)

commit v3 on v2

--- a/solution.py
+++ b/solution.py
@@ -24,7 +24,7 @@
     for band in range(bands):
         for chan in range(CHAN):
             to_band, to_chan = move(band, chan)
-            if 0 <= to_band < bands:
+            if 0 <= to_band < bands and 0 <= to_chan < CHAN:
                 pairs.append((band * CHAN + chan, to_band * CHAN + to_chan))
     return lax.ppermute(x, ("band", "chan"), pairs)
 
@@ -47,12 +47,13 @@
     return tile, block
 
 
-def pick_kernel(place, rows, codes, give_out, keep_out, far_out, listed, sems):
+def pick_kernel(place, rows, codes, give_out, keep_out, give_extra, keep_extra, far_out, listed, sems):
     band, chan = place[0], place[1]
     chip = band // 2
     near = 1 - 2 * (chip % 2)
     far = 2 - 4 * (band % 2)
     first = (CHAN - 1 - chan) * (SIDE // CHAN)
+    extra = chan * (SIDE // CHAN)
     for i in range(3 * SIDE):
         listed[i] = 0
 
@@ -72,7 +73,8 @@
     zero = jnp.int32(0)
     lax.fori_loop(0, TILES, sort, (zero, zero, zero))
     copies = []
-    for kind, (out, start) in enumerate(((give_out, first), (keep_out, first), (far_out, 0))):
+    picks = ((0, give_out, first), (1, keep_out, first), (0, give_extra, extra), (1, keep_extra, extra), (2, far_out, 0))
+    for kind, out, start in picks:
         for i in range(out.shape[0]):
             tile = listed[kind * SIDE + start + i]
             copies.append(pltpu.make_async_copy(codes.at[tile], out.at[i], sems.at[len(copies)]))
@@ -82,13 +84,13 @@
 
 
 def pick_tiles(place, rows, codes):
-    counts = (SIDE // CHAN, SIDE // CHAN, CAP)
+    counts = (SIDE // CHAN,) * 4 + (CAP,)
     smem = pl.BlockSpec(memory_space=pltpu.SMEM)
     return pl.pallas_call(
         pick_kernel,
         out_shape=[jax.ShapeDtypeStruct((count, BLK, BLK), codes.dtype) for count in counts],
         in_specs=[smem, smem, pl.BlockSpec(memory_space=pl.ANY)],
-        out_specs=[pl.BlockSpec(memory_space=pltpu.VMEM)] * 3,
+        out_specs=[pl.BlockSpec(memory_space=pltpu.VMEM)] * len(counts),
         scratch_shapes=[pltpu.SMEM((3 * SIDE,), jnp.int32), pltpu.SemaphoreType.DMA((sum(counts),))],
         cost_estimate=pl.CostEstimate(flops=10**8, bytes_accessed=2 * sum(counts) * BLK * BLK * 4, transcendentals=0),
         name="pick_tiles",
@@ -102,12 +104,18 @@
     outs = refs[5 + n_codes : 5 + n_codes + len(groups)]
     code_buf, cell_buf, cot_buf, total, sems = refs[5 + n_codes + len(groups) :]
     for parts in groups:
-        for operand, first, count in parts:
-            source = codes[operand]
-
-            def begin(i, carry, first=first, source=source):
+        for operands, first, count in parts:
+
+            def begin(i, carry, first=first, operands=operands):
                 slot = first + i
-                pltpu.make_async_copy(source.at[meta[3, slot]], code_buf.at[slot], sems.at[0, slot]).start()
+                for operand in operands:
+
+                    @pl.when((meta[4, slot] == operand) | (len(operands) == 1))
+                    def _(operand=operand):
+                        pltpu.make_async_copy(
+                            codes[operand].at[meta[3, slot]], code_buf.at[slot], sems.at[0, slot]
+                        ).start()
+
                 local = meta[2, slot]
 
                 @pl.when(meta[1, slot] == 1)
@@ -234,16 +242,33 @@
 
     rows = lax.dynamic_slice_in_dim(tile_source, band * NB_DEV, NB_DEV, 0)
     place = jnp.stack([band, chan]).astype(jnp.int32)
-    give_codes, keep_codes, far_codes = pick_tiles(place, rows, codes)
-    give_codes = go(give_codes, lambda b, c: (b - 2 * near_step(b), CHAN - 1 - c))
-    keep_codes = go(keep_codes, lambda b, c: (b ^ 2, CHAN - 1 - c))
+    give_codes, keep_codes, give_extra, keep_extra, far_codes = pick_tiles(place, rows, codes)
+    ends = (0, CHAN - 1)
+
+    def mirrored(c):
+        return CHAN - 1 - c
+
+    def if_end(c):
+        return mirrored(c) if c in ends else -1
+
+    give_codes = go(give_codes, lambda b, c: (b - 2 * near_step(b), mirrored(c)))
+    keep_codes = go(keep_codes, lambda b, c: (b ^ 2, mirrored(c)))
+    give_extra = go(give_extra, lambda b, c: (b - 2 * near_step(b), if_end(c)))
+    keep_extra = go(keep_extra, lambda b, c: (b ^ 2, if_end(c)))
     far_codes = go(far_codes, lambda b, c: (b - 2 * far_step(b), c))
+
+    def by_relay(x, extra):
+        up = go(x, lambda b, c: (b, c + 1))
+        down = go(x, lambda b, c: (b, c - 1))
+        up_up = go(up, lambda b, c: (b, c + 1 if c > 0 else -1))
+        down_down = go(down, lambda b, c: (b, c - 1 if c < CHAN - 1 else -1))
+        return [x, up, down, up_up, down_down, extra]
+
+    give_codes = by_relay(give_codes, give_extra)
+    keep_codes = by_relay(keep_codes, keep_extra)
 
     def over_chan(x):
         return [x] + [go(x, lambda b, c, by=by: (b, (c + by) % CHAN)) for by in range(1, CHAN)]
-
-    give_codes = over_chan(give_codes)
-    keep_codes = over_chan(keep_codes)
 
     dec_pair = go(decoded_saved, lambda b, c: (b, c ^ 2))
     cot_pair = go(out_cotangent, lambda b, c: (b, c ^ 1))
@@ -254,26 +279,24 @@
     offsets = jnp.array([-1, 1, 0, 0], jnp.int32) * near + jnp.array([0, 0, -1, 0], jnp.int32) * far
     tile, block = slot_table(tile_source, readers, offsets)
 
+    slots = jnp.arange(SIDE, dtype=jnp.int32)
+
     def meta_of(row, index):
         node = jnp.where(tile[row] < 0, NB_DEV, tile[row] // K)
         own = (block[row] // CB_DEV == core).astype(jnp.int32)
-        return jnp.stack([node, own, block[row] % CB_DEV, index])
+        away = slots // quarter - chan
+        operand = jnp.where(away < 0, -2 * away - 1, 2 * away)
+        operand = jnp.where(jnp.abs(away) == CHAN - 1, 5, operand)
+        return jnp.stack([node, own, block[row] % CB_DEV, index, operand])
 
     def pieces_meta(row):
-        meta = meta_of(row, jnp.arange(SIDE, dtype=jnp.int32) % quarter)
-        double = jnp.concatenate([meta, meta], axis=1)
-        parts = [
-            lax.dynamic_slice_in_dim(double, (chan + CHAN - i) * quarter, quarter, 1) for i in range(CHAN)
-        ]
-        return jnp.concatenate(parts, axis=1)
+        return meta_of(row, slots % quarter)
 
     blocks = (cells, cells_sib, cotangent, cotangent_sib)
-    piece_group = [[(i, i * quarter, quarter) for i in range(CHAN)]]
-    near_meta = jnp.concatenate(
-        [meta_of(2, jnp.arange(SIDE, dtype=jnp.int32))[:, :CAP], meta_of(3, jnp.maximum(tile[3], 0))], axis=1
-    )
+    piece_group = [[(tuple(range(6)), 0, SIDE)]]
+    near_meta = jnp.concatenate([meta_of(2, slots)[:, :CAP], meta_of(3, jnp.maximum(tile[3], 0))], axis=1)
     far_part, own_part = tile_products(
-        near_meta, [far_codes, codes], blocks, [[(0, 0, CAP)], [(1, CAP, SIDE)]], [jnp.bfloat16, jnp.float32]
+        near_meta, [far_codes, codes], blocks, [[((0,), 0, CAP)], [((1,), CAP, SIDE)]], [jnp.bfloat16, jnp.float32]
     )
     got_far = go(far_part, lambda b, c: (b + 2 * far_step(b), c))
     (give_part,) = tile_products(pieces_meta(1), give_codes, blocks, piece_group, [jnp.bfloat16])

time: 185 us -> 184 us (level)
  the two profiles are of different devices: /device:TPU:5 before, /device:TPU:34 now
where the time goes in v3:
time: 184 us; the launch traced here: 181 us
  waiting for transfers between devices  70.9 us (39%)
  starting transfers between devices  67.3 us (37%)
  Pallas kernels  22.9 us (12%)
  local copies, waits for them, and re-layouts  7.34 us (4%)
  matrix products  7.18 us (4%)
  other arithmetic  3.85 us (2%)
    ppermute x32, waiting for transfers between devices, permute(): return lax.ppermute(x, ('band', 'chan'), pairs)  70.9 us
    ppermute x32, starting transfers between devices, permute(): return lax.ppermute(x, ('band', 'chan'), pairs)  67.3 us
    pallas_call x3, Pallas kernels, tile_products(): pl.pallas_call(functools.partial(products_kernel, groups, len(codes)), ou...  15.6 us
    dot_general x4, matrix products, outer(): lax.dot_general(left, right, (((0,), (0,)), ((), ())), preferred_element_...  7.18 us
    pallas_call x1, Pallas kernels, pick_tiles(): pl.pallas_call(pick_kernel, out_shape=[jax.ShapeDtypeStruct((count, BLK,...  4.56 us
    unnamed x49, local copies, waits for them, and re-layouts  3.98 us
  transfers between devices with their start and end apart: 32, of which 13 were waited for; matrix products, arithmetic and copies ran while one was open for 8% of the time, Pallas kernels for 11%

profile of v3, /device:TPU:34, one launch (start us, length us, event | category | flops | bytes accessed | tf_op | source)
XLA Modules:
  0.0 180.9 jit_solution(15053059838732469368)
XLA Ops:
  0.9 3.3 %collective-permute-start.22 = (bf16[2048,256]{1,0:T(8,128)(2,1)}, bf16[2048,256]{1,0:T(8,128)(2,1)}, u32[]{:S(2)}, u32[]{:S(2)}) collective-permute-start(bf16[2048,256]{1,0:T(8,128)(2,1)} %param.16), channel_id=1, source_target_pairs={{0,2},{1,3},{2,0},{3,1},{4,6},{5,7},{6,4},{7,5},{8,10},{9,11},{10,... | collective-permute-start | bytes 3145736 | tf_op jit(solution)/shard_map/ppermute | solution.py:29
  6.1 4.6 %pick_tiles.1 = (s32[4,128,128]{2,1,0:T(8,128)}, s32[4,128,128]{2,1,0:T(8,128)}, s32[4,128,128]{2,1,0:T(8,128)}, s32[4,128,128]{2,1,0:T(8,128)}, s32[8,128,128]{2,1,0:T(8,128)}) custom-call(s32[2]{0:T(128)} %pad_add_fusion.1.place, s32[2,16]{1,0:T(2,128)} %constant_dynamic-slice_fusion.rows, s32[32,128,128]{2,1,0:T(8,128)} %bitcast.59), custom_call_target="tpu_custom_call" | custom-call | flops 100000000 | bytes 3145728 | tf_op jit(solution)/shard_map/pick_tiles/pallas_call | solution.py:89
  10.7 9.5 %collective-permute-start.9 = (s32[4,128,128]{2,1,0:T(8,128)}, s32[4,128,128]{2,1,0:T(8,128)S(1)}, u32[]{:S(2)}, u32[]{:S(2)}) collective-permute-start(s32[4,128,128]{2,1,0:T(8,128)} %get-tuple-element.16), channel_id=1, source_target_pairs={{8,19},{9,18},{10,17},{11,16},{12,23},{13,22},{14,21},{15,20},{16,... | collective-permute-start | bytes 786440 | tf_op jit(solution)/shard_map/ppermute | solution.py:29
  23.1 1.8 fusion.25
  24.9 36.4 %collective-permute-done.9.refs_1_ = s32[4,128,128]{2,1,0:T(8,128)S(1)} collective-permute-done((s32[4,128,128]{2,1,0:T(8,128)}, s32[4,128,128]{2,1,0:T(8,128)S(1)}, u32[]{:S(2)}, u32[]{:S(2)}) %collective-permute-start.9) | collective-permute-done | bytes 262176 | tf_op jit(solution)/shard_map/ppermute | solution.py:29
  61.4 2.9 %collective-permute-start.10 = (s32[4,128,128]{2,1,0:T(8,128)S(1)}, s32[4,128,128]{2,1,0:T(8,128)S(1)}, u32[]{:S(2)}, u32[]{:S(2)}) collective-permute-start(s32[4,128,128]{2,1,0:T(8,128)S(1)} %collective-permute-done.9.refs_1_), channel_id=1, source_target_pairs={{0,1},{1,2},{2,3},{4,5},{5,6},{6,7},{8,9},{9,10},{10,11},{12,13},{... | collective-permute-start | bytes 786440 | tf_op jit(solution)/shard_map/ppermute | solution.py:29
  64.3 1.7 fusion.26
  66.0 7.5 %collective-permute-done.3.refs_1_ = s32[4,128,128]{2,1,0:T(8,128)S(1)} collective-permute-done((s32[4,128,128]{2,1,0:T(8,128)S(1)}, s32[4,128,128]{2,1,0:T(8,128)S(1)}, u32[]{:S(2)}, u32[]{:S(2)}) %collective-permute-start.3) | collective-permute-done | bytes 262176 | tf_op jit(solution)/shard_map/ppermute | solution.py:29
  73.5 1.9 %collective-permute-start.11 = (s32[4,128,128]{2,1,0:T(8,128)S(1)}, s32[4,128,128]{2,1,0:T(8,128)S(1)}, u32[]{:S(2)}, u32[]{:S(2)}) collective-permute-start(s32[4,128,128]{2,1,0:T(8,128)S(1)} %collective-permute-done.9.refs_1_), channel_id=1, source_target_pairs={{1,0},{2,1},{3,2},{5,4},{6,5},{7,6},{9,8},{10,9},{11,10},{13,12},{... | collective-permute-start | bytes 786440 | tf_op jit(solution)/shard_map/ppermute | solution.py:29
  75.5 2.0 %collective-permute-done.10.refs_2_ = s32[4,128,128]{2,1,0:T(8,128)S(1)} collective-permute-done((s32[4,128,128]{2,1,0:T(8,128)S(1)}, s32[4,128,128]{2,1,0:T(8,128)S(1)}, u32[]{:S(2)}, u32[]{:S(2)}) %collective-permute-start.10) | collective-permute-done | bytes 262176 | tf_op jit(solution)/shard_map/ppermute | solution.py:29
  77.5 1.9 %collective-permute-start.4 = (s32[4,128,128]{2,1,0:T(8,128)S(1)}, s32[4,128,128]{2,1,0:T(8,128)}, u32[]{:S(2)}, u32[]{:S(2)}) collective-permute-start(s32[4,128,128]{2,1,0:T(8,128)S(1)} %collective-permute-done.3.refs_1_), channel_id=1, source_target_pairs={{0,1},{1,2},{2,3},{4,5},{5,6},{6,7},{8,9},{9,10},{10,11},{12,13},{... | collective-permute-start | bytes 786440 | tf_op jit(solution)/shard_map/ppermute | solution.py:29
  79.4 4.6 %collective-permute-start.5 = (s32[4,128,128]{2,1,0:T(8,128)S(1)}, s32[4,128,128]{2,1,0:T(8,128)}, u32[]{:S(2)}, u32[]{:S(2)}) collective-permute-start(s32[4,128,128]{2,1,0:T(8,128)S(1)} %collective-permute-done.3.refs_1_), channel_id=1, source_target_pairs={{1,0},{2,1},{3,2},{5,4},{6,5},{7,6},{9,8},{10,9},{11,10},{13,12},{... | collective-permute-start | bytes 786440 | tf_op jit(solution)/shard_map/ppermute | solution.py:29
  84.1 2.0 %fusion.28 = f32[256,256]{1,0:T(8,128)S(1)} fusion(bf16[2048,256]{1,0:T(8,128)(2,1)} %collective-permute-done.21, bf16[2048,256]{1,0:T(8,128)(2,1)} %collective-permute-done.22), kind=kOutput, calls=%fused_computation.124 | convolution fusion | flops 268435456 | bytes 2359296 | tf_op jit(solution)/shard_map/dot_general | solution.py:329
  86.1 2.7 %collective-permute-start = (s32[8,128,128]{2,1,0:T(8,128)}, s32[8,128,128]{2,1,0:T(8,128)}, u32[]{:S(2)}, u32[]{:S(2)}) collective-permute-start(s32[8,128,128]{2,1,0:T(8,128)} %get-tuple-element.12), channel_id=1, source_target_pairs={{4,20},{5,21},{6,22},{7,23},{12,28},{13,29},{14,30},{15,31},{16,0}... | collective-permute-start | bytes 1572872 | tf_op jit(solution)/shard_map/ppermute | solution.py:29
  90.1 3.4 %collective-permute-start.13 = (s32[4,128,128]{2,1,0:T(8,128)S(1)}, s32[4,128,128]{2,1,0:T(8,128)S(1)}, u32[]{:S(2)}, u32[]{:S(2)}) collective-permute-start(s32[4,128,128]{2,1,0:T(8,128)S(1)} %collective-permute-done.11.refs_3_), channel_id=1, source_target_pairs={{1,0},{2,1},{5,4},{6,5},{9,8},{10,9},{13,12},{14,13},{17,16},{18,1... | collective-permute-start | bytes 786440 | tf_op jit(solution)/shard_map/ppermute | solution.py:29
  93.5 1.7 fusion.27
  98.5 2.3 %collective-permute-start.6 = (s32[4,128,128]{2,1,0:T(8,128)}, s32[4,128,128]{2,1,0:T(8,128)}, u32[]{:S(2)}, u32[]{:S(2)}) collective-permute-start(s32[4,128,128]{2,1,0:T(8,128)} %collective-permute-done.4.refs_2_), channel_id=1, source_target_pairs={{1,2},{2,3},{5,6},{6,7},{9,10},{10,11},{13,14},{14,15},{17,18},{18... | collective-permute-start | bytes 786440 | tf_op jit(solution)/shard_map/ppermute | solution.py:29
  100.8 3.8 %collective-permute-start.7 = (s32[4,128,128]{2,1,0:T(8,128)}, s32[4,128,128]{2,1,0:T(8,128)S(1)}, u32[]{:S(2)}, u32[]{:S(2)}) collective-permute-start(s32[4,128,128]{2,1,0:T(8,128)} %collective-permute-done.5.refs_3_), channel_id=1, source_target_pairs={{1,0},{2,1},{5,4},{6,5},{9,8},{10,9},{13,12},{14,13},{17,16},{18,1... | collective-permute-start | bytes 786440 | tf_op jit(solution)/shard_map/ppermute | solution.py:29
  107.6 4.6 %tile_products.5 = bf16[2,256,256]{2,1,0:T(8,128)(2,1)} custom-call(s32[5,16]{1,0:T(8,128)} %stack.27.refs_0_, s32[4,128,128]{2,1,0:T(8,128)} %copy-done.9, s32[4,128,128]{2,1,0:T(8,128)} %copy-done.10, s32[4,128,128]{2,1,0:T(8,128)} %copy-done.11, s32[4,128,128]{2,1,0:T(8,128)} %copy-done.12, s32[4,128,128]{2,1,0:T(8,128)} %copy-done.13, ...), custom_call_target="tpu_custom_call" | custom-call | flops 268435456 | bytes 3145728 | tf_op jit(solution)/shard_map/tile_products/pallas_call | solution.py:174
  112.2 4.7 %collective-permute-start.15 = (bf16[2,256,256]{2,1,0:T(8,128)(2,1)}, bf16[2,256,256]{2,1,0:T(8,128)(2,1)S(1)}, u32[]{:S(2)}, u32[]{:S(2)}) collective-permute-start(bf16[2,256,256]{2,1,0:T(8,128)(2,1)} %tile_products.5), channel_id=1, source_target_pairs={{8,24},{9,25},{10,26},{11,27},{12,28},{13,29},{14,30},{15,31},{16,... | collective-permute-start | bytes 786440 | tf_op jit(solution)/shard_map/ppermute | solution.py:29
  116.9 5.9 %tile_products.3 = (bf16[2,256,256]{2,1,0:T(8,128)(2,1)}, f32[2,256,256]{2,1,0:T(8,128)}) custom-call(s32[5,24]{1,0:T(8,128)} %pad_add_fusion.refs_0_, s32[8,128,128]{2,1,0:T(8,128)} %collective-permute-done.refs_1_, s32[32,128,128]{2,1,0:T(8,128)} %bitcast.60, bf16[16,128,256]{2,1,0:T(8,128)(2,1)} %bitcast.56, bf16[16,128,256]{2,1,0:T(8,128)(2,1)} %copy-done.2, ...), custom_call_target="tpu_custom_call" | custom-call | flops 402653184 | bytes 4718592 | tf_op jit(solution)/shard_map/tile_products/pallas_call | solution.py:174
  122.8 2.1 %collective-permute-start.17 = (bf16[2,256,256]{2,1,0:T(8,128)(2,1)}, bf16[2,256,256]{2,1,0:T(8,128)(2,1)S(1)}, u32[]{:S(2)}, u32[]{:S(2)}) collective-permute-start(bf16[2,256,256]{2,1,0:T(8,128)(2,1)} %get-tuple-element.18), channel_id=1, source_target_pairs={{0,16},{1,17},{2,18},{3,19},{8,24},{9,25},{10,26},{11,27},{16,32},... | collective-permute-start | bytes 786440 | tf_op jit(solution)/shard_map/ppermute | solution.py:29
  125.7 5.1 %tile_products.4 = f32[2,256,256]{2,1,0:T(8,128)} custom-call(s32[5,16]{1,0:T(8,128)} %stack.26.refs_0_, s32[4,128,128]{2,1,0:T(8,128)} %copy-done.17, s32[4,128,128]{2,1,0:T(8,128)} %collective-permute-done.4.refs_2_, s32[4,128,128]{2,1,0:T(8,128)} %collective-permute-done.5.refs_3_, s32[4,128,128]{2,1,0:T(8,128)} %collective-permute-done.6.refs_4_, ...), custom_call_target="tpu_custom_call" | custom-call | flops 268435456 | bytes 3145728 | tf_op jit(solution)/shard_map/tile_products/pallas_call | solution.py:174
  134.0 2.5 %collective-permute-start.26 = (bf16[8,16,256]{2,1,0:T(8,128)(2,1)S(1)}, bf16[8,16,256]{2,1,0:T(8,128)(2,1)S(1)}, u32[]{:S(2)}, u32[]{:S(2)}) collective-permute-start(bf16[8,16,256]{2,1,0:T(8,128)(2,1)S(1)} %get-tuple-element.34), channel_id=1, source_target_pairs={{0,192},{1,193},{2,194},{3,195},{4,196},{5,197},{6,198},{7,199},{8... | collective-permute-start | bytes 196616 | tf_op jit(solution)/shard_map/ppermute | solution.py:29
  140.4 4.1 %collective-permute-start.28 = (f32[2,16,256]{2,1,0:T(8,128)S(1)}, f32[2,16,256]{2,1,0:T(8,128)S(1)}, u32[]{:S(2)}, u32[]{:S(2)}) collective-permute-start(f32[2,16,256]{2,1,0:T(8,128)S(1)} %get-tuple-element.38), channel_id=1, source_target_pairs={{0,32},{1,33},{2,34},{3,35},{4,36},{5,37},{6,38},{7,39},{8,40},{9,... | collective-permute-start | bytes 98312 | tf_op jit(solution)/shard_map/ppermute | solution.py:29
  144.9 1.8 collective-permute-done.28
  148.4 2.7 %collective-permute-done.16 = bf16[2,256,256]{2,1,0:T(8,128)(2,1)S(1)} collective-permute-done((bf16[2,256,256]{2,1,0:T(8,128)(2,1)S(1)}, bf16[2,256,256]{2,1,0:T(8,128)(2,1)S(1)}, u32[]{:S(2)}, u32[]{:S(2)}) %collective-permute-start.16) | collective-permute-done | bytes 262176 | tf_op jit(solution)/shard_map/ppermute | solution.py:29
  151.2 3.0 %collective-permute-start.18 = (bf16[2,256,256]{2,1,0:T(8,128)(2,1)S(1)}, bf16[2,256,256]{2,1,0:T(8,128)(2,1)S(1)}, u32[]{:S(2)}, u32[]{:S(2)}) collective-permute-start(bf16[2,256,256]{2,1,0:T(8,128)(2,1)S(1)} %multiply_convert_fusion.p0), channel_id=1, source_target_pairs={{0,1},{1,2},{2,3},{3,0},{4,5},{5,6},{6,7},{7,4},{8,9},{9,10},{10,1... | collective-permute-start | bytes 786440 | tf_op jit(solution)/shard_map/ppermute | solution.py:29
  156.5 3.2 %collective-permute-start.31 = (f32[16,256]{1,0:T(8,128)S(1)}, f32[16,256]{1,0:T(8,128)S(1)}, u32[]{:S(2)}, u32[]{:S(2)}) collective-permute-start(f32[16,256]{1,0:T(8,128)S(1)} %get-tuple-element.39), channel_id=1, source_target_pairs={{0,8},{1,9},{2,136},{3,137},{4,12},{5,13},{6,140},{7,141},{8,0},{9... | collective-permute-start | bytes 49160 | tf_op jit(solution)/shard_map/ppermute | solution.py:29
  159.7 11.1 %collective-permute-done.31 = f32[16,256]{1,0:T(8,128)S(1)} collective-permute-done((f32[16,256]{1,0:T(8,128)S(1)}, f32[16,256]{1,0:T(8,128)S(1)}, u32[]{:S(2)}, u32[]{:S(2)}) %collective-permute-start.31) | collective-permute-done | bytes 16416 | tf_op jit(solution)/shard_map/ppermute | solution.py:29
  172.5 4.3 %collective-permute-done.19.p2 = bf16[2,256,256]{2,1,0:T(8,128)(2,1)S(1)} collective-permute-done((bf16[2,256,256]{2,1,0:T(8,128)(2,1)S(1)}, bf16[2,256,256]{2,1,0:T(8,128)(2,1)S(1)}, u32[]{:S(2)}, u32[]{:S(2)}) %collective-permute-start.19) | collective-permute-done | bytes 262176 | tf_op jit(solution)/shard_map/ppermute | solution.py:29
  178.3 2.7 %project.1 = (bf16[256,256]{1,0:T(8,128)(2,1)}, bf16[256,256]{1,0:T(8,128)(2,1)}) custom-call(s32[1]{0:T(128)} %bitcast.chan_ref, bf16[2,256,256]{2,1,0:T(8,128)(2,1)} %copy-done.7, bf16[2,256,256]{2,1,0:T(8,128)(2,1)} %copy-done.14, bf16[2,256,256]{2,1,0:T(8,128)(2,1)} %copy-done.15, bf16[2,256,256]{2,1,0:T(8,128)(2,1)} %copy-done.16, ...), custom_call_target="tpu_custom_call" | custom-call | flops 268435456 | bytes 4194304 | tf_op jit(solution)/shard_map/project/pallas_call | solution.py:207
  (126 shorter events, 27.7 us)
Async XLA Ops:
  0.7 60.7 %collective-permute-start.21 = (bf16[2048,256]{1,0:T(8,128)(2,1)}, bf16[2048,256]{1,0:T(8,128)(2,1)}, u32[]{:S(2)}, u32[]{:S(2)}) collective-permute-start(bf16[2048,256]{1,0:T(8,128)(2,1)} %param.15), channel_id=1, source_target_pairs={{0,1},{1,0},{2,3},{3,2},{4,5},{5,4},{6,7},{7,6},{8,9},{9,8},{10,11... | collective-permute-start | bytes 3145736 | tf_op jit(solution)/shard_map/ppermute | solution.py:29
  0.9 78.5 %collective-permute-start.22 = (bf16[2048,256]{1,0:T(8,128)(2,1)}, bf16[2048,256]{1,0:T(8,128)(2,1)}, u32[]{:S(2)}, u32[]{:S(2)}) collective-permute-start(bf16[2048,256]{1,0:T(8,128)(2,1)} %param.16), channel_id=1, source_target_pairs={{0,2},{1,3},{2,0},{3,1},{4,6},{5,7},{6,4},{7,5},{8,10},{9,11},{10,... | collective-permute-start | bytes 3145736 | tf_op jit(solution)/shard_map/ppermute | solution.py:29
  10.7 50.6 %collective-permute-start.9 = (s32[4,128,128]{2,1,0:T(8,128)}, s32[4,128,128]{2,1,0:T(8,128)S(1)}, u32[]{:S(2)}, u32[]{:S(2)}) collective-permute-start(s32[4,128,128]{2,1,0:T(8,128)} %get-tuple-element.16), channel_id=1, source_target_pairs={{8,19},{9,18},{10,17},{11,16},{12,23},{13,22},{14,21},{15,20},{16,... | collective-permute-start | bytes 786440 | tf_op jit(solution)/shard_map/ppermute | solution.py:29
  20.2 41.1 %collective-permute-start.14 = (s32[4,128,128]{2,1,0:T(8,128)}, s32[4,128,128]{2,1,0:T(8,128)}, u32[]{:S(2)}, u32[]{:S(2)}) collective-permute-start(s32[4,128,128]{2,1,0:T(8,128)} %get-tuple-element.17), channel_id=1, source_target_pairs={{8,19},{11,16},{12,23},{15,20},{16,11},{19,8},{20,15},{23,12},{24,... | collective-permute-start | bytes 786440 | tf_op jit(solution)/shard_map/ppermute | solution.py:29
  21.6 79.2 %collective-permute-start.1 = (bf16[16,128,256]{2,1,0:T(8,128)(2,1)S(1)}, bf16[16,128,256]{2,1,0:T(8,128)(2,1)S(1)}, u32[]{:S(2)}, u32[]{:S(2)}) collective-permute-start(bf16[16,128,256]{2,1,0:T(8,128)(2,1)S(1)} %bitcast.58), channel_id=1, source_target_pairs={{0,4},{1,5},{2,6},{3,7},{4,0},{5,1},{6,2},{7,3},{8,12},{9,13},{10,... | collective-permute-start | bytes 3145736 | tf_op jit(solution)/shard_map/ppermute | solution.py:29
  61.3 43.4 %collective-permute-start.2 = (bf16[16,128,256]{2,1,0:T(8,128)(2,1)S(1)}, bf16[16,128,256]{2,1,0:T(8,128)(2,1)S(1)}, u32[]{:S(2)}, u32[]{:S(2)}) collective-permute-start(bf16[16,128,256]{2,1,0:T(8,128)(2,1)S(1)} %bitcast.54), channel_id=1, source_target_pairs={{0,4},{1,5},{2,6},{3,7},{4,0},{5,1},{6,2},{7,3},{8,12},{9,13},{10,... | collective-permute-start | bytes 3145736 | tf_op jit(solution)/shard_map/ppermute | solution.py:29
  61.3 12.3 %collective-permute-start.3 = (s32[4,128,128]{2,1,0:T(8,128)S(1)}, s32[4,128,128]{2,1,0:T(8,128)S(1)}, u32[]{:S(2)}, u32[]{:S(2)}) collective-permute-start(s32[4,128,128]{2,1,0:T(8,128)S(1)} %copy-done.23), channel_id=1, source_target_pairs={{0,11},{1,10},{2,9},{3,8},{4,15},{5,14},{6,13},{7,12},{8,3},{9,2},... | collective-permute-start | bytes 786440 | tf_op jit(solution)/shard_map/ppermute | solution.py:29
  61.4 16.1 %collective-permute-start.10 = (s32[4,128,128]{2,1,0:T(8,128)S(1)}, s32[4,128,128]{2,1,0:T(8,128)S(1)}, u32[]{:S(2)}, u32[]{:S(2)}) collective-permute-start(s32[4,128,128]{2,1,0:T(8,128)S(1)} %collective-permute-done.9.refs_1_), channel_id=1, source_target_pairs={{0,1},{1,2},{2,3},{4,5},{5,6},{6,7},{8,9},{9,10},{10,11},{12,13},{... | collective-permute-start | bytes 786440 | tf_op jit(solution)/shard_map/ppermute | solution.py:29
  73.5 12.5 %collective-permute-start.11 = (s32[4,128,128]{2,1,0:T(8,128)S(1)}, s32[4,128,128]{2,1,0:T(8,128)S(1)}, u32[]{:S(2)}, u32[]{:S(2)}) collective-permute-start(s32[4,128,128]{2,1,0:T(8,128)S(1)} %collective-permute-done.9.refs_1_), channel_id=1, source_target_pairs={{1,0},{2,1},{3,2},{5,4},{6,5},{7,6},{9,8},{10,9},{11,10},{13,12},{... | collective-permute-start | bytes 786440 | tf_op jit(solution)/shard_map/ppermute | solution.py:29
  77.5 11.3 %collective-permute-start.4 = (s32[4,128,128]{2,1,0:T(8,128)S(1)}, s32[4,128,128]{2,1,0:T(8,128)}, u32[]{:S(2)}, u32[]{:S(2)}) collective-permute-start(s32[4,128,128]{2,1,0:T(8,128)S(1)} %collective-permute-done.3.refs_1_), channel_id=1, source_target_pairs={{0,1},{1,2},{2,3},{4,5},{5,6},{6,7},{8,9},{9,10},{10,11},{12,13},{... | collective-permute-start | bytes 786440 | tf_op jit(solution)/shard_map/ppermute | solution.py:29
  79.4 10.7 %collective-permute-start.5 = (s32[4,128,128]{2,1,0:T(8,128)S(1)}, s32[4,128,128]{2,1,0:T(8,128)}, u32[]{:S(2)}, u32[]{:S(2)}) collective-permute-start(s32[4,128,128]{2,1,0:T(8,128)S(1)} %collective-permute-done.3.refs_1_), channel_id=1, source_target_pairs={{1,0},{2,1},{3,2},{5,4},{6,5},{7,6},{9,8},{10,9},{11,10},{13,12},{... | collective-permute-start | bytes 786440 | tf_op jit(solution)/shard_map/ppermute | solution.py:29
  86.1 26.1 %collective-permute-start = (s32[8,128,128]{2,1,0:T(8,128)}, s32[8,128,128]{2,1,0:T(8,128)}, u32[]{:S(2)}, u32[]{:S(2)}) collective-permute-start(s32[8,128,128]{2,1,0:T(8,128)} %get-tuple-element.12), channel_id=1, source_target_pairs={{4,20},{5,21},{6,22},{7,23},{12,28},{13,29},{14,30},{15,31},{16,0}... | collective-permute-start | bytes 1572872 | tf_op jit(solution)/shard_map/ppermute | solution.py:29
  88.8 7.4 %collective-permute-start.12 = (s32[4,128,128]{2,1,0:T(8,128)S(1)}, s32[4,128,128]{2,1,0:T(8,128)S(1)}, u32[]{:S(2)}, u32[]{:S(2)}) collective-permute-start(s32[4,128,128]{2,1,0:T(8,128)S(1)} %collective-permute-done.10.refs_2_), channel_id=1, source_target_pairs={{1,2},{2,3},{5,6},{6,7},{9,10},{10,11},{13,14},{14,15},{17,18},{18... | collective-permute-start | bytes 786440 | tf_op jit(solution)/shard_map/ppermute | solution.py:29
  90.1 8.4 %collective-permute-start.13 = (s32[4,128,128]{2,1,0:T(8,128)S(1)}, s32[4,128,128]{2,1,0:T(8,128)S(1)}, u32[]{:S(2)}, u32[]{:S(2)}) collective-permute-start(s32[4,128,128]{2,1,0:T(8,128)S(1)} %collective-permute-done.11.refs_3_), channel_id=1, source_target_pairs={{1,0},{2,1},{5,4},{6,5},{9,8},{10,9},{13,12},{14,13},{17,16},{18,1... | collective-permute-start | bytes 786440 | tf_op jit(solution)/shard_map/ppermute | solution.py:29
  96.2 26.6 %collective-permute-start.8 = (s32[4,128,128]{2,1,0:T(8,128)}, s32[4,128,128]{2,1,0:T(8,128)}, u32[]{:S(2)}, u32[]{:S(2)}) collective-permute-start(s32[4,128,128]{2,1,0:T(8,128)} %get-tuple-element.15), channel_id=1, source_target_pairs={{0,11},{3,8},{4,15},{7,12},{8,3},{11,0},{12,7},{15,4},{16,27},{19,... | collective-permute-start | bytes 786440 | tf_op jit(solution)/shard_map/ppermute | solution.py:29
  98.5 26.5 %collective-permute-start.6 = (s32[4,128,128]{2,1,0:T(8,128)}, s32[4,128,128]{2,1,0:T(8,128)}, u32[]{:S(2)}, u32[]{:S(2)}) collective-permute-start(s32[4,128,128]{2,1,0:T(8,128)} %collective-permute-done.4.refs_2_), channel_id=1, source_target_pairs={{1,2},{2,3},{5,6},{6,7},{9,10},{10,11},{13,14},{14,15},{17,18},{18... | collective-permute-start | bytes 786440 | tf_op jit(solution)/shard_map/ppermute | solution.py:29
  100.8 24.2 %collective-permute-start.7 = (s32[4,128,128]{2,1,0:T(8,128)}, s32[4,128,128]{2,1,0:T(8,128)S(1)}, u32[]{:S(2)}, u32[]{:S(2)}) collective-permute-start(s32[4,128,128]{2,1,0:T(8,128)} %collective-permute-done.5.refs_3_), channel_id=1, source_target_pairs={{1,0},{2,1},{5,4},{6,5},{9,8},{10,9},{13,12},{14,13},{17,16},{18,1... | collective-permute-start | bytes 786440 | tf_op jit(solution)/shard_map/ppermute | solution.py:29
  105.6 25.2 %collective-permute-start.23 = (bf16[4,8,16,256]{3,2,1,0:T(8,128)(2,1)}, bf16[4,8,16,256]{3,2,1,0:T(8,128)(2,1)S(1)}, u32[]{:S(2)}, u32[]{:S(2)}) collective-permute-start(bf16[4,8,16,256]{3,2,1,0:T(8,128)(2,1)} %fusion), channel_id=1, source_target_pairs={{0,4},{1,5},{2,6},{3,7},{4,0},{5,1},{6,2},{7,3},{8,12},{9,13},{10,... | collective-permute-start | bytes 786440 | tf_op jit(solution)/shard_map/ppermute | solution.py:29
  112.2 24.3 %collective-permute-start.15 = (bf16[2,256,256]{2,1,0:T(8,128)(2,1)}, bf16[2,256,256]{2,1,0:T(8,128)(2,1)S(1)}, u32[]{:S(2)}, u32[]{:S(2)}) collective-permute-start(bf16[2,256,256]{2,1,0:T(8,128)(2,1)} %tile_products.5), channel_id=1, source_target_pairs={{8,24},{9,25},{10,26},{11,27},{12,28},{13,29},{14,30},{15,31},{16,... | collective-permute-start | bytes 786440 | tf_op jit(solution)/shard_map/ppermute | solution.py:29
  122.8 25.6 %collective-permute-start.17 = (bf16[2,256,256]{2,1,0:T(8,128)(2,1)}, bf16[2,256,256]{2,1,0:T(8,128)(2,1)S(1)}, u32[]{:S(2)}, u32[]{:S(2)}) collective-permute-start(bf16[2,256,256]{2,1,0:T(8,128)(2,1)} %get-tuple-element.18), channel_id=1, source_target_pairs={{0,16},{1,17},{2,18},{3,19},{8,24},{9,25},{10,26},{11,27},{16,32},... | collective-permute-start | bytes 786440 | tf_op jit(solution)/shard_map/ppermute | solution.py:29
  131.0 7.0 %collective-permute-start.24 = (bf16[8,16,256]{2,1,0:T(8,128)(2,1)S(1)}, bf16[8,16,256]{2,1,0:T(8,128)(2,1)S(1)}, u32[]{:S(2)}, u32[]{:S(2)}) collective-permute-start(bf16[8,16,256]{2,1,0:T(8,128)(2,1)S(1)} %get-tuple-element.33), channel_id=1, source_target_pairs={{0,64},{1,65},{2,66},{3,67},{4,68},{5,69},{6,70},{7,71},{8,72},{9,... | collective-permute-start | bytes 196616 | tf_op jit(solution)/shard_map/ppermute | solution.py:29
  132.4 5.8 %collective-permute-start.25 = (bf16[8,16,256]{2,1,0:T(8,128)(2,1)S(1)}, bf16[8,16,256]{2,1,0:T(8,128)(2,1)S(1)}, u32[]{:S(2)}, u32[]{:S(2)}) collective-permute-start(bf16[8,16,256]{2,1,0:T(8,128)(2,1)S(1)} %get-tuple-element.35), channel_id=1, source_target_pairs={{0,128},{1,129},{2,130},{3,131},{4,132},{5,133},{6,134},{7,135},{8... | collective-permute-start | bytes 196616 | tf_op jit(solution)/shard_map/ppermute | solution.py:29
  134.0 4.8 %collective-permute-start.26 = (bf16[8,16,256]{2,1,0:T(8,128)(2,1)S(1)}, bf16[8,16,256]{2,1,0:T(8,128)(2,1)S(1)}, u32[]{:S(2)}, u32[]{:S(2)}) collective-permute-start(bf16[8,16,256]{2,1,0:T(8,128)(2,1)S(1)} %get-tuple-element.34), channel_id=1, source_target_pairs={{0,192},{1,193},{2,194},{3,195},{4,196},{5,197},{6,198},{7,199},{8... | collective-permute-start | bytes 196616 | tf_op jit(solution)/shard_map/ppermute | solution.py:29
  137.6 13.5 %collective-permute-start.16 = (bf16[2,256,256]{2,1,0:T(8,128)(2,1)S(1)}, bf16[2,256,256]{2,1,0:T(8,128)(2,1)S(1)}, u32[]{:S(2)}, u32[]{:S(2)}) collective-permute-start(bf16[2,256,256]{2,1,0:T(8,128)(2,1)S(1)} %add_convert_fusion), channel_id=1, source_target_pairs={{0,8},{1,9},{2,10},{3,11},{4,12},{5,13},{6,14},{7,15},{8,0},{9,1},... | collective-permute-start | bytes 786440 | tf_op jit(solution)/shard_map/ppermute | solution.py:29
  138.9 6.0 %collective-permute-start.27 = (f32[2,16,256]{2,1,0:T(8,128)S(1)}, f32[2,16,256]{2,1,0:T(8,128)S(1)}, u32[]{:S(2)}, u32[]{:S(2)}) collective-permute-start(f32[2,16,256]{2,1,0:T(8,128)S(1)} %get-tuple-element.36), channel_id=1, source_target_pairs={{0,16},{1,17},{2,18},{3,19},{4,20},{5,21},{6,22},{7,23},{8,24},{9,... | collective-permute-start | bytes 98312 | tf_op jit(solution)/shard_map/ppermute | solution.py:29
  140.4 6.4 %collective-permute-start.28 = (f32[2,16,256]{2,1,0:T(8,128)S(1)}, f32[2,16,256]{2,1,0:T(8,128)S(1)}, u32[]{:S(2)}, u32[]{:S(2)}) collective-permute-start(f32[2,16,256]{2,1,0:T(8,128)S(1)} %get-tuple-element.38), channel_id=1, source_target_pairs={{0,32},{1,33},{2,34},{3,35},{4,36},{5,37},{6,38},{7,39},{8,40},{9,... | collective-permute-start | bytes 98312 | tf_op jit(solution)/shard_map/ppermute | solution.py:29
  144.5 3.9 %collective-permute-start.29 = (f32[2,16,256]{2,1,0:T(8,128)S(1)}, f32[2,16,256]{2,1,0:T(8,128)S(1)}, u32[]{:S(2)}, u32[]{:S(2)}) collective-permute-start(f32[2,16,256]{2,1,0:T(8,128)S(1)} %get-tuple-element.37), channel_id=1, source_target_pairs={{0,48},{1,49},{2,50},{3,51},{4,52},{5,53},{6,54},{7,55},{8,56},{9,... | collective-permute-start | bytes 98312 | tf_op jit(solution)/shard_map/ppermute | solution.py:29
  151.2 21.3 %collective-permute-start.18 = (bf16[2,256,256]{2,1,0:T(8,128)(2,1)S(1)}, bf16[2,256,256]{2,1,0:T(8,128)(2,1)S(1)}, u32[]{:S(2)}, u32[]{:S(2)}) collective-permute-start(bf16[2,256,256]{2,1,0:T(8,128)(2,1)S(1)} %multiply_convert_fusion.p0), channel_id=1, source_target_pairs={{0,1},{1,2},{2,3},{3,0},{4,5},{5,6},{6,7},{7,4},{8,9},{9,10},{10,1... | collective-permute-start | bytes 786440 | tf_op jit(solution)/shard_map/ppermute | solution.py:29
  154.2 22.6 %collective-permute-start.19 = (bf16[2,256,256]{2,1,0:T(8,128)(2,1)S(1)}, bf16[2,256,256]{2,1,0:T(8,128)(2,1)S(1)}, u32[]{:S(2)}, u32[]{:S(2)}) collective-permute-start(bf16[2,256,256]{2,1,0:T(8,128)(2,1)S(1)} %multiply_convert_fusion.p0), channel_id=1, source_target_pairs={{0,2},{1,3},{2,0},{3,1},{4,6},{5,7},{6,4},{7,5},{8,10},{9,11},{10,... | collective-permute-start | bytes 786440 | tf_op jit(solution)/shard_map/ppermute | solution.py:29
  154.2 22.6 %collective-permute-start.20 = (bf16[2,256,256]{2,1,0:T(8,128)(2,1)S(1)}, bf16[2,256,256]{2,1,0:T(8,128)(2,1)S(1)}, u32[]{:S(2)}, u32[]{:S(2)}) collective-permute-start(bf16[2,256,256]{2,1,0:T(8,128)(2,1)S(1)} %multiply_convert_fusion.p0), channel_id=1, source_target_pairs={{0,3},{1,0},{2,1},{3,2},{4,7},{5,4},{6,5},{7,6},{8,11},{9,8},{10,9... | collective-permute-start | bytes 786440 | tf_op jit(solution)/shard_map/ppermute | solution.py:29
  155.8 3.9 %collective-permute-start.30 = (f32[16,256]{1,0:T(8,128)S(1)}, f32[16,256]{1,0:T(8,128)S(1)}, u32[]{:S(2)}, u32[]{:S(2)}) collective-permute-start(f32[16,256]{1,0:T(8,128)S(1)} %get-tuple-element.40), channel_id=1, source_target_pairs={{0,0},{1,1},{2,128},{3,129},{4,4},{5,5},{6,132},{7,133},{8,8},{9,9... | collective-permute-start | bytes 49160 | tf_op jit(solution)/shard_map/ppermute | solution.py:29
  156.5 14.3 %collective-permute-start.31 = (f32[16,256]{1,0:T(8,128)S(1)}, f32[16,256]{1,0:T(8,128)S(1)}, u32[]{:S(2)}, u32[]{:S(2)}) collective-permute-start(f32[16,256]{1,0:T(8,128)S(1)} %get-tuple-element.39), channel_id=1, source_target_pairs={{0,8},{1,9},{2,136},{3,137},{4,12},{5,13},{6,140},{7,141},{8,0},{9... | collective-permute-start | bytes 49160 | tf_op jit(solution)/shard_map/ppermute | solution.py:29
  (24 other events, 370.7 us)

commit v4 on v3

--- a/solution.py
+++ b/solution.py
@@ -47,18 +47,18 @@
     return tile, block
 
 
-def pick_kernel(place, rows, codes, give_out, keep_out, give_extra, keep_extra, far_out, listed, sems):
+def pick_kernel(picks, place, rows, codes, *refs):
+    outs, (listed, sems) = refs[:-2], refs[-2:]
     band, chan = place[0], place[1]
     chip = band // 2
     near = 1 - 2 * (chip % 2)
     far = 2 - 4 * (band % 2)
-    first = (CHAN - 1 - chan) * (SIDE // CHAN)
-    extra = chan * (SIDE // CHAN)
+    starts = {"mirrored": (CHAN - 1 - chan) * (SIDE // CHAN), "own": chan * (SIDE // CHAN), "all": 0}
     for i in range(3 * SIDE):
         listed[i] = 0
 
     def sort(tile, counts):
-        offset = rows[tile // K, tile % K] // PAIR_BLOCKS - chip
+        offset = rows[tile % K, band * NB_DEV + tile // K] // PAIR_BLOCKS - chip
         after = []
         for kind, (wanted, count) in enumerate(zip((-near, near, -far), counts)):
             hit = offset == wanted
@@ -73,21 +73,20 @@
     zero = jnp.int32(0)
     lax.fori_loop(0, TILES, sort, (zero, zero, zero))
     copies = []
-    picks = ((0, give_out, first), (1, keep_out, first), (0, give_extra, extra), (1, keep_extra, extra), (2, far_out, 0))
-    for kind, out, start in picks:
+    for out, (kind, which) in zip(outs, picks):
         for i in range(out.shape[0]):
-            tile = listed[kind * SIDE + start + i]
+            tile = listed[kind * SIDE + starts[which] + i]
             copies.append(pltpu.make_async_copy(codes.at[tile], out.at[i], sems.at[len(copies)]))
             copies[-1].start()
     for copy in copies:
         copy.wait()
 
 
-def pick_tiles(place, rows, codes):
-    counts = (SIDE // CHAN,) * 4 + (CAP,)
+def pick_tiles(place, rows, codes, picks):
+    counts = [CAP if which == "all" else SIDE // CHAN for _, which in picks]
     smem = pl.BlockSpec(memory_space=pltpu.SMEM)
     return pl.pallas_call(
-        pick_kernel,
+        functools.partial(pick_kernel, picks),
         out_shape=[jax.ShapeDtypeStruct((count, BLK, BLK), codes.dtype) for count in counts],
         in_specs=[smem, smem, pl.BlockSpec(memory_space=pl.ANY)],
         out_specs=[pl.BlockSpec(memory_space=pltpu.VMEM)] * len(counts),
@@ -240,9 +239,9 @@
     cells_sib = go(cells, lambda b, c: (b ^ 1, c))
     cotangent_sib = go(cotangent, lambda b, c: (b ^ 1, c))
 
-    rows = lax.dynamic_slice_in_dim(tile_source, band * NB_DEV, NB_DEV, 0)
     place = jnp.stack([band, chan]).astype(jnp.int32)
-    give_codes, keep_codes, give_extra, keep_extra, far_codes = pick_tiles(place, rows, codes)
+    give_codes, keep_codes = pick_tiles(place, tile_source.T, codes, ((0, "mirrored"), (1, "mirrored")))
+    give_extra, keep_extra, far_codes = pick_tiles(place, tile_source.T, codes, ((0, "own"), (1, "own"), (2, "all")))
     ends = (0, CHAN - 1)
 
     def mirrored(c):
@@ -257,21 +256,19 @@
     keep_extra = go(keep_extra, lambda b, c: (b ^ 2, if_end(c)))
     far_codes = go(far_codes, lambda b, c: (b - 2 * far_step(b), c))
 
-    def by_relay(x, extra):
-        up = go(x, lambda b, c: (b, c + 1))
-        down = go(x, lambda b, c: (b, c - 1))
-        up_up = go(up, lambda b, c: (b, c + 1 if c > 0 else -1))
-        down_down = go(down, lambda b, c: (b, c - 1 if c < CHAN - 1 else -1))
-        return [x, up, down, up_up, down_down, extra]
-
-    give_codes = by_relay(give_codes, give_extra)
-    keep_codes = by_relay(keep_codes, keep_extra)
+    def along_chan(x, extra):
+        return [x] + [go(x, lambda b, c, by=by: (b, c + by)) for by in (1, -1, 2, -2)] + [extra]
+
+    give_codes = along_chan(give_codes, give_extra)
+    keep_codes = along_chan(keep_codes, keep_extra)
 
     def over_chan(x):
         return [x] + [go(x, lambda b, c, by=by: (b, (c + by) % CHAN)) for by in range(1, CHAN)]
 
-    dec_pair = go(decoded_saved, lambda b, c: (b, c ^ 2))
+    half = decoded_saved.shape[0] // 2
+    dec_first = go(decoded_saved[:half], lambda b, c: (b, c ^ 2))
     cot_pair = go(out_cotangent, lambda b, c: (b, c ^ 1))
+    dec_second = go(decoded_saved[half:], lambda b, c: (b, c ^ 2))
 
     near = near_step(band)
     far = far_step_traced(core)
@@ -309,7 +306,7 @@
     pieces = over_chan(aggregates)
     hidden_nodes, node_grad = project(chan, pieces, enc_mix, dec_proj, node_embed)
 
-    w_dec_grad = projection_gradient(go, out_cotangent, decoded_saved, cot_pair, dec_pair, bands)
+    w_dec_grad = projection_gradient(go, out_cotangent, decoded_saved, cot_pair, (dec_first, dec_second), bands)
     return (hidden_nodes, node_grad, w_dec_grad)
 
 
@@ -328,9 +325,12 @@
     def outer(left, right):
         return lax.dot_general(left, right, (((0,), (0,)), ((), ())), preferred_element_type=jnp.float32)
 
+    half = cot.shape[0] // 2
     first = outer(cot, dec)
-    third = outer(cot, dec_pair)
-    second, fourth = outer(cot_pair, dec), outer(cot_pair, dec_pair)
+    third = lax.optimization_barrier(outer(cot[:half], dec_pair[0]))
+    second = outer(cot_pair, dec)
+    third = third + outer(cot[half:], dec_pair[1])
+    fourth = outer(cot_pair[:half], dec_pair[0]) + outer(cot_pair[half:], dec_pair[1])
     whole = jnp.stack([first, second, third, fourth])
     halves = whole.reshape(4, 8, 2, rows, channels)
     own = lax.dynamic_index_in_dim(halves, core, 2, keepdims=False)

time: 184 us -> 195 us (1.060)
  the two profiles are of different devices: /device:TPU:34 before, /device:TPU:7 now
where the time goes in v4:
time: 195 us; the launch traced here: 194 us
  starting transfers between devices  96.2 us (49%)
  waiting for transfers between devices  51.1 us (26%)
  Pallas kernels  26 us (13%)
  matrix products  7.99 us (4%)
  local copies, waits for them, and re-layouts  7.34 us (4%)
  other arithmetic  3.86 us (2%)
    ppermute x33, starting transfers between devices, permute(): return lax.ppermute(x, ('band', 'chan'), pairs)  96.2 us
    ppermute x33, waiting for transfers between devices, permute(): return lax.ppermute(x, ('band', 'chan'), pairs)  51.1 us
    pallas_call x3, Pallas kernels, tile_products(): pl.pallas_call(functools.partial(products_kernel, groups, len(codes)), ou...  15.3 us
    pallas_call x2, Pallas kernels, pick_tiles(): pl.pallas_call(functools.partial(pick_kernel, picks), out_shape=[jax.Shap...  8.05 us
    dot_general x6, matrix products, outer(): lax.dot_general(left, right, (((0,), (0,)), ((), ())), preferred_element_...  7.99 us
  transfers between devices with their start and end apart: 33, of which 7 were waited for; matrix products, arithmetic and copies ran while one was open for 7% of the time, Pallas kernels for 12%

profile of v4, /device:TPU:7, one launch (start us, length us, event | category | flops | bytes accessed | tf_op | source)
XLA Modules:
  0.0 194.0 jit_solution(2415609520354488698)
XLA Ops:
  0.6 2.3 %fusion.32 = (bf16[1024,256]{1,0:T(8,128)(2,1)}, bf16[1024,256]{1,0:T(8,128)(2,1)}) fusion(bf16[2048,256]{1,0:T(8,128)(2,1)} %param.16), kind=kLoop, calls=%fused_computation.128 | loop fusion | bytes 2097152 | tf_op jit(solution)/shard_map/slice | solution.py:269
  2.9 3.0 %collective-permute-start.23 = (bf16[1024,256]{1,0:T(8,128)(2,1)}, bf16[1024,256]{1,0:T(8,128)(2,1)}, u32[]{:S(2)}, u32[]{:S(2)}) collective-permute-start(bf16[1024,256]{1,0:T(8,128)(2,1)} %get-tuple-element.34), channel_id=1, source_target_pairs={{0,2},{1,3},{2,0},{3,1},{4,6},{5,7},{6,4},{7,5},{8,10},{9,11},{10,... | collective-permute-start | bytes 1572872 | tf_op jit(solution)/shard_map/ppermute | solution.py:29
  5.9 1.6 collective-permute-start.21
  8.2 4.0 %pick_tiles.3 = (s32[4,128,128]{2,1,0:T(8,128)}, s32[4,128,128]{2,1,0:T(8,128)}) custom-call(s32[2]{0:T(128)} %pad_add_fusion.1.place, s32[16,128]{1,0:T(8,128)} %bitcast.69, s32[32,128,128]{2,1,0:T(8,128)} %bitcast.52), custom_call_target="tpu_custom_call" | custom-call | flops 100000000 | bytes 1048576 | tf_op jit(solution)/shard_map/pick_tiles/pallas_call | solution.py:88
  12.2 8.5 %collective-permute-start.9 = (s32[4,128,128]{2,1,0:T(8,128)}, s32[4,128,128]{2,1,0:T(8,128)S(1)}, u32[]{:S(2)}, u32[]{:S(2)}) collective-permute-start(s32[4,128,128]{2,1,0:T(8,128)} %get-tuple-element.16), channel_id=1, source_target_pairs={{8,19},{9,18},{10,17},{11,16},{12,23},{13,22},{14,21},{15,20},{16,... | collective-permute-start | bytes 786440 | tf_op jit(solution)/shard_map/ppermute | solution.py:29
  20.7 4.1 %pick_tiles.2 = (s32[4,128,128]{2,1,0:T(8,128)}, s32[4,128,128]{2,1,0:T(8,128)}, s32[8,128,128]{2,1,0:T(8,128)}) custom-call(s32[2]{0:T(128)} %pad_add_fusion.1.place, s32[16,128]{1,0:T(8,128)} %bitcast.70, s32[32,128,128]{2,1,0:T(8,128)} %bitcast.53), custom_call_target="tpu_custom_call" | custom-call | flops 100000000 | bytes 2097152 | tf_op jit(solution)/shard_map/pick_tiles/pallas_call | solution.py:88
  24.8 2.3 %collective-permute-start.14 = (s32[4,128,128]{2,1,0:T(8,128)}, s32[4,128,128]{2,1,0:T(8,128)}, u32[]{:S(2)}, u32[]{:S(2)}) collective-permute-start(s32[4,128,128]{2,1,0:T(8,128)} %get-tuple-element.17), channel_id=1, source_target_pairs={{8,19},{11,16},{12,23},{15,20},{16,11},{19,8},{20,15},{23,12},{24,... | collective-permute-start | bytes 786440 | tf_op jit(solution)/shard_map/ppermute | solution.py:29
  29.2 21.4 %collective-permute-done.22 = bf16[1024,256]{1,0:T(8,128)(2,1)} collective-permute-done((bf16[1024,256]{1,0:T(8,128)(2,1)}, bf16[1024,256]{1,0:T(8,128)(2,1)}, u32[]{:S(2)}, u32[]{:S(2)}) %collective-permute-start.22) | collective-permute-done | bytes 524320 | tf_op jit(solution)/shard_map/ppermute | solution.py:29
  50.6 9.3 %collective-permute-start.3 = (s32[4,128,128]{2,1,0:T(8,128)S(1)}, s32[4,128,128]{2,1,0:T(8,128)}, u32[]{:S(2)}, u32[]{:S(2)}) collective-permute-start(s32[4,128,128]{2,1,0:T(8,128)S(1)} %copy-done.27), channel_id=1, source_target_pairs={{0,11},{1,10},{2,9},{3,8},{4,15},{5,14},{6,13},{7,12},{8,3},{9,2},... | collective-permute-start | bytes 786440 | tf_op jit(solution)/shard_map/ppermute | solution.py:29
  61.3 2.0 %collective-permute-start.1 = (bf16[16,128,256]{2,1,0:T(8,128)(2,1)S(1)}, bf16[16,128,256]{2,1,0:T(8,128)(2,1)S(1)}, u32[]{:S(2)}, u32[]{:S(2)}) collective-permute-start(bf16[16,128,256]{2,1,0:T(8,128)(2,1)S(1)} %bitcast.62), channel_id=1, source_target_pairs={{0,4},{1,5},{2,6},{3,7},{4,0},{5,1},{6,2},{7,3},{8,12},{9,13},{10,... | collective-permute-start | bytes 3145736 | tf_op jit(solution)/shard_map/ppermute | solution.py:29
  64.9 1.9 collective-permute-start.8
  66.8 7.0 %collective-permute-done.3.refs_1_ = s32[4,128,128]{2,1,0:T(8,128)} collective-permute-done((s32[4,128,128]{2,1,0:T(8,128)S(1)}, s32[4,128,128]{2,1,0:T(8,128)}, u32[]{:S(2)}, u32[]{:S(2)}) %collective-permute-start.3) | collective-permute-done | bytes 262176 | tf_op jit(solution)/shard_map/ppermute | solution.py:29
  76.5 1.7 fusion.34
  79.4 3.2 %collective-permute-start = (s32[8,128,128]{2,1,0:T(8,128)S(1)}, s32[8,128,128]{2,1,0:T(8,128)S(1)}, u32[]{:S(2)}, u32[]{:S(2)}) collective-permute-start(s32[8,128,128]{2,1,0:T(8,128)S(1)} %copy-done.25), channel_id=1, source_target_pairs={{4,20},{5,21},{6,22},{7,23},{12,28},{13,29},{14,30},{15,31},{16,0}... | collective-permute-start | bytes 1572872 | tf_op jit(solution)/shard_map/ppermute | solution.py:29
  89.2 6.2 %collective-permute-start.4 = (s32[4,128,128]{2,1,0:T(8,128)}, s32[4,128,128]{2,1,0:T(8,128)}, u32[]{:S(2)}, u32[]{:S(2)}) collective-permute-start(s32[4,128,128]{2,1,0:T(8,128)} %collective-permute-done.3.refs_1_), channel_id=1, source_target_pairs={{0,1},{1,2},{2,3},{4,5},{5,6},{6,7},{8,9},{9,10},{10,11},{12,13},{... | collective-permute-start | bytes 786440 | tf_op jit(solution)/shard_map/ppermute | solution.py:29
  97.7 4.4 %collective-permute-start.6 = (s32[4,128,128]{2,1,0:T(8,128)}, s32[4,128,128]{2,1,0:T(8,128)}, u32[]{:S(2)}, u32[]{:S(2)}) collective-permute-start(s32[4,128,128]{2,1,0:T(8,128)} %collective-permute-done.3.refs_1_), channel_id=1, source_target_pairs={{0,2},{1,3},{4,6},{5,7},{8,10},{9,11},{12,14},{13,15},{16,18},{17,... | collective-permute-start | bytes 786440 | tf_op jit(solution)/shard_map/ppermute | solution.py:29
  103.4 10.2 %collective-permute-start.24 = (bf16[4,8,16,256]{3,2,1,0:T(8,128)(2,1)}, bf16[4,8,16,256]{3,2,1,0:T(8,128)(2,1)S(1)}, u32[]{:S(2)}, u32[]{:S(2)}) collective-permute-start(bf16[4,8,16,256]{3,2,1,0:T(8,128)(2,1)} %fusion.7), channel_id=1, source_target_pairs={{0,4},{1,5},{2,6},{3,7},{4,0},{5,1},{6,2},{7,3},{8,12},{9,13},{10,... | collective-permute-start | bytes 786440 | tf_op jit(solution)/shard_map/ppermute | solution.py:29
  115.6 4.6 %tile_products.5 = bf16[2,256,256]{2,1,0:T(8,128)(2,1)} custom-call(s32[5,16]{1,0:T(8,128)} %stack.27.refs_0_, s32[4,128,128]{2,1,0:T(8,128)} %copy-done.8, s32[4,128,128]{2,1,0:T(8,128)} %copy-done.9, s32[4,128,128]{2,1,0:T(8,128)} %copy-done.10, s32[4,128,128]{2,1,0:T(8,128)} %copy-done.11, s32[4,128,128]{2,1,0:T(8,128)} %copy-done.12, ...), custom_call_target="tpu_custom_call" | custom-call | flops 268435456 | bytes 3145728 | tf_op jit(solution)/shard_map/tile_products/pallas_call | solution.py:173
  120.2 5.9 %tile_products.3 = (bf16[2,256,256]{2,1,0:T(8,128)(2,1)}, f32[2,256,256]{2,1,0:T(8,128)}) custom-call(s32[5,24]{1,0:T(8,128)} %pad_add_fusion.refs_0_, s32[8,128,128]{2,1,0:T(8,128)} %copy-done.6, s32[32,128,128]{2,1,0:T(8,128)} %bitcast.54, bf16[16,128,256]{2,1,0:T(8,128)(2,1)} %bitcast.60, bf16[16,128,256]{2,1,0:T(8,128)(2,1)} %copy-done.3, ...), custom_call_target="tpu_custom_call" | custom-call | flops 402653184 | bytes 4718592 | tf_op jit(solution)/shard_map/tile_products/pallas_call | solution.py:173
  126.2 1.9 collective-permute-start.15
  128.1 2.1 %collective-permute-start.17 = (bf16[2,256,256]{2,1,0:T(8,128)(2,1)}, bf16[2,256,256]{2,1,0:T(8,128)(2,1)S(1)}, u32[]{:S(2)}, u32[]{:S(2)}) collective-permute-start(bf16[2,256,256]{2,1,0:T(8,128)(2,1)} %get-tuple-element.18), channel_id=1, source_target_pairs={{0,16},{1,17},{2,18},{3,19},{8,24},{9,25},{10,26},{11,27},{16,32},... | collective-permute-start | bytes 786440 | tf_op jit(solution)/shard_map/ppermute | solution.py:29
  131.0 4.7 %tile_products.4 = f32[2,256,256]{2,1,0:T(8,128)} custom-call(s32[5,16]{1,0:T(8,128)} %stack.26.refs_0_, s32[4,128,128]{2,1,0:T(8,128)} %collective-permute-done.3.refs_1_, s32[4,128,128]{2,1,0:T(8,128)} %collective-permute-done.4.refs_2_, s32[4,128,128]{2,1,0:T(8,128)} %copy-done.18, s32[4,128,128]{2,1,0:T(8,128)} %collective-permute-done.6.refs_4_, ...), custom_call_target="tpu_custom_call" | custom-call | flops 268435456 | bytes 3145728 | tf_op jit(solution)/shard_map/tile_products/pallas_call | solution.py:173
  135.9 1.8 collective-permute-start.26
  138.9 4.2 %collective-permute-start.16 = (bf16[2,256,256]{2,1,0:T(8,128)(2,1)S(1)}, bf16[2,256,256]{2,1,0:T(8,128)(2,1)S(1)}, u32[]{:S(2)}, u32[]{:S(2)}) collective-permute-start(bf16[2,256,256]{2,1,0:T(8,128)(2,1)S(1)} %add_convert_fusion), channel_id=1, source_target_pairs={{0,8},{1,9},{2,10},{3,11},{4,12},{5,13},{6,14},{7,15},{8,0},{9,1},... | collective-permute-start | bytes 786440 | tf_op jit(solution)/shard_map/ppermute | solution.py:29
  143.7 2.3 %collective-permute-start.29 = (f32[2,16,256]{2,1,0:T(8,128)S(1)}, f32[2,16,256]{2,1,0:T(8,128)S(1)}, u32[]{:S(2)}, u32[]{:S(2)}) collective-permute-start(f32[2,16,256]{2,1,0:T(8,128)S(1)} %get-tuple-element.40), channel_id=1, source_target_pairs={{0,32},{1,33},{2,34},{3,35},{4,36},{5,37},{6,38},{7,39},{8,40},{9,... | collective-permute-start | bytes 98312 | tf_op jit(solution)/shard_map/ppermute | solution.py:29
  146.0 2.0 %collective-permute-start.30 = (f32[2,16,256]{2,1,0:T(8,128)S(1)}, f32[2,16,256]{2,1,0:T(8,128)S(1)}, u32[]{:S(2)}, u32[]{:S(2)}) collective-permute-start(f32[2,16,256]{2,1,0:T(8,128)S(1)} %get-tuple-element.39), channel_id=1, source_target_pairs={{0,48},{1,49},{2,50},{3,51},{4,52},{5,53},{6,54},{7,55},{8,56},{9,... | collective-permute-start | bytes 98312 | tf_op jit(solution)/shard_map/ppermute | solution.py:29
  149.4 1.8 collective-permute-start.18
  151.3 9.9 %collective-permute-start.19 = (bf16[2,256,256]{2,1,0:T(8,128)(2,1)S(1)}, bf16[2,256,256]{2,1,0:T(8,128)(2,1)S(1)}, u32[]{:S(2)}, u32[]{:S(2)}) collective-permute-start(bf16[2,256,256]{2,1,0:T(8,128)(2,1)S(1)} %multiply_convert_fusion.p0), channel_id=1, source_target_pairs={{0,2},{1,3},{2,0},{3,1},{4,6},{5,7},{6,4},{7,5},{8,10},{9,11},{10,... | collective-permute-start | bytes 786440 | tf_op jit(solution)/shard_map/ppermute | solution.py:29
  161.2 6.8 %collective-permute-start.31 = (f32[16,256]{1,0:T(8,128)S(1)}, f32[16,256]{1,0:T(8,128)S(1)}, u32[]{:S(2)}, u32[]{:S(2)}) collective-permute-start(f32[16,256]{1,0:T(8,128)S(1)} %get-tuple-element.42), channel_id=1, source_target_pairs={{0,0},{1,1},{2,128},{3,129},{4,4},{5,5},{6,132},{7,133},{8,8},{9,9... | collective-permute-start | bytes 49160 | tf_op jit(solution)/shard_map/ppermute | solution.py:29
  168.0 2.2 %collective-permute-start.32 = (f32[16,256]{1,0:T(8,128)S(1)}, f32[16,256]{1,0:T(8,128)S(1)}, u32[]{:S(2)}, u32[]{:S(2)}) collective-permute-start(f32[16,256]{1,0:T(8,128)S(1)} %get-tuple-element.41), channel_id=1, source_target_pairs={{0,8},{1,9},{2,136},{3,137},{4,12},{5,13},{6,140},{7,141},{8,0},{9... | collective-permute-start | bytes 49160 | tf_op jit(solution)/shard_map/ppermute | solution.py:29
  170.1 19.1 %collective-permute-done.31 = f32[16,256]{1,0:T(8,128)S(1)} collective-permute-done((f32[16,256]{1,0:T(8,128)S(1)}, f32[16,256]{1,0:T(8,128)S(1)}, u32[]{:S(2)}, u32[]{:S(2)}) %collective-permute-start.31) | collective-permute-done | bytes 16416 | tf_op jit(solution)/shard_map/ppermute | solution.py:29
  191.4 2.7 %project.1 = (bf16[256,256]{1,0:T(8,128)(2,1)}, bf16[256,256]{1,0:T(8,128)(2,1)}) custom-call(s32[1]{0:T(128)} %bitcast.chan_ref, bf16[2,256,256]{2,1,0:T(8,128)(2,1)} %copy-done.5, bf16[2,256,256]{2,1,0:T(8,128)(2,1)} %copy-done.14, bf16[2,256,256]{2,1,0:T(8,128)(2,1)} %copy-done.15, bf16[2,256,256]{2,1,0:T(8,128)(2,1)} %copy-done.16, ...), custom_call_target="tpu_custom_call" | custom-call | flops 268435456 | bytes 4194304 | tf_op jit(solution)/shard_map/project/pallas_call | solution.py:206
  (140 shorter events, 27.3 us)
Async XLA Ops:
  2.9 58.3 %collective-permute-start.23 = (bf16[1024,256]{1,0:T(8,128)(2,1)}, bf16[1024,256]{1,0:T(8,128)(2,1)}, u32[]{:S(2)}, u32[]{:S(2)}) collective-permute-start(bf16[1024,256]{1,0:T(8,128)(2,1)} %get-tuple-element.34), channel_id=1, source_target_pairs={{0,2},{1,3},{2,0},{3,1},{4,6},{5,7},{6,4},{7,5},{8,10},{9,11},{10,... | collective-permute-start | bytes 1572872 | tf_op jit(solution)/shard_map/ppermute | solution.py:29
  5.9 69.2 %collective-permute-start.21 = (bf16[2048,256]{1,0:T(8,128)(2,1)S(1)}, bf16[2048,256]{1,0:T(8,128)(2,1)}, u32[]{:S(2)}, u32[]{:S(2)}) collective-permute-start(bf16[2048,256]{1,0:T(8,128)(2,1)S(1)} %copy-done), channel_id=1, source_target_pairs={{0,1},{1,0},{2,3},{3,2},{4,5},{5,4},{6,7},{7,6},{8,9},{9,8},{10,11... | collective-permute-start | bytes 3145736 | tf_op jit(solution)/shard_map/ppermute | solution.py:29
  7.6 43.0 %collective-permute-start.22 = (bf16[1024,256]{1,0:T(8,128)(2,1)}, bf16[1024,256]{1,0:T(8,128)(2,1)}, u32[]{:S(2)}, u32[]{:S(2)}) collective-permute-start(bf16[1024,256]{1,0:T(8,128)(2,1)} %get-tuple-element.33), channel_id=1, source_target_pairs={{0,2},{1,3},{2,0},{3,1},{4,6},{5,7},{6,4},{7,5},{8,10},{9,11},{10,... | collective-permute-start | bytes 1572872 | tf_op jit(solution)/shard_map/ppermute | solution.py:29
  12.2 52.5 %collective-permute-start.9 = (s32[4,128,128]{2,1,0:T(8,128)}, s32[4,128,128]{2,1,0:T(8,128)S(1)}, u32[]{:S(2)}, u32[]{:S(2)}) collective-permute-start(s32[4,128,128]{2,1,0:T(8,128)} %get-tuple-element.16), channel_id=1, source_target_pairs={{8,19},{9,18},{10,17},{11,16},{12,23},{13,22},{14,21},{15,20},{16,... | collective-permute-start | bytes 786440 | tf_op jit(solution)/shard_map/ppermute | solution.py:29
  24.8 40.1 %collective-permute-start.14 = (s32[4,128,128]{2,1,0:T(8,128)}, s32[4,128,128]{2,1,0:T(8,128)}, u32[]{:S(2)}, u32[]{:S(2)}) collective-permute-start(s32[4,128,128]{2,1,0:T(8,128)} %get-tuple-element.17), channel_id=1, source_target_pairs={{8,19},{11,16},{12,23},{15,20},{16,11},{19,8},{20,15},{23,12},{24,... | collective-permute-start | bytes 786440 | tf_op jit(solution)/shard_map/ppermute | solution.py:29
  50.6 23.2 %collective-permute-start.3 = (s32[4,128,128]{2,1,0:T(8,128)S(1)}, s32[4,128,128]{2,1,0:T(8,128)}, u32[]{:S(2)}, u32[]{:S(2)}) collective-permute-start(s32[4,128,128]{2,1,0:T(8,128)S(1)} %copy-done.27), channel_id=1, source_target_pairs={{0,11},{1,10},{2,9},{3,8},{4,15},{5,14},{6,13},{7,12},{8,3},{9,2},... | collective-permute-start | bytes 786440 | tf_op jit(solution)/shard_map/ppermute | solution.py:29
  61.3 40.8 %collective-permute-start.1 = (bf16[16,128,256]{2,1,0:T(8,128)(2,1)S(1)}, bf16[16,128,256]{2,1,0:T(8,128)(2,1)S(1)}, u32[]{:S(2)}, u32[]{:S(2)}) collective-permute-start(bf16[16,128,256]{2,1,0:T(8,128)(2,1)S(1)} %bitcast.62), channel_id=1, source_target_pairs={{0,4},{1,5},{2,6},{3,7},{4,0},{5,1},{6,2},{7,3},{8,12},{9,13},{10,... | collective-permute-start | bytes 3145736 | tf_op jit(solution)/shard_map/ppermute | solution.py:29
  64.7 38.6 %collective-permute-start.2 = (bf16[16,128,256]{2,1,0:T(8,128)(2,1)S(1)}, bf16[16,128,256]{2,1,0:T(8,128)(2,1)S(1)}, u32[]{:S(2)}, u32[]{:S(2)}) collective-permute-start(bf16[16,128,256]{2,1,0:T(8,128)(2,1)S(1)} %bitcast.58), channel_id=1, source_target_pairs={{0,4},{1,5},{2,6},{3,7},{4,0},{5,1},{6,2},{7,3},{8,12},{9,13},{10,... | collective-permute-start | bytes 3145736 | tf_op jit(solution)/shard_map/ppermute | solution.py:29
  64.9 14.5 %collective-permute-start.8 = (s32[4,128,128]{2,1,0:T(8,128)S(1)}, s32[4,128,128]{2,1,0:T(8,128)S(1)}, u32[]{:S(2)}, u32[]{:S(2)}) collective-permute-start(s32[4,128,128]{2,1,0:T(8,128)S(1)} %copy-done.26), channel_id=1, source_target_pairs={{0,11},{3,8},{4,15},{7,12},{8,3},{11,0},{12,7},{15,4},{16,27},{19,... | collective-permute-start | bytes 786440 | tf_op jit(solution)/shard_map/ppermute | solution.py:29
  73.9 10.3 %collective-permute-start.10 = (s32[4,128,128]{2,1,0:T(8,128)S(1)}, s32[4,128,128]{2,1,0:T(8,128)S(1)}, u32[]{:S(2)}, u32[]{:S(2)}) collective-permute-start(s32[4,128,128]{2,1,0:T(8,128)S(1)} %collective-permute-done.9.refs_1_), channel_id=1, source_target_pairs={{0,1},{1,2},{2,3},{4,5},{5,6},{6,7},{8,9},{9,10},{10,11},{12,13},{... | collective-permute-start | bytes 786440 | tf_op jit(solution)/shard_map/ppermute | solution.py:29
  75.2 10.3 %collective-permute-start.11 = (s32[4,128,128]{2,1,0:T(8,128)S(1)}, s32[4,128,128]{2,1,0:T(8,128)S(1)}, u32[]{:S(2)}, u32[]{:S(2)}) collective-permute-start(s32[4,128,128]{2,1,0:T(8,128)S(1)} %collective-permute-done.9.refs_1_), channel_id=1, source_target_pairs={{1,0},{2,1},{3,2},{5,4},{6,5},{7,6},{9,8},{10,9},{11,10},{13,12},{... | collective-permute-start | bytes 786440 | tf_op jit(solution)/shard_map/ppermute | solution.py:29
  79.4 18.3 %collective-permute-start = (s32[8,128,128]{2,1,0:T(8,128)S(1)}, s32[8,128,128]{2,1,0:T(8,128)S(1)}, u32[]{:S(2)}, u32[]{:S(2)}) collective-permute-start(s32[8,128,128]{2,1,0:T(8,128)S(1)} %copy-done.25), channel_id=1, source_target_pairs={{4,20},{5,21},{6,22},{7,23},{12,28},{13,29},{14,30},{15,31},{16,0}... | collective-permute-start | bytes 1572872 | tf_op jit(solution)/shard_map/ppermute | solution.py:29
  84.1 5.1 %collective-permute-start.12 = (s32[4,128,128]{2,1,0:T(8,128)S(1)}, s32[4,128,128]{2,1,0:T(8,128)S(1)}, u32[]{:S(2)}, u32[]{:S(2)}) collective-permute-start(s32[4,128,128]{2,1,0:T(8,128)S(1)} %collective-permute-done.9.refs_1_), channel_id=1, source_target_pairs={{0,2},{1,3},{4,6},{5,7},{8,10},{9,11},{12,14},{13,15},{16,18},{17,... | collective-permute-start | bytes 786440 | tf_op jit(solution)/shard_map/ppermute | solution.py:29
  85.5 10.8 %collective-permute-start.13 = (s32[4,128,128]{2,1,0:T(8,128)S(1)}, s32[4,128,128]{2,1,0:T(8,128)S(1)}, u32[]{:S(2)}, u32[]{:S(2)}) collective-permute-start(s32[4,128,128]{2,1,0:T(8,128)S(1)} %collective-permute-done.9.refs_1_), channel_id=1, source_target_pairs={{2,0},{3,1},{6,4},{7,5},{10,8},{11,9},{14,12},{15,13},{18,16},{19,... | collective-permute-start | bytes 786440 | tf_op jit(solution)/shard_map/ppermute | solution.py:29
  89.2 36.9 %collective-permute-start.4 = (s32[4,128,128]{2,1,0:T(8,128)}, s32[4,128,128]{2,1,0:T(8,128)}, u32[]{:S(2)}, u32[]{:S(2)}) collective-permute-start(s32[4,128,128]{2,1,0:T(8,128)} %collective-permute-done.3.refs_1_), channel_id=1, source_target_pairs={{0,1},{1,2},{2,3},{4,5},{5,6},{6,7},{8,9},{9,10},{10,11},{12,13},{... | collective-permute-start | bytes 786440 | tf_op jit(solution)/shard_map/ppermute | solution.py:29
  96.4 31.8 %collective-permute-start.5 = (s32[4,128,128]{2,1,0:T(8,128)}, s32[4,128,128]{2,1,0:T(8,128)S(1)}, u32[]{:S(2)}, u32[]{:S(2)}) collective-permute-start(s32[4,128,128]{2,1,0:T(8,128)} %collective-permute-done.3.refs_1_), channel_id=1, source_target_pairs={{1,0},{2,1},{3,2},{5,4},{6,5},{7,6},{9,8},{10,9},{11,10},{13,12},{... | collective-permute-start | bytes 786440 | tf_op jit(solution)/shard_map/ppermute | solution.py:29
  97.7 32.6 %collective-permute-start.6 = (s32[4,128,128]{2,1,0:T(8,128)}, s32[4,128,128]{2,1,0:T(8,128)}, u32[]{:S(2)}, u32[]{:S(2)}) collective-permute-start(s32[4,128,128]{2,1,0:T(8,128)} %collective-permute-done.3.refs_1_), channel_id=1, source_target_pairs={{0,2},{1,3},{4,6},{5,7},{8,10},{9,11},{12,14},{13,15},{16,18},{17,... | collective-permute-start | bytes 786440 | tf_op jit(solution)/shard_map/ppermute | solution.py:29
  102.1 28.2 %collective-permute-start.7 = (s32[4,128,128]{2,1,0:T(8,128)}, s32[4,128,128]{2,1,0:T(8,128)S(1)}, u32[]{:S(2)}, u32[]{:S(2)}) collective-permute-start(s32[4,128,128]{2,1,0:T(8,128)} %collective-permute-done.3.refs_1_), channel_id=1, source_target_pairs={{2,0},{3,1},{6,4},{7,5},{10,8},{11,9},{14,12},{15,13},{18,16},{19,... | collective-permute-start | bytes 786440 | tf_op jit(solution)/shard_map/ppermute | solution.py:29
  103.4 32.3 %collective-permute-start.24 = (bf16[4,8,16,256]{3,2,1,0:T(8,128)(2,1)}, bf16[4,8,16,256]{3,2,1,0:T(8,128)(2,1)S(1)}, u32[]{:S(2)}, u32[]{:S(2)}) collective-permute-start(bf16[4,8,16,256]{3,2,1,0:T(8,128)(2,1)} %fusion.7), channel_id=1, source_target_pairs={{0,4},{1,5},{2,6},{3,7},{4,0},{5,1},{6,2},{7,3},{8,12},{9,13},{10,... | collective-permute-start | bytes 786440 | tf_op jit(solution)/shard_map/ppermute | solution.py:29
  126.2 11.6 %collective-permute-start.15 = (bf16[2,256,256]{2,1,0:T(8,128)(2,1)S(1)}, bf16[2,256,256]{2,1,0:T(8,128)(2,1)S(1)}, u32[]{:S(2)}, u32[]{:S(2)}) collective-permute-start(bf16[2,256,256]{2,1,0:T(8,128)(2,1)S(1)} %copy-done.13), channel_id=1, source_target_pairs={{8,24},{9,25},{10,26},{11,27},{12,28},{13,29},{14,30},{15,31},{16,... | collective-permute-start | bytes 786440 | tf_op jit(solution)/shard_map/ppermute | solution.py:29
  128.1 20.9 %collective-permute-start.17 = (bf16[2,256,256]{2,1,0:T(8,128)(2,1)}, bf16[2,256,256]{2,1,0:T(8,128)(2,1)S(1)}, u32[]{:S(2)}, u32[]{:S(2)}) collective-permute-start(bf16[2,256,256]{2,1,0:T(8,128)(2,1)} %get-tuple-element.18), channel_id=1, source_target_pairs={{0,16},{1,17},{2,18},{3,19},{8,24},{9,25},{10,26},{11,27},{16,32},... | collective-permute-start | bytes 786440 | tf_op jit(solution)/shard_map/ppermute | solution.py:29
  135.8 7.2 %collective-permute-start.25 = (bf16[8,16,256]{2,1,0:T(8,128)(2,1)S(1)}, bf16[8,16,256]{2,1,0:T(8,128)(2,1)S(1)}, u32[]{:S(2)}, u32[]{:S(2)}) collective-permute-start(bf16[8,16,256]{2,1,0:T(8,128)(2,1)S(1)} %get-tuple-element.35), channel_id=1, source_target_pairs={{0,64},{1,65},{2,66},{3,67},{4,68},{5,69},{6,70},{7,71},{8,72},{9,... | collective-permute-start | bytes 196616 | tf_op jit(solution)/shard_map/ppermute | solution.py:29
  135.9 7.1 %collective-permute-start.26 = (bf16[8,16,256]{2,1,0:T(8,128)(2,1)S(1)}, bf16[8,16,256]{2,1,0:T(8,128)(2,1)S(1)}, u32[]{:S(2)}, u32[]{:S(2)}) collective-permute-start(bf16[8,16,256]{2,1,0:T(8,128)(2,1)S(1)} %get-tuple-element.37), channel_id=1, source_target_pairs={{0,128},{1,129},{2,130},{3,131},{4,132},{5,133},{6,134},{7,135},{8... | collective-permute-start | bytes 196616 | tf_op jit(solution)/shard_map/ppermute | solution.py:29
  137.8 5.3 %collective-permute-start.27 = (bf16[8,16,256]{2,1,0:T(8,128)(2,1)S(1)}, bf16[8,16,256]{2,1,0:T(8,128)(2,1)S(1)}, u32[]{:S(2)}, u32[]{:S(2)}) collective-permute-start(bf16[8,16,256]{2,1,0:T(8,128)(2,1)S(1)} %get-tuple-element.36), channel_id=1, source_target_pairs={{0,192},{1,193},{2,194},{3,195},{4,196},{5,197},{6,198},{7,199},{8... | collective-permute-start | bytes 196616 | tf_op jit(solution)/shard_map/ppermute | solution.py:29
  138.9 10.4 %collective-permute-start.16 = (bf16[2,256,256]{2,1,0:T(8,128)(2,1)S(1)}, bf16[2,256,256]{2,1,0:T(8,128)(2,1)S(1)}, u32[]{:S(2)}, u32[]{:S(2)}) collective-permute-start(bf16[2,256,256]{2,1,0:T(8,128)(2,1)S(1)} %add_convert_fusion), channel_id=1, source_target_pairs={{0,8},{1,9},{2,10},{3,11},{4,12},{5,13},{6,14},{7,15},{8,0},{9,1},... | collective-permute-start | bytes 786440 | tf_op jit(solution)/shard_map/ppermute | solution.py:29
  143.1 4.8 %collective-permute-start.28 = (f32[2,16,256]{2,1,0:T(8,128)S(1)}, f32[2,16,256]{2,1,0:T(8,128)S(1)}, u32[]{:S(2)}, u32[]{:S(2)}) collective-permute-start(f32[2,16,256]{2,1,0:T(8,128)S(1)} %get-tuple-element.38), channel_id=1, source_target_pairs={{0,16},{1,17},{2,18},{3,19},{4,20},{5,21},{6,22},{7,23},{8,24},{9,... | collective-permute-start | bytes 98312 | tf_op jit(solution)/shard_map/ppermute | solution.py:29
  143.7 4.3 %collective-permute-start.29 = (f32[2,16,256]{2,1,0:T(8,128)S(1)}, f32[2,16,256]{2,1,0:T(8,128)S(1)}, u32[]{:S(2)}, u32[]{:S(2)}) collective-permute-start(f32[2,16,256]{2,1,0:T(8,128)S(1)} %get-tuple-element.40), channel_id=1, source_target_pairs={{0,32},{1,33},{2,34},{3,35},{4,36},{5,37},{6,38},{7,39},{8,40},{9,... | collective-permute-start | bytes 98312 | tf_op jit(solution)/shard_map/ppermute | solution.py:29
  149.4 40.4 %collective-permute-start.18 = (bf16[2,256,256]{2,1,0:T(8,128)(2,1)S(1)}, bf16[2,256,256]{2,1,0:T(8,128)(2,1)S(1)}, u32[]{:S(2)}, u32[]{:S(2)}) collective-permute-start(bf16[2,256,256]{2,1,0:T(8,128)(2,1)S(1)} %multiply_convert_fusion.p0), channel_id=1, source_target_pairs={{0,1},{1,2},{2,3},{3,0},{4,5},{5,6},{6,7},{7,4},{8,9},{9,10},{10,1... | collective-permute-start | bytes 786440 | tf_op jit(solution)/shard_map/ppermute | solution.py:29
  151.3 38.6 %collective-permute-start.19 = (bf16[2,256,256]{2,1,0:T(8,128)(2,1)S(1)}, bf16[2,256,256]{2,1,0:T(8,128)(2,1)S(1)}, u32[]{:S(2)}, u32[]{:S(2)}) collective-permute-start(bf16[2,256,256]{2,1,0:T(8,128)(2,1)S(1)} %multiply_convert_fusion.p0), channel_id=1, source_target_pairs={{0,2},{1,3},{2,0},{3,1},{4,6},{5,7},{6,4},{7,5},{8,10},{9,11},{10,... | collective-permute-start | bytes 786440 | tf_op jit(solution)/shard_map/ppermute | solution.py:29
  161.2 28.7 %collective-permute-start.20 = (bf16[2,256,256]{2,1,0:T(8,128)(2,1)S(1)}, bf16[2,256,256]{2,1,0:T(8,128)(2,1)S(1)}, u32[]{:S(2)}, u32[]{:S(2)}) collective-permute-start(bf16[2,256,256]{2,1,0:T(8,128)(2,1)S(1)} %multiply_convert_fusion.p0), channel_id=1, source_target_pairs={{0,3},{1,0},{2,1},{3,2},{4,7},{5,4},{6,5},{7,6},{8,11},{9,8},{10,9... | collective-permute-start | bytes 786440 | tf_op jit(solution)/shard_map/ppermute | solution.py:29
  161.2 28.1 %collective-permute-start.31 = (f32[16,256]{1,0:T(8,128)S(1)}, f32[16,256]{1,0:T(8,128)S(1)}, u32[]{:S(2)}, u32[]{:S(2)}) collective-permute-start(f32[16,256]{1,0:T(8,128)S(1)} %get-tuple-element.42), channel_id=1, source_target_pairs={{0,0},{1,1},{2,128},{3,129},{4,4},{5,5},{6,132},{7,133},{8,8},{9,9... | collective-permute-start | bytes 49160 | tf_op jit(solution)/shard_map/ppermute | solution.py:29
  168.0 21.3 %collective-permute-start.32 = (f32[16,256]{1,0:T(8,128)S(1)}, f32[16,256]{1,0:T(8,128)S(1)}, u32[]{:S(2)}, u32[]{:S(2)}) collective-permute-start(f32[16,256]{1,0:T(8,128)S(1)} %get-tuple-element.41), channel_id=1, source_target_pairs={{0,8},{1,9},{2,136},{3,137},{4,12},{5,13},{6,140},{7,141},{8,0},{9... | collective-permute-start | bytes 49160 | tf_op jit(solution)/shard_map/ppermute | solution.py:29
  (29 other events, 406.8 us)

commit v5 on v4

--- a/solution.py
+++ b/solution.py
@@ -191,8 +191,8 @@
 def project_kernel(chan_ref, p0, p1, p2, p3, enc_mix, dec_proj, node_embed, hidden, node_grad):
     chan = chan_ref[0]
     mixed = None
-    for back, piece in enumerate((p0, p1, p2, p3)):
-        rows = pl.ds(pl.multiple_of(((chan + CHAN - back) % CHAN) * 256, 256), 256)
+    for by, piece in enumerate((p0, p1, p2, p3)):
+        rows = pl.ds(pl.multiple_of((chan ^ by) * 256, 256), 256)
         left = jnp.dot(piece[0], enc_mix[rows, :], preferred_element_type=jnp.float32)
         right = jnp.dot(piece[1], dec_proj[rows, :], preferred_element_type=jnp.float32)
         mixed, grad = (left, right) if mixed is None else (mixed + left, grad + right)
@@ -242,28 +242,32 @@
     place = jnp.stack([band, chan]).astype(jnp.int32)
     give_codes, keep_codes = pick_tiles(place, tile_source.T, codes, ((0, "mirrored"), (1, "mirrored")))
     give_extra, keep_extra, far_codes = pick_tiles(place, tile_source.T, codes, ((0, "own"), (1, "own"), (2, "all")))
-    ends = (0, CHAN - 1)
 
     def mirrored(c):
         return CHAN - 1 - c
 
-    def if_end(c):
-        return mirrored(c) if c in ends else -1
-
-    give_codes = go(give_codes, lambda b, c: (b - 2 * near_step(b), mirrored(c)))
-    keep_codes = go(keep_codes, lambda b, c: (b ^ 2, mirrored(c)))
-    give_extra = go(give_extra, lambda b, c: (b - 2 * near_step(b), if_end(c)))
-    keep_extra = go(keep_extra, lambda b, c: (b ^ 2, if_end(c)))
+    give_to = lambda b: b - 2 * near_step(b)
+    keep_to = lambda b: b ^ 2
+
+    give_codes = go(give_codes, lambda b, c: (give_to(b), mirrored(c)))
+    keep_codes = go(keep_codes, lambda b, c: (keep_to(b), mirrored(c)))
     far_codes = go(far_codes, lambda b, c: (b - 2 * far_step(b), c))
 
-    def along_chan(x, extra):
-        return [x] + [go(x, lambda b, c, by=by: (b, c + by)) for by in (1, -1, 2, -2)] + [extra]
-
-    give_codes = along_chan(give_codes, give_extra)
-    keep_codes = along_chan(keep_codes, keep_extra)
+    at_end = (chan == 0) | (chan == CHAN - 1)
+
+    def along_chan(x, extra, reader):
+        one, two = (go(x, lambda b, c, by=by: (b, c ^ by)) for by in (1, 2))
+        three = go(
+            jnp.where(at_end, extra, x),
+            lambda b, c: (reader(b) if c in (0, CHAN - 1) else b, mirrored(c)),
+        )
+        return [x, one, two, three]
+
+    give_codes = along_chan(give_codes, give_extra, give_to)
+    keep_codes = along_chan(keep_codes, keep_extra, keep_to)
 
     def over_chan(x):
-        return [x] + [go(x, lambda b, c, by=by: (b, (c + by) % CHAN)) for by in range(1, CHAN)]
+        return [x] + [go(x, lambda b, c, by=by: (b, c ^ by)) for by in range(1, CHAN)]
 
     half = decoded_saved.shape[0] // 2
     dec_first = go(decoded_saved[:half], lambda b, c: (b, c ^ 2))
@@ -281,16 +285,13 @@
     def meta_of(row, index):
         node = jnp.where(tile[row] < 0, NB_DEV, tile[row] // K)
         own = (block[row] // CB_DEV == core).astype(jnp.int32)
-        away = slots // quarter - chan
-        operand = jnp.where(away < 0, -2 * away - 1, 2 * away)
-        operand = jnp.where(jnp.abs(away) == CHAN - 1, 5, operand)
-        return jnp.stack([node, own, block[row] % CB_DEV, index, operand])
+        return jnp.stack([node, own, block[row] % CB_DEV, index, (slots // quarter) ^ chan])
 
     def pieces_meta(row):
         return meta_of(row, slots % quarter)
 
     blocks = (cells, cells_sib, cotangent, cotangent_sib)
-    piece_group = [[(tuple(range(6)), 0, SIDE)]]
+    piece_group = [[(tuple(range(CHAN)), 0, SIDE)]]
     near_meta = jnp.concatenate([meta_of(2, slots)[:, :CAP], meta_of(3, jnp.maximum(tile[3], 0))], axis=1)
     far_part, own_part = tile_products(
         near_meta, [far_codes, codes], blocks, [[((0,), 0, CAP)], [((1,), CAP, SIDE)]], [jnp.bfloat16, jnp.float32]
@@ -329,8 +330,9 @@
     first = outer(cot, dec)
     third = lax.optimization_barrier(outer(cot[:half], dec_pair[0]))
     second = outer(cot_pair, dec)
+    fourth = lax.optimization_barrier(outer(cot_pair[:half], dec_pair[0]))
     third = third + outer(cot[half:], dec_pair[1])
-    fourth = outer(cot_pair[:half], dec_pair[0]) + outer(cot_pair[half:], dec_pair[1])
+    fourth = fourth + outer(cot_pair[half:], dec_pair[1])
     whole = jnp.stack([first, second, third, fourth])
     halves = whole.reshape(4, 8, 2, rows, channels)
     own = lax.dynamic_index_in_dim(halves, core, 2, keepdims=False)
@@ -342,14 +344,13 @@
 
     share = take(x ^ chan)
     for by in range(1, 4):
-        sent = take(((x + by) % 4) ^ chan).astype(jnp.bfloat16)
-        share = share + go(sent, lambda b, c: ((b + by * 4 * along) % bands, c)).astype(jnp.float32)
+        sent = take(x ^ by ^ chan).astype(jnp.bfloat16)
+        share = share + go(sent, lambda b, c: (b ^ (by * 4 * along), c)).astype(jnp.float32)
 
     own = share.reshape(4, 2, rows, channels)
     share = take(y)
     for by in range(1, 4):
-        sent = take((y + by) % 4)
-        share = share + go(sent, lambda b, c: (b // 16 * 16 + (b % 16 + by * 4) % 16, c))
+        share = share + go(take(y ^ by), lambda b, c: (b ^ (by * 4), c))
 
     def home(b, c):
         at_x, rest = b // 16, b % 16

time: 195 us -> 182 us (0.933)
  the two profiles are of different devices: /device:TPU:7 before, /device:TPU:4 now
where the time goes in v5:
time: 182 us; the launch traced here: 181 us
  starting transfers between devices  72.7 us (40%)
  waiting for transfers between devices  57.4 us (32%)
  Pallas kernels  26.2 us (14%)
  matrix products  8.74 us (5%)
  local copies, waits for them, and re-layouts  8.33 us (5%)
  other arithmetic  6.69 us (4%)
    ppermute x29, starting transfers between devices, permute(): return lax.ppermute(x, ('band', 'chan'), pairs)  72.7 us
    ppermute x29, waiting for transfers between devices, permute(): return lax.ppermute(x, ('band', 'chan'), pairs)  57.4 us
    pallas_call x3, Pallas kernels, tile_products(): pl.pallas_call(functools.partial(products_kernel, groups, len(codes)), ou...  15.5 us
    dot_general x6, matrix products, outer(): lax.dot_general(left, right, (((0,), (0,)), ((), ())), preferred_element_...  8.74 us
    pallas_call x2, Pallas kernels, pick_tiles(): pl.pallas_call(functools.partial(pick_kernel, picks), out_shape=[jax.Shap...  8.05 us
  transfers between devices with their start and end apart: 29, of which 9 were waited for; matrix products, arithmetic and copies ran while one was open for 10% of the time, Pallas kernels for 13%

profile of v5, /device:TPU:4, one launch (start us, length us, event | category | flops | bytes accessed | tf_op | source)
XLA Modules:
  0.0 181.3 jit_solution(15018775725359133437)
XLA Ops:
  0.7 2.4 %fusion.33 = (bf16[1024,256]{1,0:T(8,128)(2,1)}, bf16[1024,256]{1,0:T(8,128)(2,1)}) fusion(bf16[2048,256]{1,0:T(8,128)(2,1)} %param.16), kind=kLoop, calls=%fused_computation.128 | loop fusion | bytes 2097152 | tf_op jit(solution)/shard_map/slice | solution.py:275
  3.0 3.3 %collective-permute-start.19 = (bf16[1024,256]{1,0:T(8,128)(2,1)}, bf16[1024,256]{1,0:T(8,128)(2,1)}, u32[]{:S(2)}, u32[]{:S(2)}) collective-permute-start(bf16[1024,256]{1,0:T(8,128)(2,1)} %get-tuple-element.33), channel_id=1, source_target_pairs={{0,2},{1,3},{2,0},{3,1},{4,6},{5,7},{6,4},{7,5},{8,10},{9,11},{10,... | collective-permute-start | bytes 1572872 | tf_op jit(solution)/shard_map/ppermute | solution.py:29
  6.3 1.9 %collective-permute-start.17 = (bf16[2048,256]{1,0:T(8,128)(2,1)S(1)}, bf16[2048,256]{1,0:T(8,128)(2,1)}, u32[]{:S(2)}, u32[]{:S(2)}) collective-permute-start(bf16[2048,256]{1,0:T(8,128)(2,1)S(1)} %copy-done), channel_id=1, source_target_pairs={{0,1},{1,0},{2,3},{3,2},{4,5},{5,4},{6,7},{7,6},{8,9},{9,8},{10,11... | collective-permute-start | bytes 3145736 | tf_op jit(solution)/shard_map/ppermute | solution.py:29
  8.9 4.0 %pick_tiles.3 = (s32[4,128,128]{2,1,0:T(8,128)}, s32[4,128,128]{2,1,0:T(8,128)}) custom-call(s32[2]{0:T(128)} %pad_add_fusion.1.place, s32[16,128]{1,0:T(8,128)} %bitcast.69, s32[32,128,128]{2,1,0:T(8,128)} %bitcast.52), custom_call_target="tpu_custom_call" | custom-call | flops 100000000 | bytes 1048576 | tf_op jit(solution)/shard_map/pick_tiles/pallas_call | solution.py:88
  12.9 8.7 %collective-permute-start.7 = (s32[4,128,128]{2,1,0:T(8,128)}, s32[4,128,128]{2,1,0:T(8,128)}, u32[]{:S(2)}, u32[]{:S(2)}) collective-permute-start(s32[4,128,128]{2,1,0:T(8,128)} %get-tuple-element.16), channel_id=1, source_target_pairs={{8,19},{9,18},{10,17},{11,16},{12,23},{13,22},{14,21},{15,20},{16,... | collective-permute-start | bytes 786440 | tf_op jit(solution)/shard_map/ppermute | solution.py:29
  24.4 4.1 %pick_tiles.2 = (s32[4,128,128]{2,1,0:T(8,128)}, s32[4,128,128]{2,1,0:T(8,128)}, s32[8,128,128]{2,1,0:T(8,128)}) custom-call(s32[2]{0:T(128)} %pad_add_fusion.1.place, s32[16,128]{1,0:T(8,128)} %bitcast.70, s32[32,128,128]{2,1,0:T(8,128)} %bitcast.53), custom_call_target="tpu_custom_call" | custom-call | flops 100000000 | bytes 2097152 | tf_op jit(solution)/shard_map/pick_tiles/pallas_call | solution.py:88
  30.0 2.2 %collective-permute-done.3.refs_1_ = s32[4,128,128]{2,1,0:T(8,128)S(1)} collective-permute-done((s32[4,128,128]{2,1,0:T(8,128)}, s32[4,128,128]{2,1,0:T(8,128)S(1)}, u32[]{:S(2)}, u32[]{:S(2)}) %collective-permute-start.3) | collective-permute-done | bytes 262176 | tf_op jit(solution)/shard_map/ppermute | solution.py:29
  32.2 1.8 broadcast_select_fusion.1
  34.0 17.6 %collective-permute-done.18 = bf16[1024,256]{1,0:T(8,128)(2,1)} collective-permute-done((bf16[1024,256]{1,0:T(8,128)(2,1)}, bf16[1024,256]{1,0:T(8,128)(2,1)}, u32[]{:S(2)}, u32[]{:S(2)}) %collective-permute-start.18) | collective-permute-done | bytes 524320 | tf_op jit(solution)/shard_map/ppermute | solution.py:29
  51.6 4.9 %collective-permute-start = (s32[8,128,128]{2,1,0:T(8,128)}, s32[8,128,128]{2,1,0:T(8,128)}, u32[]{:S(2)}, u32[]{:S(2)}) collective-permute-start(s32[8,128,128]{2,1,0:T(8,128)} %get-tuple-element.12), channel_id=1, source_target_pairs={{4,20},{5,21},{6,22},{7,23},{12,28},{13,29},{14,30},{15,31},{16,0}... | collective-permute-start | bytes 1572872 | tf_op jit(solution)/shard_map/ppermute | solution.py:29
  57.8 17.4 %collective-permute-start.10 = (s32[4,128,128]{2,1,0:T(8,128)S(1)}, s32[4,128,128]{2,1,0:T(8,128)S(1)}, u32[]{:S(2)}, u32[]{:S(2)}) collective-permute-start(s32[4,128,128]{2,1,0:T(8,128)S(1)} %broadcast_select_fusion), channel_id=1, source_target_pairs={{1,2},{2,1},{5,6},{6,5},{8,19},{9,10},{10,9},{11,16},{12,23},{13,1... | collective-permute-start | bytes 786440 | tf_op jit(solution)/shard_map/ppermute | solution.py:29
  76.6 4.5 %collective-permute-start.8 = (s32[4,128,128]{2,1,0:T(8,128)}, s32[4,128,128]{2,1,0:T(8,128)S(1)}, u32[]{:S(2)}, u32[]{:S(2)}) collective-permute-start(s32[4,128,128]{2,1,0:T(8,128)} %collective-permute-done.7.refs_1_), channel_id=1, source_target_pairs={{0,1},{1,0},{2,3},{3,2},{4,5},{5,4},{6,7},{7,6},{8,9},{9,8},{10,11... | collective-permute-start | bytes 786440 | tf_op jit(solution)/shard_map/ppermute | solution.py:29
  81.2 1.7 fusion.35
  88.5 10.7 %collective-permute-done.9.refs_3_ = s32[4,128,128]{2,1,0:T(8,128)S(1)} collective-permute-done((s32[4,128,128]{2,1,0:T(8,128)}, s32[4,128,128]{2,1,0:T(8,128)S(1)}, u32[]{:S(2)}, u32[]{:S(2)}) %collective-permute-start.9) | collective-permute-done | bytes 262176 | tf_op jit(solution)/shard_map/ppermute | solution.py:29
  99.1 2.5 %collective-permute-start.5 = (s32[4,128,128]{2,1,0:T(8,128)S(1)}, s32[4,128,128]{2,1,0:T(8,128)S(1)}, u32[]{:S(2)}, u32[]{:S(2)}) collective-permute-start(s32[4,128,128]{2,1,0:T(8,128)S(1)} %collective-permute-done.3.refs_1_), channel_id=1, source_target_pairs={{0,2},{1,3},{2,0},{3,1},{4,6},{5,7},{6,4},{7,5},{8,10},{9,11},{10,... | collective-permute-start | bytes 786440 | tf_op jit(solution)/shard_map/ppermute | solution.py:29
  104.6 4.6 %tile_products.5 = bf16[2,256,256]{2,1,0:T(8,128)(2,1)} custom-call(s32[5,16]{1,0:T(8,128)} %stack.27.refs_0_, s32[4,128,128]{2,1,0:T(8,128)} %collective-permute-done.7.refs_1_, s32[4,128,128]{2,1,0:T(8,128)} %copy-done.10, s32[4,128,128]{2,1,0:T(8,128)} %copy-done.12, s32[4,128,128]{2,1,0:T(8,128)} %copy-done.9, bf16[16,128,256]{2,1,0:T(8,128)(2,1)} %bitcast.59, ...), custom_call_target="tpu_custom_call" | custom-call | flops 268435456 | bytes 3145728 | tf_op jit(solution)/shard_map/tile_products/pallas_call | solution.py:173
  109.2 4.3 %collective-permute-start.11 = (bf16[2,256,256]{2,1,0:T(8,128)(2,1)}, bf16[2,256,256]{2,1,0:T(8,128)(2,1)S(1)}, u32[]{:S(2)}, u32[]{:S(2)}) collective-permute-start(bf16[2,256,256]{2,1,0:T(8,128)(2,1)} %tile_products.5), channel_id=1, source_target_pairs={{8,24},{9,25},{10,26},{11,27},{12,28},{13,29},{14,30},{15,31},{16,... | collective-permute-start | bytes 786440 | tf_op jit(solution)/shard_map/ppermute | solution.py:29
  113.5 6.1 %tile_products.3 = (bf16[2,256,256]{2,1,0:T(8,128)(2,1)}, f32[2,256,256]{2,1,0:T(8,128)}) custom-call(s32[5,24]{1,0:T(8,128)} %pad_add_fusion.refs_0_, s32[8,128,128]{2,1,0:T(8,128)} %collective-permute-done.refs_1_, s32[32,128,128]{2,1,0:T(8,128)} %bitcast.54, bf16[16,128,256]{2,1,0:T(8,128)(2,1)} %bitcast.60, bf16[16,128,256]{2,1,0:T(8,128)(2,1)} %copy-done.3, ...), custom_call_target="tpu_custom_call" | custom-call | flops 402653184 | bytes 4718592 | tf_op jit(solution)/shard_map/tile_products/pallas_call | solution.py:173
  119.7 2.1 %collective-permute-start.13 = (bf16[2,256,256]{2,1,0:T(8,128)(2,1)}, bf16[2,256,256]{2,1,0:T(8,128)(2,1)S(1)}, u32[]{:S(2)}, u32[]{:S(2)}) collective-permute-start(bf16[2,256,256]{2,1,0:T(8,128)(2,1)} %get-tuple-element.18), channel_id=1, source_target_pairs={{0,16},{1,17},{2,18},{3,19},{8,24},{9,25},{10,26},{11,27},{16,32},... | collective-permute-start | bytes 786440 | tf_op jit(solution)/shard_map/ppermute | solution.py:29
  122.5 4.7 %tile_products.4 = f32[2,256,256]{2,1,0:T(8,128)} custom-call(s32[5,16]{1,0:T(8,128)} %stack.26.refs_0_, s32[4,128,128]{2,1,0:T(8,128)} %copy-done.6, s32[4,128,128]{2,1,0:T(8,128)} %collective-permute-done.4.refs_2_, s32[4,128,128]{2,1,0:T(8,128)} %copy-done.11, s32[4,128,128]{2,1,0:T(8,128)} %collective-permute-done.6.refs_4_, ...), custom_call_target="tpu_custom_call" | custom-call | flops 268435456 | bytes 3145728 | tf_op jit(solution)/shard_map/tile_products/pallas_call | solution.py:173
  127.4 1.9 %collective-permute-start.21 = (bf16[8,16,256]{2,1,0:T(8,128)(2,1)S(1)}, bf16[8,16,256]{2,1,0:T(8,128)(2,1)S(1)}, u32[]{:S(2)}, u32[]{:S(2)}) collective-permute-start(bf16[8,16,256]{2,1,0:T(8,128)(2,1)S(1)} %get-tuple-element.35), channel_id=1, source_target_pairs={{0,64},{1,65},{2,66},{3,67},{4,68},{5,69},{6,70},{7,71},{8,72},{9,... | collective-permute-start | bytes 196616 | tf_op jit(solution)/shard_map/ppermute | solution.py:29
  133.4 1.7 collective-permute-done.22
  135.8 4.4 %collective-permute-start.25 = (f32[2,16,256]{2,1,0:T(8,128)S(1)}, f32[2,16,256]{2,1,0:T(8,128)S(1)}, u32[]{:S(2)}, u32[]{:S(2)}) collective-permute-start(f32[2,16,256]{2,1,0:T(8,128)S(1)} %get-tuple-element.40), channel_id=1, source_target_pairs={{0,32},{1,33},{2,34},{3,35},{4,36},{5,37},{6,38},{7,39},{8,40},{9,... | collective-permute-start | bytes 98312 | tf_op jit(solution)/shard_map/ppermute | solution.py:29
  140.2 2.2 %collective-permute-done.25 = f32[2,16,256]{2,1,0:T(8,128)S(1)} collective-permute-done((f32[2,16,256]{2,1,0:T(8,128)S(1)}, f32[2,16,256]{2,1,0:T(8,128)S(1)}, u32[]{:S(2)}, u32[]{:S(2)}) %collective-permute-start.25) | collective-permute-done | bytes 32800 | tf_op jit(solution)/shard_map/ppermute | solution.py:29
  142.4 2.9 %collective-permute-done.26 = f32[2,16,256]{2,1,0:T(8,128)S(1)} collective-permute-done((f32[2,16,256]{2,1,0:T(8,128)S(1)}, f32[2,16,256]{2,1,0:T(8,128)S(1)}, u32[]{:S(2)}, u32[]{:S(2)}) %collective-permute-start.26) | collective-permute-done | bytes 32800 | tf_op jit(solution)/shard_map/ppermute | solution.py:29
  145.3 3.8 %collective-permute-done.12 = bf16[2,256,256]{2,1,0:T(8,128)(2,1)S(1)} collective-permute-done((bf16[2,256,256]{2,1,0:T(8,128)(2,1)S(1)}, bf16[2,256,256]{2,1,0:T(8,128)(2,1)S(1)}, u32[]{:S(2)}, u32[]{:S(2)}) %collective-permute-start.12) | collective-permute-done | bytes 262176 | tf_op jit(solution)/shard_map/ppermute | solution.py:29
  149.3 2.5 %collective-permute-start.15 = (bf16[2,256,256]{2,1,0:T(8,128)(2,1)S(1)}, bf16[2,256,256]{2,1,0:T(8,128)(2,1)S(1)}, u32[]{:S(2)}, u32[]{:S(2)}) collective-permute-start(bf16[2,256,256]{2,1,0:T(8,128)(2,1)S(1)} %multiply_convert_fusion.p0), channel_id=1, source_target_pairs={{0,2},{1,3},{2,0},{3,1},{4,6},{5,7},{6,4},{7,5},{8,10},{9,11},{10,... | collective-permute-start | bytes 786440 | tf_op jit(solution)/shard_map/ppermute | solution.py:29
  151.9 1.9 %collective-permute-start.16 = (bf16[2,256,256]{2,1,0:T(8,128)(2,1)S(1)}, bf16[2,256,256]{2,1,0:T(8,128)(2,1)S(1)}, u32[]{:S(2)}, u32[]{:S(2)}) collective-permute-start(bf16[2,256,256]{2,1,0:T(8,128)(2,1)S(1)} %multiply_convert_fusion.p0), channel_id=1, source_target_pairs={{0,3},{1,2},{2,1},{3,0},{4,7},{5,6},{6,5},{7,4},{8,11},{9,10},{10,... | collective-permute-start | bytes 786440 | tf_op jit(solution)/shard_map/ppermute | solution.py:29
  153.7 2.3 %collective-permute-start.27 = (f32[16,256]{1,0:T(8,128)S(1)}, f32[16,256]{1,0:T(8,128)S(1)}, u32[]{:S(2)}, u32[]{:S(2)}) collective-permute-start(f32[16,256]{1,0:T(8,128)S(1)} %get-tuple-element.42), channel_id=1, source_target_pairs={{0,0},{1,1},{2,128},{3,129},{4,4},{5,5},{6,132},{7,133},{8,8},{9,9... | collective-permute-start | bytes 49160 | tf_op jit(solution)/shard_map/ppermute | solution.py:29
  156.1 4.6 %collective-permute-start.28 = (f32[16,256]{1,0:T(8,128)S(1)}, f32[16,256]{1,0:T(8,128)S(1)}, u32[]{:S(2)}, u32[]{:S(2)}) collective-permute-start(f32[16,256]{1,0:T(8,128)S(1)} %get-tuple-element.41), channel_id=1, source_target_pairs={{0,8},{1,9},{2,136},{3,137},{4,12},{5,13},{6,140},{7,141},{8,0},{9... | collective-permute-start | bytes 49160 | tf_op jit(solution)/shard_map/ppermute | solution.py:29
  160.7 15.8 %collective-permute-done.27 = f32[16,256]{1,0:T(8,128)S(1)} collective-permute-done((f32[16,256]{1,0:T(8,128)S(1)}, f32[16,256]{1,0:T(8,128)S(1)}, u32[]{:S(2)}, u32[]{:S(2)}) %collective-permute-start.27) | collective-permute-done | bytes 16416 | tf_op jit(solution)/shard_map/ppermute | solution.py:29
  178.7 2.7 %project.1 = (bf16[256,256]{1,0:T(8,128)(2,1)}, bf16[256,256]{1,0:T(8,128)(2,1)}) custom-call(s32[1]{0:T(128)} %bitcast.chan_ref, bf16[2,256,256]{2,1,0:T(8,128)(2,1)} %copy-done.5, bf16[2,256,256]{2,1,0:T(8,128)(2,1)} %copy-done.13, bf16[2,256,256]{2,1,0:T(8,128)(2,1)} %copy-done.14, bf16[2,256,256]{2,1,0:T(8,128)(2,1)} %copy-done.15, ...), custom_call_target="tpu_custom_call" | custom-call | flops 268435456 | bytes 4194304 | tf_op jit(solution)/shard_map/project/pallas_call | solution.py:206
  (121 shorter events, 24.0 us)
Async XLA Ops:
  3.0 54.8 %collective-permute-start.19 = (bf16[1024,256]{1,0:T(8,128)(2,1)}, bf16[1024,256]{1,0:T(8,128)(2,1)}, u32[]{:S(2)}, u32[]{:S(2)}) collective-permute-start(bf16[1024,256]{1,0:T(8,128)(2,1)} %get-tuple-element.33), channel_id=1, source_target_pairs={{0,2},{1,3},{2,0},{3,1},{4,6},{5,7},{6,4},{7,5},{8,10},{9,11},{10,... | collective-permute-start | bytes 1572872 | tf_op jit(solution)/shard_map/ppermute | solution.py:29
  6.3 70.3 %collective-permute-start.17 = (bf16[2048,256]{1,0:T(8,128)(2,1)S(1)}, bf16[2048,256]{1,0:T(8,128)(2,1)}, u32[]{:S(2)}, u32[]{:S(2)}) collective-permute-start(bf16[2048,256]{1,0:T(8,128)(2,1)S(1)} %copy-done), channel_id=1, source_target_pairs={{0,1},{1,0},{2,3},{3,2},{4,5},{5,4},{6,7},{7,6},{8,9},{9,8},{10,11... | collective-permute-start | bytes 3145736 | tf_op jit(solution)/shard_map/ppermute | solution.py:29
  8.2 43.3 %collective-permute-start.18 = (bf16[1024,256]{1,0:T(8,128)(2,1)}, bf16[1024,256]{1,0:T(8,128)(2,1)}, u32[]{:S(2)}, u32[]{:S(2)}) collective-permute-start(bf16[1024,256]{1,0:T(8,128)(2,1)} %get-tuple-element.34), channel_id=1, source_target_pairs={{0,2},{1,3},{2,0},{3,1},{4,6},{5,7},{6,4},{7,5},{8,10},{9,11},{10,... | collective-permute-start | bytes 1572872 | tf_op jit(solution)/shard_map/ppermute | solution.py:29
  12.9 16.2 %collective-permute-start.7 = (s32[4,128,128]{2,1,0:T(8,128)}, s32[4,128,128]{2,1,0:T(8,128)}, u32[]{:S(2)}, u32[]{:S(2)}) collective-permute-start(s32[4,128,128]{2,1,0:T(8,128)} %get-tuple-element.16), channel_id=1, source_target_pairs={{8,19},{9,18},{10,17},{11,16},{12,23},{13,22},{14,21},{15,20},{16,... | collective-permute-start | bytes 786440 | tf_op jit(solution)/shard_map/ppermute | solution.py:29
  21.6 10.6 %collective-permute-start.3 = (s32[4,128,128]{2,1,0:T(8,128)}, s32[4,128,128]{2,1,0:T(8,128)S(1)}, u32[]{:S(2)}, u32[]{:S(2)}) collective-permute-start(s32[4,128,128]{2,1,0:T(8,128)} %get-tuple-element.14), channel_id=1, source_target_pairs={{0,11},{1,10},{2,9},{3,8},{4,15},{5,14},{6,13},{7,12},{8,3},{9,2},... | collective-permute-start | bytes 786440 | tf_op jit(solution)/shard_map/ppermute | solution.py:29
  29.1 70.1 %collective-permute-start.1 = (bf16[16,128,256]{2,1,0:T(8,128)(2,1)S(1)}, bf16[16,128,256]{2,1,0:T(8,128)(2,1)S(1)}, u32[]{:S(2)}, u32[]{:S(2)}) collective-permute-start(bf16[16,128,256]{2,1,0:T(8,128)(2,1)S(1)} %bitcast.62), channel_id=1, source_target_pairs={{0,4},{1,5},{2,6},{3,7},{4,0},{5,1},{6,2},{7,3},{8,12},{9,13},{10,... | collective-permute-start | bytes 3145736 | tf_op jit(solution)/shard_map/ppermute | solution.py:29
  32.2 66.9 %copy-start.6 = (s32[4,128,128]{2,1,0:T(8,128)}, s32[4,128,128]{2,1,0:T(8,128)S(1)}, u32[]{:S(2)}) copy-start(s32[4,128,128]{2,1,0:T(8,128)S(1)} %collective-permute-done.3.refs_1_) | copy-start | bytes 786436
  32.2 69.4 %collective-permute-start.2 = (bf16[16,128,256]{2,1,0:T(8,128)(2,1)S(1)}, bf16[16,128,256]{2,1,0:T(8,128)(2,1)S(1)}, u32[]{:S(2)}, u32[]{:S(2)}) collective-permute-start(bf16[16,128,256]{2,1,0:T(8,128)(2,1)S(1)} %bitcast.58), channel_id=1, source_target_pairs={{0,4},{1,5},{2,6},{3,7},{4,0},{5,1},{6,2},{7,3},{8,12},{9,13},{10,... | collective-permute-start | bytes 3145736 | tf_op jit(solution)/shard_map/ppermute | solution.py:29
  51.6 57.7 %collective-permute-start = (s32[8,128,128]{2,1,0:T(8,128)}, s32[8,128,128]{2,1,0:T(8,128)}, u32[]{:S(2)}, u32[]{:S(2)}) collective-permute-start(s32[8,128,128]{2,1,0:T(8,128)} %get-tuple-element.12), channel_id=1, source_target_pairs={{4,20},{5,21},{6,22},{7,23},{12,28},{13,29},{14,30},{15,31},{16,0}... | collective-permute-start | bytes 1572872 | tf_op jit(solution)/shard_map/ppermute | solution.py:29
  57.8 26.6 %collective-permute-start.10 = (s32[4,128,128]{2,1,0:T(8,128)S(1)}, s32[4,128,128]{2,1,0:T(8,128)S(1)}, u32[]{:S(2)}, u32[]{:S(2)}) collective-permute-start(s32[4,128,128]{2,1,0:T(8,128)S(1)} %broadcast_select_fusion), channel_id=1, source_target_pairs={{1,2},{2,1},{5,6},{6,5},{8,19},{9,10},{10,9},{11,16},{12,23},{13,1... | collective-permute-start | bytes 786440 | tf_op jit(solution)/shard_map/ppermute | solution.py:29
  76.6 11.8 %collective-permute-start.8 = (s32[4,128,128]{2,1,0:T(8,128)}, s32[4,128,128]{2,1,0:T(8,128)S(1)}, u32[]{:S(2)}, u32[]{:S(2)}) collective-permute-start(s32[4,128,128]{2,1,0:T(8,128)} %collective-permute-done.7.refs_1_), channel_id=1, source_target_pairs={{0,1},{1,0},{2,3},{3,2},{4,5},{5,4},{6,7},{7,6},{8,9},{9,8},{10,11... | collective-permute-start | bytes 786440 | tf_op jit(solution)/shard_map/ppermute | solution.py:29
  84.5 14.6 %collective-permute-start.9 = (s32[4,128,128]{2,1,0:T(8,128)}, s32[4,128,128]{2,1,0:T(8,128)S(1)}, u32[]{:S(2)}, u32[]{:S(2)}) collective-permute-start(s32[4,128,128]{2,1,0:T(8,128)} %collective-permute-done.7.refs_1_), channel_id=1, source_target_pairs={{0,2},{1,3},{2,0},{3,1},{4,6},{5,7},{6,4},{7,5},{8,10},{9,11},{10,... | collective-permute-start | bytes 786440 | tf_op jit(solution)/shard_map/ppermute | solution.py:29
  88.4 31.2 %collective-permute-start.6 = (s32[4,128,128]{2,1,0:T(8,128)}, s32[4,128,128]{2,1,0:T(8,128)}, u32[]{:S(2)}, u32[]{:S(2)}) collective-permute-start(s32[4,128,128]{2,1,0:T(8,128)} %broadcast_select_fusion.1), channel_id=1, source_target_pairs={{0,11},{1,2},{2,1},{3,8},{4,15},{5,6},{6,5},{7,12},{8,3},{9,10},{1... | collective-permute-start | bytes 786440 | tf_op jit(solution)/shard_map/ppermute | solution.py:29
  99.1 22.7 %collective-permute-start.4 = (s32[4,128,128]{2,1,0:T(8,128)S(1)}, s32[4,128,128]{2,1,0:T(8,128)}, u32[]{:S(2)}, u32[]{:S(2)}) collective-permute-start(s32[4,128,128]{2,1,0:T(8,128)S(1)} %collective-permute-done.3.refs_1_), channel_id=1, source_target_pairs={{0,1},{1,0},{2,3},{3,2},{4,5},{5,4},{6,7},{7,6},{8,9},{9,8},{10,11... | collective-permute-start | bytes 786440 | tf_op jit(solution)/shard_map/ppermute | solution.py:29
  99.1 22.6 %collective-permute-start.5 = (s32[4,128,128]{2,1,0:T(8,128)S(1)}, s32[4,128,128]{2,1,0:T(8,128)S(1)}, u32[]{:S(2)}, u32[]{:S(2)}) collective-permute-start(s32[4,128,128]{2,1,0:T(8,128)S(1)} %collective-permute-done.3.refs_1_), channel_id=1, source_target_pairs={{0,2},{1,3},{2,0},{3,1},{4,6},{5,7},{6,4},{7,5},{8,10},{9,11},{10,... | collective-permute-start | bytes 786440 | tf_op jit(solution)/shard_map/ppermute | solution.py:29
  101.7 25.6 %collective-permute-start.20 = (bf16[4,8,16,256]{3,2,1,0:T(8,128)(2,1)}, bf16[4,8,16,256]{3,2,1,0:T(8,128)(2,1)S(1)}, u32[]{:S(2)}, u32[]{:S(2)}) collective-permute-start(bf16[4,8,16,256]{3,2,1,0:T(8,128)(2,1)} %fusion.8), channel_id=1, source_target_pairs={{0,4},{1,5},{2,6},{3,7},{4,0},{5,1},{6,2},{7,3},{8,12},{9,13},{10,... | collective-permute-start | bytes 786440 | tf_op jit(solution)/shard_map/ppermute | solution.py:29
  109.2 21.7 %collective-permute-start.11 = (bf16[2,256,256]{2,1,0:T(8,128)(2,1)}, bf16[2,256,256]{2,1,0:T(8,128)(2,1)S(1)}, u32[]{:S(2)}, u32[]{:S(2)}) collective-permute-start(bf16[2,256,256]{2,1,0:T(8,128)(2,1)} %tile_products.5), channel_id=1, source_target_pairs={{8,24},{9,25},{10,26},{11,27},{12,28},{13,29},{14,30},{15,31},{16,... | collective-permute-start | bytes 786440 | tf_op jit(solution)/shard_map/ppermute | solution.py:29
  119.7 25.7 %collective-permute-start.13 = (bf16[2,256,256]{2,1,0:T(8,128)(2,1)}, bf16[2,256,256]{2,1,0:T(8,128)(2,1)S(1)}, u32[]{:S(2)}, u32[]{:S(2)}) collective-permute-start(bf16[2,256,256]{2,1,0:T(8,128)(2,1)} %get-tuple-element.18), channel_id=1, source_target_pairs={{0,16},{1,17},{2,18},{3,19},{8,24},{9,25},{10,26},{11,27},{16,32},... | collective-permute-start | bytes 786440 | tf_op jit(solution)/shard_map/ppermute | solution.py:29
  127.2 21.9 %copy-start.8 = (f32[2,256,256]{2,1,0:T(8,128)S(1)}, f32[2,256,256]{2,1,0:T(8,128)}, u32[]{:S(2)}) copy-start(f32[2,256,256]{2,1,0:T(8,128)} %get-tuple-element.13) | copy-start | bytes 1572868
  127.4 6.0 %collective-permute-start.21 = (bf16[8,16,256]{2,1,0:T(8,128)(2,1)S(1)}, bf16[8,16,256]{2,1,0:T(8,128)(2,1)S(1)}, u32[]{:S(2)}, u32[]{:S(2)}) collective-permute-start(bf16[8,16,256]{2,1,0:T(8,128)(2,1)S(1)} %get-tuple-element.35), channel_id=1, source_target_pairs={{0,64},{1,65},{2,66},{3,67},{4,68},{5,69},{6,70},{7,71},{8,72},{9,... | collective-permute-start | bytes 196616 | tf_op jit(solution)/shard_map/ppermute | solution.py:29
  129.3 5.8 %collective-permute-start.22 = (bf16[8,16,256]{2,1,0:T(8,128)(2,1)S(1)}, bf16[8,16,256]{2,1,0:T(8,128)(2,1)S(1)}, u32[]{:S(2)}, u32[]{:S(2)}) collective-permute-start(bf16[8,16,256]{2,1,0:T(8,128)(2,1)S(1)} %get-tuple-element.37), channel_id=1, source_target_pairs={{0,128},{1,129},{2,130},{3,131},{4,132},{5,133},{6,134},{7,135},{8... | collective-permute-start | bytes 196616 | tf_op jit(solution)/shard_map/ppermute | solution.py:29
  129.8 5.2 %collective-permute-start.23 = (bf16[8,16,256]{2,1,0:T(8,128)(2,1)S(1)}, bf16[8,16,256]{2,1,0:T(8,128)(2,1)S(1)}, u32[]{:S(2)}, u32[]{:S(2)}) collective-permute-start(bf16[8,16,256]{2,1,0:T(8,128)(2,1)S(1)} %get-tuple-element.36), channel_id=1, source_target_pairs={{0,192},{1,193},{2,194},{3,195},{4,196},{5,197},{6,198},{7,199},{8... | collective-permute-start | bytes 196616 | tf_op jit(solution)/shard_map/ppermute | solution.py:29
  132.1 17.1 %collective-permute-start.12 = (bf16[2,256,256]{2,1,0:T(8,128)(2,1)S(1)}, bf16[2,256,256]{2,1,0:T(8,128)(2,1)S(1)}, u32[]{:S(2)}, u32[]{:S(2)}) collective-permute-start(bf16[2,256,256]{2,1,0:T(8,128)(2,1)S(1)} %add_convert_fusion), channel_id=1, source_target_pairs={{0,8},{1,9},{2,10},{3,11},{4,12},{5,13},{6,14},{7,15},{8,0},{9,1},... | collective-permute-start | bytes 786440 | tf_op jit(solution)/shard_map/ppermute | solution.py:29
  135.2 5.0 %collective-permute-start.24 = (f32[2,16,256]{2,1,0:T(8,128)S(1)}, f32[2,16,256]{2,1,0:T(8,128)S(1)}, u32[]{:S(2)}, u32[]{:S(2)}) collective-permute-start(f32[2,16,256]{2,1,0:T(8,128)S(1)} %get-tuple-element.38), channel_id=1, source_target_pairs={{0,16},{1,17},{2,18},{3,19},{4,20},{5,21},{6,22},{7,23},{8,24},{9,... | collective-permute-start | bytes 98312 | tf_op jit(solution)/shard_map/ppermute | solution.py:29
  135.8 6.6 %collective-permute-start.25 = (f32[2,16,256]{2,1,0:T(8,128)S(1)}, f32[2,16,256]{2,1,0:T(8,128)S(1)}, u32[]{:S(2)}, u32[]{:S(2)}) collective-permute-start(f32[2,16,256]{2,1,0:T(8,128)S(1)} %get-tuple-element.40), channel_id=1, source_target_pairs={{0,32},{1,33},{2,34},{3,35},{4,36},{5,37},{6,38},{7,39},{8,40},{9,... | collective-permute-start | bytes 98312 | tf_op jit(solution)/shard_map/ppermute | solution.py:29
  140.2 5.1 %collective-permute-start.26 = (f32[2,16,256]{2,1,0:T(8,128)S(1)}, f32[2,16,256]{2,1,0:T(8,128)S(1)}, u32[]{:S(2)}, u32[]{:S(2)}) collective-permute-start(f32[2,16,256]{2,1,0:T(8,128)S(1)} %get-tuple-element.39), channel_id=1, source_target_pairs={{0,48},{1,49},{2,50},{3,51},{4,52},{5,53},{6,54},{7,55},{8,56},{9,... | collective-permute-start | bytes 98312 | tf_op jit(solution)/shard_map/ppermute | solution.py:29
  149.2 27.9 %copy-start.5 = (bf16[2,256,256]{2,1,0:T(8,128)(2,1)}, bf16[2,256,256]{2,1,0:T(8,128)(2,1)S(1)}, u32[]{:S(2)}) copy-start(bf16[2,256,256]{2,1,0:T(8,128)(2,1)S(1)} %multiply_convert_fusion.p0) | copy-start | bytes 786436
  149.2 27.9 %collective-permute-start.14 = (bf16[2,256,256]{2,1,0:T(8,128)(2,1)S(1)}, bf16[2,256,256]{2,1,0:T(8,128)(2,1)S(1)}, u32[]{:S(2)}, u32[]{:S(2)}) collective-permute-start(bf16[2,256,256]{2,1,0:T(8,128)(2,1)S(1)} %multiply_convert_fusion.p0), channel_id=1, source_target_pairs={{0,1},{1,0},{2,3},{3,2},{4,5},{5,4},{6,7},{7,6},{8,9},{9,8},{10,11... | collective-permute-start | bytes 786440 | tf_op jit(solution)/shard_map/ppermute | solution.py:29
  149.3 27.8 %collective-permute-start.15 = (bf16[2,256,256]{2,1,0:T(8,128)(2,1)S(1)}, bf16[2,256,256]{2,1,0:T(8,128)(2,1)S(1)}, u32[]{:S(2)}, u32[]{:S(2)}) collective-permute-start(bf16[2,256,256]{2,1,0:T(8,128)(2,1)S(1)} %multiply_convert_fusion.p0), channel_id=1, source_target_pairs={{0,2},{1,3},{2,0},{3,1},{4,6},{5,7},{6,4},{7,5},{8,10},{9,11},{10,... | collective-permute-start | bytes 786440 | tf_op jit(solution)/shard_map/ppermute | solution.py:29
  151.9 25.3 %collective-permute-start.16 = (bf16[2,256,256]{2,1,0:T(8,128)(2,1)S(1)}, bf16[2,256,256]{2,1,0:T(8,128)(2,1)S(1)}, u32[]{:S(2)}, u32[]{:S(2)}) collective-permute-start(bf16[2,256,256]{2,1,0:T(8,128)(2,1)S(1)} %multiply_convert_fusion.p0), channel_id=1, source_target_pairs={{0,3},{1,2},{2,1},{3,0},{4,7},{5,6},{6,5},{7,4},{8,11},{9,10},{10,... | collective-permute-start | bytes 786440 | tf_op jit(solution)/shard_map/ppermute | solution.py:29
  153.7 22.8 %collective-permute-start.27 = (f32[16,256]{1,0:T(8,128)S(1)}, f32[16,256]{1,0:T(8,128)S(1)}, u32[]{:S(2)}, u32[]{:S(2)}) collective-permute-start(f32[16,256]{1,0:T(8,128)S(1)} %get-tuple-element.42), channel_id=1, source_target_pairs={{0,0},{1,1},{2,128},{3,129},{4,4},{5,5},{6,132},{7,133},{8,8},{9,9... | collective-permute-start | bytes 49160 | tf_op jit(solution)/shard_map/ppermute | solution.py:29
  156.1 20.4 %collective-permute-start.28 = (f32[16,256]{1,0:T(8,128)S(1)}, f32[16,256]{1,0:T(8,128)S(1)}, u32[]{:S(2)}, u32[]{:S(2)}) collective-permute-start(f32[16,256]{1,0:T(8,128)S(1)} %get-tuple-element.41), channel_id=1, source_target_pairs={{0,8},{1,9},{2,136},{3,137},{4,12},{5,13},{6,140},{7,141},{8,0},{9... | collective-permute-start | bytes 49160 | tf_op jit(solution)/shard_map/ppermute | solution.py:29
  (18 other events, 137.5 us)

commit v6 on v5

--- a/solution.py
+++ b/solution.py
@@ -17,6 +17,7 @@
 TILES = NB_DEV * K
 PAIR_BLOCKS = 2 * CB_DEV
 SIDE = 2 * CAP
+VMEM_GRANT = 12 * 2**20
 
 
 def permute(x, move, bands):
@@ -92,6 +93,7 @@
         out_specs=[pl.BlockSpec(memory_space=pltpu.VMEM)] * len(counts),
         scratch_shapes=[pltpu.SMEM((3 * SIDE,), jnp.int32), pltpu.SemaphoreType.DMA((sum(counts),))],
         cost_estimate=pl.CostEstimate(flops=10**8, bytes_accessed=2 * sum(counts) * BLK * BLK * 4, transcendentals=0),
+        compiler_params=pltpu.CompilerParams(vmem_limit_bytes=VMEM_GRANT),
         name="pick_tiles",
     )(place, rows, codes)
 
@@ -184,6 +186,7 @@
             pltpu.SemaphoreType.DMA((3, slots)),
         ],
         cost_estimate=pl.CostEstimate(flops=flops, bytes_accessed=moved, transcendentals=0),
+        compiler_params=pltpu.CompilerParams(vmem_limit_bytes=VMEM_GRANT),
         name="tile_products",
     )(meta, *codes, *blocks)
 
@@ -213,6 +216,7 @@
             bytes_accessed=4 * CHAN * rows * channels * 4,
             transcendentals=rows * channels,
         ),
+        compiler_params=pltpu.CompilerParams(vmem_limit_bytes=VMEM_GRANT),
         name="project",
     )(chan.reshape(1), *pieces, enc_mix, dec_proj, node_embed)
 
@@ -269,10 +273,8 @@
     def over_chan(x):
         return [x] + [go(x, lambda b, c, by=by: (b, c ^ by)) for by in range(1, CHAN)]
 
-    half = decoded_saved.shape[0] // 2
-    dec_first = go(decoded_saved[:half], lambda b, c: (b, c ^ 2))
+    dec_pair = go(decoded_saved, lambda b, c: (b, c ^ 2))
     cot_pair = go(out_cotangent, lambda b, c: (b, c ^ 1))
-    dec_second = go(decoded_saved[half:], lambda b, c: (b, c ^ 2))
 
     near = near_step(band)
     far = far_step_traced(core)
@@ -307,7 +309,7 @@
     pieces = over_chan(aggregates)
     hidden_nodes, node_grad = project(chan, pieces, enc_mix, dec_proj, node_embed)
 
-    w_dec_grad = projection_gradient(go, out_cotangent, decoded_saved, cot_pair, (dec_first, dec_second), bands)
+    w_dec_grad = projection_gradient(go, out_cotangent, decoded_saved, cot_pair, dec_pair, bands)
     return (hidden_nodes, node_grad, w_dec_grad)
 
 
@@ -326,13 +328,8 @@
     def outer(left, right):
         return lax.dot_general(left, right, (((0,), (0,)), ((), ())), preferred_element_type=jnp.float32)
 
-    half = cot.shape[0] // 2
     first = outer(cot, dec)
-    third = lax.optimization_barrier(outer(cot[:half], dec_pair[0]))
-    second = outer(cot_pair, dec)
-    fourth = lax.optimization_barrier(outer(cot_pair[:half], dec_pair[0]))
-    third = third + outer(cot[half:], dec_pair[1])
-    fourth = fourth + outer(cot_pair[half:], dec_pair[1])
+    second, third, fourth = outer(cot_pair, dec), outer(cot, dec_pair), outer(cot_pair, dec_pair)
     whole = jnp.stack([first, second, third, fourth])
     halves = whole.reshape(4, 8, 2, rows, channels)
     own = lax.dynamic_index_in_dim(halves, core, 2, keepdims=False)

time: 182 us -> 184 us (1.011)
  the two profiles are of different devices: /device:TPU:4 before, /device:TPU:28 now
where the time goes in v6:
time: 184 us; the launch traced here: 183 us
  starting transfers between devices  72.3 us (39%)
  waiting for transfers between devices  53.9 us (29%)
  Pallas kernels  30.9 us (17%)
  local copies, waits for them, and re-layouts  13.2 us (7%)
  matrix products  7.79 us (4%)
  other arithmetic  3.5 us (2%)
    ppermute x28, starting transfers between devices, permute(): return lax.ppermute(x, ('band', 'chan'), pairs)  72.3 us
    ppermute x28, waiting for transfers between devices, permute(): return lax.ppermute(x, ('band', 'chan'), pairs)  53.9 us
    pallas_call x3, Pallas kernels, tile_products(): pl.pallas_call(functools.partial(products_kernel, groups, len(codes)), ou...  22.6 us
    unnamed x57, local copies, waits for them, and re-layouts  11.6 us
    dot_general x4, matrix products, outer(): lax.dot_general(left, right, (((0,), (0,)), ((), ())), preferred_element_...  7.79 us
    pallas_call x2, Pallas kernels, pick_tiles(): pl.pallas_call(functools.partial(pick_kernel, picks), out_shape=[jax.Shap...  7.15 us
  transfers between devices with their start and end apart: 28, of which 10 were waited for; matrix products, arithmetic and copies ran while one was open for 7% of the time, Pallas kernels for 16%

profile of v6, /device:TPU:28, one launch (start us, length us, event | category | flops | bytes accessed | tf_op | source)
XLA Modules:
  0.0 182.9 jit_solution(14109625079368827173)
XLA Ops:
  0.6 2.0 %collective-permute-start.17 = (bf16[2048,256]{1,0:T(8,128)(2,1)}, bf16[2048,256]{1,0:T(8,128)(2,1)}, u32[]{:S(2)}, u32[]{:S(2)}) collective-permute-start(bf16[2048,256]{1,0:T(8,128)(2,1)} %param.15), channel_id=1, source_target_pairs={{0,1},{1,0},{2,3},{3,2},{4,5},{5,4},{6,7},{7,6},{8,9},{9,8},{10,11... | collective-permute-start | bytes 3145736 | tf_op jit(solution)/shard_map/ppermute | solution.py:30
  2.6 3.3 %collective-permute-start.18 = (bf16[2048,256]{1,0:T(8,128)(2,1)}, bf16[2048,256]{1,0:T(8,128)(2,1)}, u32[]{:S(2)}, u32[]{:S(2)}) collective-permute-start(bf16[2048,256]{1,0:T(8,128)(2,1)} %param.16), channel_id=1, source_target_pairs={{0,2},{1,3},{2,0},{3,1},{4,6},{5,7},{6,4},{7,5},{8,10},{9,11},{10,... | collective-permute-start | bytes 3145736 | tf_op jit(solution)/shard_map/ppermute | solution.py:30
  8.3 3.2 %pick_tiles.3 = (s32[4,128,128]{2,1,0:T(8,128)}, s32[4,128,128]{2,1,0:T(8,128)}) custom-call(s32[2]{0:T(128)S(1)} %pad_add_fusion.1.place, s32[16,128]{1,0:T(8,128)S(1)} %bitcast.63, s32[32,128,128]{2,1,0:T(8,128)S(1)} %bitcast.56), custom_call_target="tpu_custom_call" | custom-call | flops 100000000 | bytes 1048576 | tf_op jit(solution)/shard_map/pick_tiles/pallas_call | solution.py:89
  11.5 5.2 %collective-permute-start.7 = (s32[4,128,128]{2,1,0:T(8,128)}, s32[4,128,128]{2,1,0:T(8,128)}, u32[]{:S(2)}, u32[]{:S(2)}) collective-permute-start(s32[4,128,128]{2,1,0:T(8,128)} %get-tuple-element.16), channel_id=1, source_target_pairs={{8,19},{9,18},{10,17},{11,16},{12,23},{13,22},{14,21},{15,20},{16,... | collective-permute-start | bytes 786440 | tf_op jit(solution)/shard_map/ppermute | solution.py:30
  17.2 2.4 %fusion.25 = f32[256,256]{1,0:T(8,128)} fusion(bf16[2048,256]{1,0:T(8,128)(2,1)S(1)} %copy-done, bf16[2048,256]{1,0:T(8,128)(2,1)} %param.16), kind=kOutput, calls=%fused_computation.120 | convolution fusion | flops 268435456 | bytes 2359296 | tf_op jit(solution)/shard_map/dot_general | solution.py:329
  21.1 3.9 %pick_tiles.2 = (s32[4,128,128]{2,1,0:T(8,128)S(1)}, s32[4,128,128]{2,1,0:T(8,128)S(1)}, s32[8,128,128]{2,1,0:T(8,128)}) custom-call(s32[2]{0:T(128)S(1)} %pad_add_fusion.1.place, s32[16,128]{1,0:T(8,128)S(1)} %bitcast.64, s32[32,128,128]{2,1,0:T(8,128)S(1)} %bitcast.57), custom_call_target="tpu_custom_call" | custom-call | flops 100000000 | bytes 2097152 | tf_op jit(solution)/shard_map/pick_tiles/pallas_call | solution.py:89
  25.4 2.9 %collective-permute-done.3.refs_1_ = s32[4,128,128]{2,1,0:T(8,128)S(1)} collective-permute-done((s32[4,128,128]{2,1,0:T(8,128)}, s32[4,128,128]{2,1,0:T(8,128)S(1)}, u32[]{:S(2)}, u32[]{:S(2)}) %collective-permute-start.3) | collective-permute-done | bytes 262176 | tf_op jit(solution)/shard_map/ppermute | solution.py:30
  28.2 3.1 %collective-permute-start = (s32[8,128,128]{2,1,0:T(8,128)}, s32[8,128,128]{2,1,0:T(8,128)}, u32[]{:S(2)}, u32[]{:S(2)}) collective-permute-start(s32[8,128,128]{2,1,0:T(8,128)} %get-tuple-element.12), channel_id=1, source_target_pairs={{4,20},{5,21},{6,22},{7,23},{12,28},{13,29},{14,30},{15,31},{16,0}... | collective-permute-start | bytes 1572872 | tf_op jit(solution)/shard_map/ppermute | solution.py:30
  32.1 17.3 %collective-permute-done.17 = bf16[2048,256]{1,0:T(8,128)(2,1)} collective-permute-done((bf16[2048,256]{1,0:T(8,128)(2,1)}, bf16[2048,256]{1,0:T(8,128)(2,1)}, u32[]{:S(2)}, u32[]{:S(2)}) %collective-permute-start.17) | collective-permute-done | bytes 1048608 | tf_op jit(solution)/shard_map/ppermute | solution.py:30
  49.3 8.2 %collective-permute-start.10 = (s32[4,128,128]{2,1,0:T(8,128)S(1)}, s32[4,128,128]{2,1,0:T(8,128)S(1)}, u32[]{:S(2)}, u32[]{:S(2)}) collective-permute-start(s32[4,128,128]{2,1,0:T(8,128)S(1)} %broadcast_select_fusion), channel_id=1, source_target_pairs={{1,2},{2,1},{5,6},{6,5},{8,19},{9,10},{10,9},{11,16},{12,23},{13,1... | collective-permute-start | bytes 786440 | tf_op jit(solution)/shard_map/ppermute | solution.py:30
  57.5 1.7 fusion.26
  59.2 15.3 %collective-permute-start.8 = (s32[4,128,128]{2,1,0:T(8,128)}, s32[4,128,128]{2,1,0:T(8,128)S(1)}, u32[]{:S(2)}, u32[]{:S(2)}) collective-permute-start(s32[4,128,128]{2,1,0:T(8,128)} %collective-permute-done.7.refs_1_), channel_id=1, source_target_pairs={{0,1},{1,0},{2,3},{3,2},{4,5},{5,4},{6,7},{7,6},{8,9},{9,8},{10,11... | collective-permute-start | bytes 786440 | tf_op jit(solution)/shard_map/ppermute | solution.py:30
  74.5 2.0 %fusion.28 = f32[256,256]{1,0:T(8,128)S(1)} fusion(bf16[2048,256]{1,0:T(8,128)(2,1)} %collective-permute-done.17, bf16[2048,256]{1,0:T(8,128)(2,1)} %collective-permute-done.18), kind=kOutput, calls=%fused_computation.123 | convolution fusion | flops 268435456 | bytes 2359296 | tf_op jit(solution)/shard_map/dot_general | solution.py:329
  77.3 3.5 %collective-permute-start.9 = (s32[4,128,128]{2,1,0:T(8,128)}, s32[4,128,128]{2,1,0:T(8,128)S(1)}, u32[]{:S(2)}, u32[]{:S(2)}) collective-permute-start(s32[4,128,128]{2,1,0:T(8,128)} %collective-permute-done.7.refs_1_), channel_id=1, source_target_pairs={{0,2},{1,3},{2,0},{3,1},{4,6},{5,7},{6,4},{7,5},{8,10},{9,11},{10,... | collective-permute-start | bytes 786440 | tf_op jit(solution)/shard_map/ppermute | solution.py:30
  80.7 1.7 fusion.27
  84.1 9.6 %collective-permute-done.9.refs_3_ = s32[4,128,128]{2,1,0:T(8,128)S(1)} collective-permute-done((s32[4,128,128]{2,1,0:T(8,128)}, s32[4,128,128]{2,1,0:T(8,128)S(1)}, u32[]{:S(2)}, u32[]{:S(2)}) %collective-permute-start.9) | collective-permute-done | bytes 262176 | tf_op jit(solution)/shard_map/ppermute | solution.py:30
  94.4 2.5 %collective-permute-start.5 = (s32[4,128,128]{2,1,0:T(8,128)S(1)}, s32[4,128,128]{2,1,0:T(8,128)}, u32[]{:S(2)}, u32[]{:S(2)}) collective-permute-start(s32[4,128,128]{2,1,0:T(8,128)S(1)} %collective-permute-done.3.refs_1_), channel_id=1, source_target_pairs={{0,2},{1,3},{2,0},{3,1},{4,6},{5,7},{6,4},{7,5},{8,10},{9,11},{10,... | collective-permute-start | bytes 786440 | tf_op jit(solution)/shard_map/ppermute | solution.py:30
  103.3 7.1 %tile_products.5 = bf16[2,256,256]{2,1,0:T(8,128)(2,1)S(1)} custom-call(s32[5,16]{1,0:T(8,128)S(1)} %stack.27.refs_0_, s32[4,128,128]{2,1,0:T(8,128)} %collective-permute-done.7.refs_1_, s32[4,128,128]{2,1,0:T(8,128)S(1)} %copy-done.14, s32[4,128,128]{2,1,0:T(8,128)S(1)} %copy-done.16, s32[4,128,128]{2,1,0:T(8,128)S(1)} %copy-done.12, ...), custom_call_target="tpu_custom_call" | custom-call | flops 268435456 | bytes 3145728 | tf_op jit(solution)/shard_map/tile_products/pallas_call | solution.py:175
  110.5 1.9 %collective-permute-start.11 = (bf16[2,256,256]{2,1,0:T(8,128)(2,1)S(1)}, bf16[2,256,256]{2,1,0:T(8,128)(2,1)S(1)}, u32[]{:S(2)}, u32[]{:S(2)}) collective-permute-start(bf16[2,256,256]{2,1,0:T(8,128)(2,1)S(1)} %tile_products.5), channel_id=1, source_target_pairs={{8,24},{9,25},{10,26},{11,27},{12,28},{13,29},{14,30},{15,31},{16,... | collective-permute-start | bytes 786440 | tf_op jit(solution)/shard_map/ppermute | solution.py:30
  112.4 9.4 %tile_products.3 = (bf16[2,256,256]{2,1,0:T(8,128)(2,1)}, f32[2,256,256]{2,1,0:T(8,128)S(1)}) custom-call(s32[5,24]{1,0:T(8,128)S(1)} %pad_add_fusion.refs_0_, s32[8,128,128]{2,1,0:T(8,128)} %collective-permute-done.refs_1_, s32[32,128,128]{2,1,0:T(8,128)S(1)} %bitcast.58, bf16[16,128,256]{2,1,0:T(8,128)(2,1)S(1)} %bitcast.61, ...), custom_call_target="tpu_custom_call" | custom-call | flops 402653184 | bytes 4718592 | tf_op jit(solution)/shard_map/tile_products/pallas_call | solution.py:175
  122.6 6.5 %collective-permute-start.13 = (bf16[2,256,256]{2,1,0:T(8,128)(2,1)}, bf16[2,256,256]{2,1,0:T(8,128)(2,1)S(1)}, u32[]{:S(2)}, u32[]{:S(2)}) collective-permute-start(bf16[2,256,256]{2,1,0:T(8,128)(2,1)} %get-tuple-element.18), channel_id=1, source_target_pairs={{0,16},{1,17},{2,18},{3,19},{8,24},{9,25},{10,26},{11,27},{16,32},... | collective-permute-start | bytes 786440 | tf_op jit(solution)/shard_map/ppermute | solution.py:30
  129.1 6.1 %tile_products.4 = f32[2,256,256]{2,1,0:T(8,128)S(1)} custom-call(s32[5,16]{1,0:T(8,128)S(1)} %stack.26.refs_0_, s32[4,128,128]{2,1,0:T(8,128)S(1)} %collective-permute-done.3.refs_1_, s32[4,128,128]{2,1,0:T(8,128)} %collective-permute-done.4.refs_2_, s32[4,128,128]{2,1,0:T(8,128)} %collective-permute-done.5.refs_3_, ...), custom_call_target="tpu_custom_call" | custom-call | flops 268435456 | bytes 3145728 | tf_op jit(solution)/shard_map/tile_products/pallas_call | solution.py:175
  138.3 1.9 %collective-permute-start.22 = (bf16[8,16,256]{2,1,0:T(8,128)(2,1)S(1)}, bf16[8,16,256]{2,1,0:T(8,128)(2,1)S(1)}, u32[]{:S(2)}, u32[]{:S(2)}) collective-permute-start(bf16[8,16,256]{2,1,0:T(8,128)(2,1)S(1)} %get-tuple-element.34), channel_id=1, source_target_pairs={{0,192},{1,193},{2,194},{3,195},{4,196},{5,197},{6,198},{7,199},{8... | collective-permute-start | bytes 196616 | tf_op jit(solution)/shard_map/ppermute | solution.py:30
  140.9 1.7 collective-permute-done.21
  144.0 2.2 %collective-permute-start.24 = (f32[2,16,256]{2,1,0:T(8,128)S(1)}, f32[2,16,256]{2,1,0:T(8,128)S(1)}, u32[]{:S(2)}, u32[]{:S(2)}) collective-permute-start(f32[2,16,256]{2,1,0:T(8,128)S(1)} %get-tuple-element.38), channel_id=1, source_target_pairs={{0,32},{1,33},{2,34},{3,35},{4,36},{5,37},{6,38},{7,39},{8,40},{9,... | collective-permute-start | bytes 98312 | tf_op jit(solution)/shard_map/ppermute | solution.py:30
  146.2 1.9 %collective-permute-start.25 = (f32[2,16,256]{2,1,0:T(8,128)S(1)}, f32[2,16,256]{2,1,0:T(8,128)S(1)}, u32[]{:S(2)}, u32[]{:S(2)}) collective-permute-start(f32[2,16,256]{2,1,0:T(8,128)S(1)} %get-tuple-element.37), channel_id=1, source_target_pairs={{0,48},{1,49},{2,50},{3,51},{4,52},{5,53},{6,54},{7,55},{8,56},{9,... | collective-permute-start | bytes 98312 | tf_op jit(solution)/shard_map/ppermute | solution.py:30
  149.4 1.9 %collective-permute-done.25 = f32[2,16,256]{2,1,0:T(8,128)S(1)} collective-permute-done((f32[2,16,256]{2,1,0:T(8,128)S(1)}, f32[2,16,256]{2,1,0:T(8,128)S(1)}, u32[]{:S(2)}, u32[]{:S(2)}) %collective-permute-start.25) | collective-permute-done | bytes 32800 | tf_op jit(solution)/shard_map/ppermute | solution.py:30
  151.3 1.7 collective-permute-done.12
  153.2 4.5 %collective-permute-start.15 = (bf16[2,256,256]{2,1,0:T(8,128)(2,1)S(1)}, bf16[2,256,256]{2,1,0:T(8,128)(2,1)S(1)}, u32[]{:S(2)}, u32[]{:S(2)}) collective-permute-start(bf16[2,256,256]{2,1,0:T(8,128)(2,1)S(1)} %multiply_convert_fusion.p0), channel_id=1, source_target_pairs={{0,2},{1,3},{2,0},{3,1},{4,6},{5,7},{6,4},{7,5},{8,10},{9,11},{10,... | collective-permute-start | bytes 786440 | tf_op jit(solution)/shard_map/ppermute | solution.py:30
  158.5 4.1 %collective-permute-start.26 = (f32[16,256]{1,0:T(8,128)S(1)}, f32[16,256]{1,0:T(8,128)S(1)}, u32[]{:S(2)}, u32[]{:S(2)}) collective-permute-start(f32[16,256]{1,0:T(8,128)S(1)} %get-tuple-element.40), channel_id=1, source_target_pairs={{0,0},{1,1},{2,128},{3,129},{4,4},{5,5},{6,132},{7,133},{8,8},{9,9... | collective-permute-start | bytes 49160 | tf_op jit(solution)/shard_map/ppermute | solution.py:30
  162.6 2.2 %collective-permute-start.27 = (f32[16,256]{1,0:T(8,128)S(1)}, f32[16,256]{1,0:T(8,128)S(1)}, u32[]{:S(2)}, u32[]{:S(2)}) collective-permute-start(f32[16,256]{1,0:T(8,128)S(1)} %get-tuple-element.39), channel_id=1, source_target_pairs={{0,8},{1,9},{2,136},{3,137},{4,12},{5,13},{6,140},{7,141},{8,0},{9... | collective-permute-start | bytes 49160 | tf_op jit(solution)/shard_map/ppermute | solution.py:30
  164.8 16.3 %collective-permute-done.26 = f32[16,256]{1,0:T(8,128)S(1)} collective-permute-done((f32[16,256]{1,0:T(8,128)S(1)}, f32[16,256]{1,0:T(8,128)S(1)}, u32[]{:S(2)}, u32[]{:S(2)}) %collective-permute-start.26) | collective-permute-done | bytes 16416 | tf_op jit(solution)/shard_map/ppermute | solution.py:30
  (128 shorter events, 24.6 us)
Async XLA Ops:
  0.6 48.7 %collective-permute-start.17 = (bf16[2048,256]{1,0:T(8,128)(2,1)}, bf16[2048,256]{1,0:T(8,128)(2,1)}, u32[]{:S(2)}, u32[]{:S(2)}) collective-permute-start(bf16[2048,256]{1,0:T(8,128)(2,1)} %param.15), channel_id=1, source_target_pairs={{0,1},{1,0},{2,3},{3,2},{4,5},{5,4},{6,7},{7,6},{8,9},{9,8},{10,11... | collective-permute-start | bytes 3145736 | tf_op jit(solution)/shard_map/ppermute | solution.py:30
  2.6 56.6 %collective-permute-start.18 = (bf16[2048,256]{1,0:T(8,128)(2,1)}, bf16[2048,256]{1,0:T(8,128)(2,1)}, u32[]{:S(2)}, u32[]{:S(2)}) collective-permute-start(bf16[2048,256]{1,0:T(8,128)(2,1)} %param.16), channel_id=1, source_target_pairs={{0,2},{1,3},{2,0},{3,1},{4,6},{5,7},{6,4},{7,5},{8,10},{9,11},{10,... | collective-permute-start | bytes 3145736 | tf_op jit(solution)/shard_map/ppermute | solution.py:30
  11.5 13.5 %collective-permute-start.7 = (s32[4,128,128]{2,1,0:T(8,128)}, s32[4,128,128]{2,1,0:T(8,128)}, u32[]{:S(2)}, u32[]{:S(2)}) collective-permute-start(s32[4,128,128]{2,1,0:T(8,128)} %get-tuple-element.16), channel_id=1, source_target_pairs={{8,19},{9,18},{10,17},{11,16},{12,23},{13,22},{14,21},{15,20},{16,... | collective-permute-start | bytes 786440 | tf_op jit(solution)/shard_map/ppermute | solution.py:30
  16.8 77.6 %collective-permute-start.1 = (bf16[16,128,256]{2,1,0:T(8,128)(2,1)}, bf16[16,128,256]{2,1,0:T(8,128)(2,1)}, u32[]{:S(2)}, u32[]{:S(2)}) collective-permute-start(bf16[16,128,256]{2,1,0:T(8,128)(2,1)} %bitcast.59), channel_id=1, source_target_pairs={{0,4},{1,5},{2,6},{3,7},{4,0},{5,1},{6,2},{7,3},{8,12},{9,13},{10,... | collective-permute-start | bytes 3145736 | tf_op jit(solution)/shard_map/ppermute | solution.py:30
  16.9 11.4 %collective-permute-start.3 = (s32[4,128,128]{2,1,0:T(8,128)}, s32[4,128,128]{2,1,0:T(8,128)S(1)}, u32[]{:S(2)}, u32[]{:S(2)}) collective-permute-start(s32[4,128,128]{2,1,0:T(8,128)} %get-tuple-element.14), channel_id=1, source_target_pairs={{0,11},{1,10},{2,9},{3,8},{4,15},{5,14},{6,13},{7,12},{8,3},{9,2},... | collective-permute-start | bytes 786440 | tf_op jit(solution)/shard_map/ppermute | solution.py:30
  21.1 36.4 %copy-start.20 = (bf16[2048,256]{1,0:T(8,128)(2,1)S(1)}, bf16[2048,256]{1,0:T(8,128)(2,1)}, u32[]{:S(2)}) copy-start(bf16[2048,256]{1,0:T(8,128)(2,1)} %param.16) | copy-start | bytes 3145732
  25.1 71.8 %collective-permute-start.2 = (bf16[16,128,256]{2,1,0:T(8,128)(2,1)S(1)}, bf16[16,128,256]{2,1,0:T(8,128)(2,1)S(1)}, u32[]{:S(2)}, u32[]{:S(2)}) collective-permute-start(bf16[16,128,256]{2,1,0:T(8,128)(2,1)S(1)} %bitcast.52), channel_id=1, source_target_pairs={{0,4},{1,5},{2,6},{3,7},{4,0},{5,1},{6,2},{7,3},{8,12},{9,13},{10,... | collective-permute-start | bytes 3145736 | tf_op jit(solution)/shard_map/ppermute | solution.py:30
  28.2 82.2 %collective-permute-start = (s32[8,128,128]{2,1,0:T(8,128)}, s32[8,128,128]{2,1,0:T(8,128)}, u32[]{:S(2)}, u32[]{:S(2)}) collective-permute-start(s32[8,128,128]{2,1,0:T(8,128)} %get-tuple-element.12), channel_id=1, source_target_pairs={{4,20},{5,21},{6,22},{7,23},{12,28},{13,29},{14,30},{15,31},{16,0}... | collective-permute-start | bytes 1572872 | tf_op jit(solution)/shard_map/ppermute | solution.py:30
  49.3 27.2 %collective-permute-start.10 = (s32[4,128,128]{2,1,0:T(8,128)S(1)}, s32[4,128,128]{2,1,0:T(8,128)S(1)}, u32[]{:S(2)}, u32[]{:S(2)}) collective-permute-start(s32[4,128,128]{2,1,0:T(8,128)S(1)} %broadcast_select_fusion), channel_id=1, source_target_pairs={{1,2},{2,1},{5,6},{6,5},{8,19},{9,10},{10,9},{11,16},{12,23},{13,1... | collective-permute-start | bytes 786440 | tf_op jit(solution)/shard_map/ppermute | solution.py:30
  59.2 24.1 %collective-permute-start.8 = (s32[4,128,128]{2,1,0:T(8,128)}, s32[4,128,128]{2,1,0:T(8,128)S(1)}, u32[]{:S(2)}, u32[]{:S(2)}) collective-permute-start(s32[4,128,128]{2,1,0:T(8,128)} %collective-permute-done.7.refs_1_), channel_id=1, source_target_pairs={{0,1},{1,0},{2,3},{3,2},{4,5},{5,4},{6,7},{7,6},{8,9},{9,8},{10,11... | collective-permute-start | bytes 786440 | tf_op jit(solution)/shard_map/ppermute | solution.py:30
  77.3 16.4 %collective-permute-start.9 = (s32[4,128,128]{2,1,0:T(8,128)}, s32[4,128,128]{2,1,0:T(8,128)S(1)}, u32[]{:S(2)}, u32[]{:S(2)}) collective-permute-start(s32[4,128,128]{2,1,0:T(8,128)} %collective-permute-done.7.refs_1_), channel_id=1, source_target_pairs={{0,2},{1,3},{2,0},{3,1},{4,6},{5,7},{6,4},{7,5},{8,10},{9,11},{10,... | collective-permute-start | bytes 786440 | tf_op jit(solution)/shard_map/ppermute | solution.py:30
  84.1 38.5 %collective-permute-start.6 = (s32[4,128,128]{2,1,0:T(8,128)}, s32[4,128,128]{2,1,0:T(8,128)}, u32[]{:S(2)}, u32[]{:S(2)}) collective-permute-start(s32[4,128,128]{2,1,0:T(8,128)} %broadcast_select_fusion.1), channel_id=1, source_target_pairs={{0,11},{1,2},{2,1},{3,8},{4,15},{5,6},{6,5},{7,12},{8,3},{9,10},{1... | collective-permute-start | bytes 786440 | tf_op jit(solution)/shard_map/ppermute | solution.py:30
  94.4 34.7 %collective-permute-start.4 = (s32[4,128,128]{2,1,0:T(8,128)S(1)}, s32[4,128,128]{2,1,0:T(8,128)}, u32[]{:S(2)}, u32[]{:S(2)}) collective-permute-start(s32[4,128,128]{2,1,0:T(8,128)S(1)} %collective-permute-done.3.refs_1_), channel_id=1, source_target_pairs={{0,1},{1,0},{2,3},{3,2},{4,5},{5,4},{6,7},{7,6},{8,9},{9,8},{10,11... | collective-permute-start | bytes 786440 | tf_op jit(solution)/shard_map/ppermute | solution.py:30
  94.4 34.7 %collective-permute-start.5 = (s32[4,128,128]{2,1,0:T(8,128)S(1)}, s32[4,128,128]{2,1,0:T(8,128)}, u32[]{:S(2)}, u32[]{:S(2)}) collective-permute-start(s32[4,128,128]{2,1,0:T(8,128)S(1)} %collective-permute-done.3.refs_1_), channel_id=1, source_target_pairs={{0,2},{1,3},{2,0},{3,1},{4,6},{5,7},{6,4},{7,5},{8,10},{9,11},{10,... | collective-permute-start | bytes 786440 | tf_op jit(solution)/shard_map/ppermute | solution.py:30
  97.8 37.4 %collective-permute-start.19 = (bf16[4,8,16,256]{3,2,1,0:T(8,128)(2,1)}, bf16[4,8,16,256]{3,2,1,0:T(8,128)(2,1)}, u32[]{:S(2)}, u32[]{:S(2)}) collective-permute-start(bf16[4,8,16,256]{3,2,1,0:T(8,128)(2,1)} %fusion), channel_id=1, source_target_pairs={{0,4},{1,5},{2,6},{3,7},{4,0},{5,1},{6,2},{7,3},{8,12},{9,13},{10,... | collective-permute-start | bytes 786440 | tf_op jit(solution)/shard_map/ppermute | solution.py:30
  110.5 29.7 %collective-permute-start.11 = (bf16[2,256,256]{2,1,0:T(8,128)(2,1)S(1)}, bf16[2,256,256]{2,1,0:T(8,128)(2,1)S(1)}, u32[]{:S(2)}, u32[]{:S(2)}) collective-permute-start(bf16[2,256,256]{2,1,0:T(8,128)(2,1)S(1)} %tile_products.5), channel_id=1, source_target_pairs={{8,24},{9,25},{10,26},{11,27},{12,28},{13,29},{14,30},{15,31},{16,... | collective-permute-start | bytes 786440 | tf_op jit(solution)/shard_map/ppermute | solution.py:30
  122.6 28.7 %collective-permute-start.13 = (bf16[2,256,256]{2,1,0:T(8,128)(2,1)}, bf16[2,256,256]{2,1,0:T(8,128)(2,1)S(1)}, u32[]{:S(2)}, u32[]{:S(2)}) collective-permute-start(bf16[2,256,256]{2,1,0:T(8,128)(2,1)} %get-tuple-element.18), channel_id=1, source_target_pairs={{0,16},{1,17},{2,18},{3,19},{8,24},{9,25},{10,26},{11,27},{16,32},... | collective-permute-start | bytes 786440 | tf_op jit(solution)/shard_map/ppermute | solution.py:30
  136.3 45.4 %copy-start.7 = (bf16[1024,256]{1,0:T(8,128)(2,1)S(1)}, bf16[1024,256]{1,0:T(8,128)(2,1)}, u32[]{:S(2)}) copy-start(bf16[1024,256]{1,0:T(8,128)(2,1)} %enc_mix.1) | copy-start | bytes 1572868
  136.3 45.4 %copy-start.8 = (bf16[1024,256]{1,0:T(8,128)(2,1)S(1)}, bf16[1024,256]{1,0:T(8,128)(2,1)}, u32[]{:S(2)}) copy-start(bf16[1024,256]{1,0:T(8,128)(2,1)} %dec_proj.1) | copy-start | bytes 1572868
  136.4 45.4 %copy-start.17 = (bf16[256,256]{1,0:T(8,128)(2,1)S(1)}, bf16[256,256]{1,0:T(8,128)(2,1)}, u32[]{:S(2)}) copy-start(bf16[256,256]{1,0:T(8,128)(2,1)} %node_embed.1) | copy-start | bytes 393220
  136.4 4.5 %collective-permute-start.20 = (bf16[8,16,256]{2,1,0:T(8,128)(2,1)S(1)}, bf16[8,16,256]{2,1,0:T(8,128)(2,1)S(1)}, u32[]{:S(2)}, u32[]{:S(2)}) collective-permute-start(bf16[8,16,256]{2,1,0:T(8,128)(2,1)S(1)} %get-tuple-element.33), channel_id=1, source_target_pairs={{0,64},{1,65},{2,66},{3,67},{4,68},{5,69},{6,70},{7,71},{8,72},{9,... | collective-permute-start | bytes 196616 | tf_op jit(solution)/shard_map/ppermute | solution.py:30
  136.7 6.0 %collective-permute-start.21 = (bf16[8,16,256]{2,1,0:T(8,128)(2,1)S(1)}, bf16[8,16,256]{2,1,0:T(8,128)(2,1)S(1)}, u32[]{:S(2)}, u32[]{:S(2)}) collective-permute-start(bf16[8,16,256]{2,1,0:T(8,128)(2,1)S(1)} %get-tuple-element.35), channel_id=1, source_target_pairs={{0,128},{1,129},{2,130},{3,131},{4,132},{5,133},{6,134},{7,135},{8... | collective-permute-start | bytes 196616 | tf_op jit(solution)/shard_map/ppermute | solution.py:30
  138.3 5.0 %collective-permute-start.22 = (bf16[8,16,256]{2,1,0:T(8,128)(2,1)S(1)}, bf16[8,16,256]{2,1,0:T(8,128)(2,1)S(1)}, u32[]{:S(2)}, u32[]{:S(2)}) collective-permute-start(bf16[8,16,256]{2,1,0:T(8,128)(2,1)S(1)} %get-tuple-element.34), channel_id=1, source_target_pairs={{0,192},{1,193},{2,194},{3,195},{4,196},{5,197},{6,198},{7,199},{8... | collective-permute-start | bytes 196616 | tf_op jit(solution)/shard_map/ppermute | solution.py:30
  140.2 12.8 %collective-permute-start.12 = (bf16[2,256,256]{2,1,0:T(8,128)(2,1)S(1)}, bf16[2,256,256]{2,1,0:T(8,128)(2,1)S(1)}, u32[]{:S(2)}, u32[]{:S(2)}) collective-permute-start(bf16[2,256,256]{2,1,0:T(8,128)(2,1)S(1)} %add_convert_fusion), channel_id=1, source_target_pairs={{0,8},{1,9},{2,10},{3,11},{4,12},{5,13},{6,14},{7,15},{8,0},{9,1},... | collective-permute-start | bytes 786440 | tf_op jit(solution)/shard_map/ppermute | solution.py:30
  143.3 4.8 %collective-permute-start.23 = (f32[2,16,256]{2,1,0:T(8,128)S(1)}, f32[2,16,256]{2,1,0:T(8,128)S(1)}, u32[]{:S(2)}, u32[]{:S(2)}) collective-permute-start(f32[2,16,256]{2,1,0:T(8,128)S(1)} %get-tuple-element.36), channel_id=1, source_target_pairs={{0,16},{1,17},{2,18},{3,19},{4,20},{5,21},{6,22},{7,23},{8,24},{9,... | collective-permute-start | bytes 98312 | tf_op jit(solution)/shard_map/ppermute | solution.py:30
  144.0 5.4 %collective-permute-start.24 = (f32[2,16,256]{2,1,0:T(8,128)S(1)}, f32[2,16,256]{2,1,0:T(8,128)S(1)}, u32[]{:S(2)}, u32[]{:S(2)}) collective-permute-start(f32[2,16,256]{2,1,0:T(8,128)S(1)} %get-tuple-element.38), channel_id=1, source_target_pairs={{0,32},{1,33},{2,34},{3,35},{4,36},{5,37},{6,38},{7,39},{8,40},{9,... | collective-permute-start | bytes 98312 | tf_op jit(solution)/shard_map/ppermute | solution.py:30
  146.2 5.1 %collective-permute-start.25 = (f32[2,16,256]{2,1,0:T(8,128)S(1)}, f32[2,16,256]{2,1,0:T(8,128)S(1)}, u32[]{:S(2)}, u32[]{:S(2)}) collective-permute-start(f32[2,16,256]{2,1,0:T(8,128)S(1)} %get-tuple-element.37), channel_id=1, source_target_pairs={{0,48},{1,49},{2,50},{3,51},{4,52},{5,53},{6,54},{7,55},{8,56},{9,... | collective-permute-start | bytes 98312 | tf_op jit(solution)/shard_map/ppermute | solution.py:30
  153.1 28.6 %collective-permute-start.14 = (bf16[2,256,256]{2,1,0:T(8,128)(2,1)S(1)}, bf16[2,256,256]{2,1,0:T(8,128)(2,1)S(1)}, u32[]{:S(2)}, u32[]{:S(2)}) collective-permute-start(bf16[2,256,256]{2,1,0:T(8,128)(2,1)S(1)} %multiply_convert_fusion.p0), channel_id=1, source_target_pairs={{0,1},{1,0},{2,3},{3,2},{4,5},{5,4},{6,7},{7,6},{8,9},{9,8},{10,11... | collective-permute-start | bytes 786440 | tf_op jit(solution)/shard_map/ppermute | solution.py:30
  153.2 28.5 %collective-permute-start.15 = (bf16[2,256,256]{2,1,0:T(8,128)(2,1)S(1)}, bf16[2,256,256]{2,1,0:T(8,128)(2,1)S(1)}, u32[]{:S(2)}, u32[]{:S(2)}) collective-permute-start(bf16[2,256,256]{2,1,0:T(8,128)(2,1)S(1)} %multiply_convert_fusion.p0), channel_id=1, source_target_pairs={{0,2},{1,3},{2,0},{3,1},{4,6},{5,7},{6,4},{7,5},{8,10},{9,11},{10,... | collective-permute-start | bytes 786440 | tf_op jit(solution)/shard_map/ppermute | solution.py:30
  157.7 24.0 %collective-permute-start.16 = (bf16[2,256,256]{2,1,0:T(8,128)(2,1)S(1)}, bf16[2,256,256]{2,1,0:T(8,128)(2,1)S(1)}, u32[]{:S(2)}, u32[]{:S(2)}) collective-permute-start(bf16[2,256,256]{2,1,0:T(8,128)(2,1)S(1)} %multiply_convert_fusion.p0), channel_id=1, source_target_pairs={{0,3},{1,2},{2,1},{3,0},{4,7},{5,6},{6,5},{7,4},{8,11},{9,10},{10,... | collective-permute-start | bytes 786440 | tf_op jit(solution)/shard_map/ppermute | solution.py:30
  158.5 22.6 %collective-permute-start.26 = (f32[16,256]{1,0:T(8,128)S(1)}, f32[16,256]{1,0:T(8,128)S(1)}, u32[]{:S(2)}, u32[]{:S(2)}) collective-permute-start(f32[16,256]{1,0:T(8,128)S(1)} %get-tuple-element.40), channel_id=1, source_target_pairs={{0,0},{1,1},{2,128},{3,129},{4,4},{5,5},{6,132},{7,133},{8,8},{9,9... | collective-permute-start | bytes 49160 | tf_op jit(solution)/shard_map/ppermute | solution.py:30
  162.6 18.5 %collective-permute-start.27 = (f32[16,256]{1,0:T(8,128)S(1)}, f32[16,256]{1,0:T(8,128)S(1)}, u32[]{:S(2)}, u32[]{:S(2)}) collective-permute-start(f32[16,256]{1,0:T(8,128)S(1)} %get-tuple-element.39), channel_id=1, source_target_pairs={{0,8},{1,9},{2,136},{3,137},{4,12},{5,13},{6,140},{7,141},{8,0},{9... | collective-permute-start | bytes 49160 | tf_op jit(solution)/shard_map/ppermute | solution.py:30
  (24 other events, 176.3 us)

commit v7 on v5

--- a/solution.py
+++ b/solution.py
@@ -17,6 +17,7 @@
 TILES = NB_DEV * K
 PAIR_BLOCKS = 2 * CB_DEV
 SIDE = 2 * CAP
+VMEM_GRANT = 12 * 2**20
 
 
 def permute(x, move, bands):
@@ -92,6 +93,7 @@
         out_specs=[pl.BlockSpec(memory_space=pltpu.VMEM)] * len(counts),
         scratch_shapes=[pltpu.SMEM((3 * SIDE,), jnp.int32), pltpu.SemaphoreType.DMA((sum(counts),))],
         cost_estimate=pl.CostEstimate(flops=10**8, bytes_accessed=2 * sum(counts) * BLK * BLK * 4, transcendentals=0),
+        compiler_params=pltpu.CompilerParams(vmem_limit_bytes=VMEM_GRANT),
         name="pick_tiles",
     )(place, rows, codes)
 
@@ -184,6 +186,7 @@
             pltpu.SemaphoreType.DMA((3, slots)),
         ],
         cost_estimate=pl.CostEstimate(flops=flops, bytes_accessed=moved, transcendentals=0),
+        compiler_params=pltpu.CompilerParams(vmem_limit_bytes=VMEM_GRANT),
         name="tile_products",
     )(meta, *codes, *blocks)
 
@@ -213,6 +216,7 @@
             bytes_accessed=4 * CHAN * rows * channels * 4,
             transcendentals=rows * channels,
         ),
+        compiler_params=pltpu.CompilerParams(vmem_limit_bytes=VMEM_GRANT),
         name="project",
     )(chan.reshape(1), *pieces, enc_mix, dec_proj, node_embed)
 
@@ -272,7 +276,7 @@
     half = decoded_saved.shape[0] // 2
     dec_first = go(decoded_saved[:half], lambda b, c: (b, c ^ 2))
     cot_pair = go(out_cotangent, lambda b, c: (b, c ^ 1))
-    dec_second = go(decoded_saved[half:], lambda b, c: (b, c ^ 2))
+    dec_second = go(lax.optimization_barrier(decoded_saved)[half:], lambda b, c: (b, c ^ 2))
 
     near = near_step(band)
     far = far_step_traced(core)

time: 182 us -> 192 us (1.055)
  local copies, waits for them, and re-layouts: 8.33 us -> 16.1 us
  Pallas kernels: 26.2 us -> 32.3 us
  starting transfers between devices: 72.7 us -> 68.5 us
  other arithmetic: 6.69 us -> 3.56 us
    pallas_call x3, Pallas kernels: 15.5 us -> 24 us  [tile_products(): pl.pallas_call(functools.partial(products_kernel, groups, len(codes)), ou...]
    unnamed x43 -> x61, local copies, waits for them, and re-layouts: 3.25 us -> 10.8 us
    ppermute x29, starting transfers between devices: 72.7 us -> 68.5 us  [permute(): return lax.ppermute(x, ('band', 'chan'), pairs)]
    select_n x2, other arithmetic: 2.76 us -> 0.78 us  [along_chan(): jnp.where(at_end, extra, x)]
  transfers between devices with their start and end apart: 29 -> 29, of which waited for: 9 -> 9; matrix products, arithmetic and copies ran while one was open for 10% -> 10% of each run, Pallas kernels for 13% -> 16%
where the time goes in v7:
time: 192 us; the launch traced here: 191 us
  starting transfers between devices  68.5 us (36%)
  waiting for transfers between devices  59 us (31%)
  Pallas kernels  32.3 us (17%)
  local copies, waits for them, and re-layouts  16.1 us (8%)
  matrix products  9.97 us (5%)
  other arithmetic  3.56 us (2%)
    ppermute x29, starting transfers between devices, permute(): return lax.ppermute(x, ('band', 'chan'), pairs)  68.5 us
    ppermute x29, waiting for transfers between devices, permute(): return lax.ppermute(x, ('band', 'chan'), pairs)  59 us
    pallas_call x3, Pallas kernels, tile_products(): pl.pallas_call(functools.partial(products_kernel, groups, len(codes)), ou...  24 us
    unnamed x61, local copies, waits for them, and re-layouts  10.8 us
    dot_general x6, matrix products, outer(): lax.dot_general(left, right, (((0,), (0,)), ((), ())), preferred_element_...  9.97 us
    pallas_call x2, Pallas kernels, pick_tiles(): pl.pallas_call(functools.partial(pick_kernel, picks), out_shape=[jax.Shap...  7.14 us
  transfers between devices with their start and end apart: 29, of which 9 were waited for; matrix products, arithmetic and copies ran while one was open for 10% of the time, Pallas kernels for 16%

profile of v7, /device:TPU:4, one launch (start us, length us, event | category | flops | bytes accessed | tf_op | source)
XLA Modules:
  0.0 190.8 jit_solution(2332616608324075224)
XLA Ops:
  0.7 2.0 %collective-permute-start.17 = (bf16[2048,256]{1,0:T(8,128)(2,1)}, bf16[2048,256]{1,0:T(8,128)(2,1)}, u32[]{:S(2)}, u32[]{:S(2)}) collective-permute-start(bf16[2048,256]{1,0:T(8,128)(2,1)} %param.15), channel_id=1, source_target_pairs={{0,1},{1,0},{2,3},{3,2},{4,5},{5,4},{6,7},{7,6},{8,9},{9,8},{10,11... | collective-permute-start | bytes 3145736 | tf_op jit(solution)/shard_map/ppermute | solution.py:30
  2.7 1.9 slice.71
  4.5 3.3 %collective-permute-start.19 = (bf16[1024,256]{1,0:T(8,128)(2,1)}, bf16[1024,256]{1,0:T(8,128)(2,1)}, u32[]{:S(2)}, u32[]{:S(2)}) collective-permute-start(bf16[1024,256]{1,0:T(8,128)(2,1)} %slice.71), channel_id=1, source_target_pairs={{0,2},{1,3},{2,0},{3,1},{4,6},{5,7},{6,4},{7,5},{8,10},{9,11},{10,... | collective-permute-start | bytes 1572872 | tf_op jit(solution)/shard_map/ppermute | solution.py:30
  7.8 1.9 slice.64
  10.5 3.2 %pick_tiles.3 = (s32[4,128,128]{2,1,0:T(8,128)}, s32[4,128,128]{2,1,0:T(8,128)}) custom-call(s32[2]{0:T(128)S(1)} %pad_add_fusion.1.place, s32[16,128]{1,0:T(8,128)S(1)} %bitcast.63, s32[32,128,128]{2,1,0:T(8,128)S(1)} %bitcast.52), custom_call_target="tpu_custom_call" | custom-call | flops 100000000 | bytes 1048576 | tf_op jit(solution)/shard_map/pick_tiles/pallas_call | solution.py:89
  13.7 8.9 %collective-permute-start.7 = (s32[4,128,128]{2,1,0:T(8,128)}, s32[4,128,128]{2,1,0:T(8,128)}, u32[]{:S(2)}, u32[]{:S(2)}) collective-permute-start(s32[4,128,128]{2,1,0:T(8,128)} %get-tuple-element.16), channel_id=1, source_target_pairs={{8,19},{9,18},{10,17},{11,16},{12,23},{13,22},{14,21},{15,20},{16,... | collective-permute-start | bytes 786440 | tf_op jit(solution)/shard_map/ppermute | solution.py:30
  22.7 2.4 %fusion.33 = f32[256,256]{1,0:T(8,128)} fusion(bf16[2048,256]{1,0:T(8,128)(2,1)S(1)} %copy-done.1, bf16[2048,256]{1,0:T(8,128)(2,1)} %param.16), kind=kOutput, calls=%fused_computation.128 | convolution fusion | flops 268435456 | bytes 2359296 | tf_op jit(solution)/shard_map/dot_general | solution.py:331
  26.7 3.9 %pick_tiles.2 = (s32[4,128,128]{2,1,0:T(8,128)S(1)}, s32[4,128,128]{2,1,0:T(8,128)S(1)}, s32[8,128,128]{2,1,0:T(8,128)}) custom-call(s32[2]{0:T(128)S(1)} %pad_add_fusion.1.place, s32[16,128]{1,0:T(8,128)S(1)} %bitcast.64, s32[32,128,128]{2,1,0:T(8,128)S(1)} %bitcast.53), custom_call_target="tpu_custom_call" | custom-call | flops 100000000 | bytes 2097152 | tf_op jit(solution)/shard_map/pick_tiles/pallas_call | solution.py:89
  30.8 2.6 %collective-permute-done.3.refs_1_ = s32[4,128,128]{2,1,0:T(8,128)S(1)} collective-permute-done((s32[4,128,128]{2,1,0:T(8,128)}, s32[4,128,128]{2,1,0:T(8,128)S(1)}, u32[]{:S(2)}, u32[]{:S(2)}) %collective-permute-start.3) | collective-permute-done | bytes 262176 | tf_op jit(solution)/shard_map/ppermute | solution.py:30
  34.1 19.5 %collective-permute-done.18 = bf16[1024,256]{1,0:T(8,128)(2,1)} collective-permute-done((bf16[1024,256]{1,0:T(8,128)(2,1)}, bf16[1024,256]{1,0:T(8,128)(2,1)}, u32[]{:S(2)}, u32[]{:S(2)}) %collective-permute-start.18) | collective-permute-done | bytes 524320 | tf_op jit(solution)/shard_map/ppermute | solution.py:30
  53.6 4.9 %collective-permute-start = (s32[8,128,128]{2,1,0:T(8,128)}, s32[8,128,128]{2,1,0:T(8,128)}, u32[]{:S(2)}, u32[]{:S(2)}) collective-permute-start(s32[8,128,128]{2,1,0:T(8,128)} %get-tuple-element.12), channel_id=1, source_target_pairs={{4,20},{5,21},{6,22},{7,23},{12,28},{13,29},{14,30},{15,31},{16,0}... | collective-permute-start | bytes 1572872 | tf_op jit(solution)/shard_map/ppermute | solution.py:30
  59.9 12.6 %collective-permute-start.10 = (s32[4,128,128]{2,1,0:T(8,128)S(1)}, s32[4,128,128]{2,1,0:T(8,128)S(1)}, u32[]{:S(2)}, u32[]{:S(2)}) collective-permute-start(s32[4,128,128]{2,1,0:T(8,128)S(1)} %broadcast_select_fusion), channel_id=1, source_target_pairs={{1,2},{2,1},{5,6},{6,5},{8,19},{9,10},{10,9},{11,16},{12,23},{13,1... | collective-permute-start | bytes 786440 | tf_op jit(solution)/shard_map/ppermute | solution.py:30
  73.9 4.1 %collective-permute-start.8 = (s32[4,128,128]{2,1,0:T(8,128)}, s32[4,128,128]{2,1,0:T(8,128)S(1)}, u32[]{:S(2)}, u32[]{:S(2)}) collective-permute-start(s32[4,128,128]{2,1,0:T(8,128)} %collective-permute-done.7.refs_1_), channel_id=1, source_target_pairs={{0,1},{1,0},{2,3},{3,2},{4,5},{5,4},{6,7},{7,6},{8,9},{9,8},{10,11... | collective-permute-start | bytes 786440 | tf_op jit(solution)/shard_map/ppermute | solution.py:30
  78.0 1.7 fusion.34
  86.2 9.8 %collective-permute-done.9.refs_3_ = s32[4,128,128]{2,1,0:T(8,128)S(1)} collective-permute-done((s32[4,128,128]{2,1,0:T(8,128)}, s32[4,128,128]{2,1,0:T(8,128)S(1)}, u32[]{:S(2)}, u32[]{:S(2)}) %collective-permute-start.9) | collective-permute-done | bytes 262176 | tf_op jit(solution)/shard_map/ppermute | solution.py:30
  97.7 2.4 %collective-permute-start.5 = (s32[4,128,128]{2,1,0:T(8,128)S(1)}, s32[4,128,128]{2,1,0:T(8,128)}, u32[]{:S(2)}, u32[]{:S(2)}) collective-permute-start(s32[4,128,128]{2,1,0:T(8,128)S(1)} %collective-permute-done.3.refs_1_), channel_id=1, source_target_pairs={{0,2},{1,3},{2,0},{3,1},{4,6},{5,7},{6,4},{7,5},{8,10},{9,11},{10,... | collective-permute-start | bytes 786440 | tf_op jit(solution)/shard_map/ppermute | solution.py:30
  107.9 7.3 %tile_products.5 = bf16[2,256,256]{2,1,0:T(8,128)(2,1)S(1)} custom-call(s32[5,16]{1,0:T(8,128)S(1)} %stack.27.refs_0_, s32[4,128,128]{2,1,0:T(8,128)} %collective-permute-done.7.refs_1_, s32[4,128,128]{2,1,0:T(8,128)S(1)} %copy-done.16, s32[4,128,128]{2,1,0:T(8,128)S(1)} %copy-done.18, s32[4,128,128]{2,1,0:T(8,128)S(1)} %copy-done.14, ...), custom_call_target="tpu_custom_call" | custom-call | flops 268435456 | bytes 3145728 | tf_op jit(solution)/shard_map/tile_products/pallas_call | solution.py:175
  115.2 4.3 %collective-permute-start.11 = (bf16[2,256,256]{2,1,0:T(8,128)(2,1)S(1)}, bf16[2,256,256]{2,1,0:T(8,128)(2,1)S(1)}, u32[]{:S(2)}, u32[]{:S(2)}) collective-permute-start(bf16[2,256,256]{2,1,0:T(8,128)(2,1)S(1)} %tile_products.5), channel_id=1, source_target_pairs={{8,24},{9,25},{10,26},{11,27},{12,28},{13,29},{14,30},{15,31},{16,... | collective-permute-start | bytes 786440 | tf_op jit(solution)/shard_map/ppermute | solution.py:30
  119.5 10.3 %tile_products.3 = (bf16[2,256,256]{2,1,0:T(8,128)(2,1)}, f32[2,256,256]{2,1,0:T(8,128)S(1)}) custom-call(s32[5,24]{1,0:T(8,128)S(1)} %pad_add_fusion.refs_0_, s32[8,128,128]{2,1,0:T(8,128)} %collective-permute-done.refs_1_, s32[32,128,128]{2,1,0:T(8,128)S(1)} %bitcast.54, bf16[16,128,256]{2,1,0:T(8,128)(2,1)S(1)} %bitcast.61, ...), custom_call_target="tpu_custom_call" | custom-call | flops 402653184 | bytes 4718592 | tf_op jit(solution)/shard_map/tile_products/pallas_call | solution.py:175
  129.9 2.2 %collective-permute-start.13 = (bf16[2,256,256]{2,1,0:T(8,128)(2,1)}, bf16[2,256,256]{2,1,0:T(8,128)(2,1)S(1)}, u32[]{:S(2)}, u32[]{:S(2)}) collective-permute-start(bf16[2,256,256]{2,1,0:T(8,128)(2,1)} %get-tuple-element.18), channel_id=1, source_target_pairs={{0,16},{1,17},{2,18},{3,19},{8,24},{9,25},{10,26},{11,27},{16,32},... | collective-permute-start | bytes 786440 | tf_op jit(solution)/shard_map/ppermute | solution.py:30
  132.1 6.4 %tile_products.4 = f32[2,256,256]{2,1,0:T(8,128)S(1)} custom-call(s32[5,16]{1,0:T(8,128)S(1)} %stack.26.refs_0_, s32[4,128,128]{2,1,0:T(8,128)S(1)} %collective-permute-done.3.refs_1_, s32[4,128,128]{2,1,0:T(8,128)} %collective-permute-done.4.refs_2_, s32[4,128,128]{2,1,0:T(8,128)} %collective-permute-done.5.refs_3_, ...), custom_call_target="tpu_custom_call" | custom-call | flops 268435456 | bytes 3145728 | tf_op jit(solution)/shard_map/tile_products/pallas_call | solution.py:175
  143.4 1.8 collective-permute-start.12
  145.2 2.1 %collective-permute-done.22 = bf16[8,16,256]{2,1,0:T(8,128)(2,1)S(1)} collective-permute-done((bf16[8,16,256]{2,1,0:T(8,128)(2,1)S(1)}, bf16[8,16,256]{2,1,0:T(8,128)(2,1)S(1)}, u32[]{:S(2)}, u32[]{:S(2)}) %collective-permute-start.22) | collective-permute-done | bytes 65568 | tf_op jit(solution)/shard_map/ppermute | solution.py:30
  148.5 3.4 %collective-permute-start.25 = (f32[2,16,256]{2,1,0:T(8,128)S(1)}, f32[2,16,256]{2,1,0:T(8,128)S(1)}, u32[]{:S(2)}, u32[]{:S(2)}) collective-permute-start(f32[2,16,256]{2,1,0:T(8,128)S(1)} %get-tuple-element.38), channel_id=1, source_target_pairs={{0,32},{1,33},{2,34},{3,35},{4,36},{5,37},{6,38},{7,39},{8,40},{9,... | collective-permute-start | bytes 98312 | tf_op jit(solution)/shard_map/ppermute | solution.py:30
  152.4 1.8 collective-permute-done.25
  154.1 2.9 %collective-permute-done.26 = f32[2,16,256]{2,1,0:T(8,128)S(1)} collective-permute-done((f32[2,16,256]{2,1,0:T(8,128)S(1)}, f32[2,16,256]{2,1,0:T(8,128)S(1)}, u32[]{:S(2)}, u32[]{:S(2)}) %collective-permute-start.26) | collective-permute-done | bytes 32800 | tf_op jit(solution)/shard_map/ppermute | solution.py:30
  157.1 3.6 %collective-permute-done.12 = bf16[2,256,256]{2,1,0:T(8,128)(2,1)S(1)} collective-permute-done((bf16[2,256,256]{2,1,0:T(8,128)(2,1)S(1)}, bf16[2,256,256]{2,1,0:T(8,128)(2,1)S(1)}, u32[]{:S(2)}, u32[]{:S(2)}) %collective-permute-start.12) | collective-permute-done | bytes 262176 | tf_op jit(solution)/shard_map/ppermute | solution.py:30
  160.8 2.4 %collective-permute-start.15 = (bf16[2,256,256]{2,1,0:T(8,128)(2,1)S(1)}, bf16[2,256,256]{2,1,0:T(8,128)(2,1)S(1)}, u32[]{:S(2)}, u32[]{:S(2)}) collective-permute-start(bf16[2,256,256]{2,1,0:T(8,128)(2,1)S(1)} %multiply_convert_fusion.p0), channel_id=1, source_target_pairs={{0,2},{1,3},{2,0},{3,1},{4,6},{5,7},{6,4},{7,5},{8,10},{9,11},{10,... | collective-permute-start | bytes 786440 | tf_op jit(solution)/shard_map/ppermute | solution.py:30
  163.2 2.0 %collective-permute-start.16 = (bf16[2,256,256]{2,1,0:T(8,128)(2,1)S(1)}, bf16[2,256,256]{2,1,0:T(8,128)(2,1)S(1)}, u32[]{:S(2)}, u32[]{:S(2)}) collective-permute-start(bf16[2,256,256]{2,1,0:T(8,128)(2,1)S(1)} %multiply_convert_fusion.p0), channel_id=1, source_target_pairs={{0,3},{1,2},{2,1},{3,0},{4,7},{5,6},{6,5},{7,4},{8,11},{9,10},{10,... | collective-permute-start | bytes 786440 | tf_op jit(solution)/shard_map/ppermute | solution.py:30
  165.2 2.4 %collective-permute-start.27 = (f32[16,256]{1,0:T(8,128)S(1)}, f32[16,256]{1,0:T(8,128)S(1)}, u32[]{:S(2)}, u32[]{:S(2)}) collective-permute-start(f32[16,256]{1,0:T(8,128)S(1)} %get-tuple-element.40), channel_id=1, source_target_pairs={{0,0},{1,1},{2,128},{3,129},{4,4},{5,5},{6,132},{7,133},{8,8},{9,9... | collective-permute-start | bytes 49160 | tf_op jit(solution)/shard_map/ppermute | solution.py:30
  167.7 4.9 %collective-permute-start.28 = (f32[16,256]{1,0:T(8,128)S(1)}, f32[16,256]{1,0:T(8,128)S(1)}, u32[]{:S(2)}, u32[]{:S(2)}) collective-permute-start(f32[16,256]{1,0:T(8,128)S(1)} %get-tuple-element.39), channel_id=1, source_target_pairs={{0,8},{1,9},{2,136},{3,137},{4,12},{5,13},{6,140},{7,141},{8,0},{9... | collective-permute-start | bytes 49160 | tf_op jit(solution)/shard_map/ppermute | solution.py:30
  172.6 16.5 %collective-permute-done.27 = f32[16,256]{1,0:T(8,128)S(1)} collective-permute-done((f32[16,256]{1,0:T(8,128)S(1)}, f32[16,256]{1,0:T(8,128)S(1)}, u32[]{:S(2)}, u32[]{:S(2)}) %collective-permute-start.27) | collective-permute-done | bytes 16416 | tf_op jit(solution)/shard_map/ppermute | solution.py:30
  (140 shorter events, 30.1 us)
Async XLA Ops:
  0.7 73.2 %collective-permute-start.17 = (bf16[2048,256]{1,0:T(8,128)(2,1)}, bf16[2048,256]{1,0:T(8,128)(2,1)}, u32[]{:S(2)}, u32[]{:S(2)}) collective-permute-start(bf16[2048,256]{1,0:T(8,128)(2,1)} %param.15), channel_id=1, source_target_pairs={{0,1},{1,0},{2,3},{3,2},{4,5},{5,4},{6,7},{7,6},{8,9},{9,8},{10,11... | collective-permute-start | bytes 3145736 | tf_op jit(solution)/shard_map/ppermute | solution.py:30
  4.5 55.4 %collective-permute-start.19 = (bf16[1024,256]{1,0:T(8,128)(2,1)}, bf16[1024,256]{1,0:T(8,128)(2,1)}, u32[]{:S(2)}, u32[]{:S(2)}) collective-permute-start(bf16[1024,256]{1,0:T(8,128)(2,1)} %slice.71), channel_id=1, source_target_pairs={{0,2},{1,3},{2,0},{3,1},{4,6},{5,7},{6,4},{7,5},{8,10},{9,11},{10,... | collective-permute-start | bytes 1572872 | tf_op jit(solution)/shard_map/ppermute | solution.py:30
  9.7 43.9 %collective-permute-start.18 = (bf16[1024,256]{1,0:T(8,128)(2,1)}, bf16[1024,256]{1,0:T(8,128)(2,1)}, u32[]{:S(2)}, u32[]{:S(2)}) collective-permute-start(bf16[1024,256]{1,0:T(8,128)(2,1)} %slice.64), channel_id=1, source_target_pairs={{0,2},{1,3},{2,0},{3,1},{4,6},{5,7},{6,4},{7,5},{8,10},{9,11},{10,... | collective-permute-start | bytes 1572872 | tf_op jit(solution)/shard_map/ppermute | solution.py:30
  13.7 16.9 %collective-permute-start.7 = (s32[4,128,128]{2,1,0:T(8,128)}, s32[4,128,128]{2,1,0:T(8,128)}, u32[]{:S(2)}, u32[]{:S(2)}) collective-permute-start(s32[4,128,128]{2,1,0:T(8,128)} %get-tuple-element.16), channel_id=1, source_target_pairs={{8,19},{9,18},{10,17},{11,16},{12,23},{13,22},{14,21},{15,20},{16,... | collective-permute-start | bytes 786440 | tf_op jit(solution)/shard_map/ppermute | solution.py:30
  22.6 10.7 %collective-permute-start.3 = (s32[4,128,128]{2,1,0:T(8,128)}, s32[4,128,128]{2,1,0:T(8,128)S(1)}, u32[]{:S(2)}, u32[]{:S(2)}) collective-permute-start(s32[4,128,128]{2,1,0:T(8,128)} %get-tuple-element.14), channel_id=1, source_target_pairs={{0,11},{1,10},{2,9},{3,8},{4,15},{5,14},{6,13},{7,12},{8,3},{9,2},... | collective-permute-start | bytes 786440 | tf_op jit(solution)/shard_map/ppermute | solution.py:30
  30.6 66.1 %collective-permute-start.1 = (bf16[16,128,256]{2,1,0:T(8,128)(2,1)S(1)}, bf16[16,128,256]{2,1,0:T(8,128)(2,1)S(1)}, u32[]{:S(2)}, u32[]{:S(2)}) collective-permute-start(bf16[16,128,256]{2,1,0:T(8,128)(2,1)S(1)} %bitcast.59), channel_id=1, source_target_pairs={{0,4},{1,5},{2,6},{3,7},{4,0},{5,1},{6,2},{7,3},{8,12},{9,13},{10,... | collective-permute-start | bytes 3145736 | tf_op jit(solution)/shard_map/ppermute | solution.py:30
  33.4 66.8 %collective-permute-start.2 = (bf16[16,128,256]{2,1,0:T(8,128)(2,1)S(1)}, bf16[16,128,256]{2,1,0:T(8,128)(2,1)S(1)}, u32[]{:S(2)}, u32[]{:S(2)}) collective-permute-start(bf16[16,128,256]{2,1,0:T(8,128)(2,1)S(1)} %bitcast.55), channel_id=1, source_target_pairs={{0,4},{1,5},{2,6},{3,7},{4,0},{5,1},{6,2},{7,3},{8,12},{9,13},{10,... | collective-permute-start | bytes 3145736 | tf_op jit(solution)/shard_map/ppermute | solution.py:30
  53.6 61.6 %collective-permute-start = (s32[8,128,128]{2,1,0:T(8,128)}, s32[8,128,128]{2,1,0:T(8,128)}, u32[]{:S(2)}, u32[]{:S(2)}) collective-permute-start(s32[8,128,128]{2,1,0:T(8,128)} %get-tuple-element.12), channel_id=1, source_target_pairs={{4,20},{5,21},{6,22},{7,23},{12,28},{13,29},{14,30},{15,31},{16,0}... | collective-permute-start | bytes 1572872 | tf_op jit(solution)/shard_map/ppermute | solution.py:30
  59.9 21.4 %collective-permute-start.10 = (s32[4,128,128]{2,1,0:T(8,128)S(1)}, s32[4,128,128]{2,1,0:T(8,128)S(1)}, u32[]{:S(2)}, u32[]{:S(2)}) collective-permute-start(s32[4,128,128]{2,1,0:T(8,128)S(1)} %broadcast_select_fusion), channel_id=1, source_target_pairs={{1,2},{2,1},{5,6},{6,5},{8,19},{9,10},{10,9},{11,16},{12,23},{13,1... | collective-permute-start | bytes 786440 | tf_op jit(solution)/shard_map/ppermute | solution.py:30
  73.9 11.5 %collective-permute-start.8 = (s32[4,128,128]{2,1,0:T(8,128)}, s32[4,128,128]{2,1,0:T(8,128)S(1)}, u32[]{:S(2)}, u32[]{:S(2)}) collective-permute-start(s32[4,128,128]{2,1,0:T(8,128)} %collective-permute-done.7.refs_1_), channel_id=1, source_target_pairs={{0,1},{1,0},{2,3},{3,2},{4,5},{5,4},{6,7},{7,6},{8,9},{9,8},{10,11... | collective-permute-start | bytes 786440 | tf_op jit(solution)/shard_map/ppermute | solution.py:30
  81.3 14.7 %collective-permute-start.9 = (s32[4,128,128]{2,1,0:T(8,128)}, s32[4,128,128]{2,1,0:T(8,128)S(1)}, u32[]{:S(2)}, u32[]{:S(2)}) collective-permute-start(s32[4,128,128]{2,1,0:T(8,128)} %collective-permute-done.7.refs_1_), channel_id=1, source_target_pairs={{0,2},{1,3},{2,0},{3,1},{4,6},{5,7},{6,4},{7,5},{8,10},{9,11},{10,... | collective-permute-start | bytes 786440 | tf_op jit(solution)/shard_map/ppermute | solution.py:30
  86.1 43.7 %collective-permute-start.6 = (s32[4,128,128]{2,1,0:T(8,128)}, s32[4,128,128]{2,1,0:T(8,128)}, u32[]{:S(2)}, u32[]{:S(2)}) collective-permute-start(s32[4,128,128]{2,1,0:T(8,128)} %broadcast_select_fusion.1), channel_id=1, source_target_pairs={{0,11},{1,2},{2,1},{3,8},{4,15},{5,6},{6,5},{7,12},{8,3},{9,10},{1... | collective-permute-start | bytes 786440 | tf_op jit(solution)/shard_map/ppermute | solution.py:30
  96.7 35.4 %collective-permute-start.4 = (s32[4,128,128]{2,1,0:T(8,128)S(1)}, s32[4,128,128]{2,1,0:T(8,128)}, u32[]{:S(2)}, u32[]{:S(2)}) collective-permute-start(s32[4,128,128]{2,1,0:T(8,128)S(1)} %collective-permute-done.3.refs_1_), channel_id=1, source_target_pairs={{0,1},{1,0},{2,3},{3,2},{4,5},{5,4},{6,7},{7,6},{8,9},{9,8},{10,11... | collective-permute-start | bytes 786440 | tf_op jit(solution)/shard_map/ppermute | solution.py:30
  97.7 34.4 %collective-permute-start.5 = (s32[4,128,128]{2,1,0:T(8,128)S(1)}, s32[4,128,128]{2,1,0:T(8,128)}, u32[]{:S(2)}, u32[]{:S(2)}) collective-permute-start(s32[4,128,128]{2,1,0:T(8,128)S(1)} %collective-permute-done.3.refs_1_), channel_id=1, source_target_pairs={{0,2},{1,3},{2,0},{3,1},{4,6},{5,7},{6,4},{7,5},{8,10},{9,11},{10,... | collective-permute-start | bytes 786440 | tf_op jit(solution)/shard_map/ppermute | solution.py:30
  101.2 37.4 %collective-permute-start.20 = (bf16[4,8,16,256]{3,2,1,0:T(8,128)(2,1)}, bf16[4,8,16,256]{3,2,1,0:T(8,128)(2,1)}, u32[]{:S(2)}, u32[]{:S(2)}) collective-permute-start(bf16[4,8,16,256]{3,2,1,0:T(8,128)(2,1)} %fusion.8), channel_id=1, source_target_pairs={{0,4},{1,5},{2,6},{3,7},{4,0},{5,1},{6,2},{7,3},{8,12},{9,13},{10,... | collective-permute-start | bytes 786440 | tf_op jit(solution)/shard_map/ppermute | solution.py:30
  115.2 28.2 %collective-permute-start.11 = (bf16[2,256,256]{2,1,0:T(8,128)(2,1)S(1)}, bf16[2,256,256]{2,1,0:T(8,128)(2,1)S(1)}, u32[]{:S(2)}, u32[]{:S(2)}) collective-permute-start(bf16[2,256,256]{2,1,0:T(8,128)(2,1)S(1)} %tile_products.5), channel_id=1, source_target_pairs={{8,24},{9,25},{10,26},{11,27},{12,28},{13,29},{14,30},{15,31},{16,... | collective-permute-start | bytes 786440 | tf_op jit(solution)/shard_map/ppermute | solution.py:30
  129.9 27.2 %collective-permute-start.13 = (bf16[2,256,256]{2,1,0:T(8,128)(2,1)}, bf16[2,256,256]{2,1,0:T(8,128)(2,1)S(1)}, u32[]{:S(2)}, u32[]{:S(2)}) collective-permute-start(bf16[2,256,256]{2,1,0:T(8,128)(2,1)} %get-tuple-element.18), channel_id=1, source_target_pairs={{0,16},{1,17},{2,18},{3,19},{8,24},{9,25},{10,26},{11,27},{16,32},... | collective-permute-start | bytes 786440 | tf_op jit(solution)/shard_map/ppermute | solution.py:30
  139.7 49.9 %copy-start.9 = (bf16[1024,256]{1,0:T(8,128)(2,1)S(1)}, bf16[1024,256]{1,0:T(8,128)(2,1)}, u32[]{:S(2)}) copy-start(bf16[1024,256]{1,0:T(8,128)(2,1)} %enc_mix.1) | copy-start | bytes 1572868
  139.7 49.9 %copy-start.10 = (bf16[1024,256]{1,0:T(8,128)(2,1)S(1)}, bf16[1024,256]{1,0:T(8,128)(2,1)}, u32[]{:S(2)}) copy-start(bf16[1024,256]{1,0:T(8,128)(2,1)} %dec_proj.1) | copy-start | bytes 1572868
  139.7 49.9 %copy-start.19 = (bf16[256,256]{1,0:T(8,128)(2,1)S(1)}, bf16[256,256]{1,0:T(8,128)(2,1)}, u32[]{:S(2)}) copy-start(bf16[256,256]{1,0:T(8,128)(2,1)} %node_embed.1) | copy-start | bytes 393220
  139.8 5.4 %collective-permute-start.21 = (bf16[8,16,256]{2,1,0:T(8,128)(2,1)S(1)}, bf16[8,16,256]{2,1,0:T(8,128)(2,1)S(1)}, u32[]{:S(2)}, u32[]{:S(2)}) collective-permute-start(bf16[8,16,256]{2,1,0:T(8,128)(2,1)S(1)} %get-tuple-element.33), channel_id=1, source_target_pairs={{0,64},{1,65},{2,66},{3,67},{4,68},{5,69},{6,70},{7,71},{8,72},{9,... | collective-permute-start | bytes 196616 | tf_op jit(solution)/shard_map/ppermute | solution.py:30
  141.1 6.3 %collective-permute-start.22 = (bf16[8,16,256]{2,1,0:T(8,128)(2,1)S(1)}, bf16[8,16,256]{2,1,0:T(8,128)(2,1)S(1)}, u32[]{:S(2)}, u32[]{:S(2)}) collective-permute-start(bf16[8,16,256]{2,1,0:T(8,128)(2,1)S(1)} %get-tuple-element.35), channel_id=1, source_target_pairs={{0,128},{1,129},{2,130},{3,131},{4,132},{5,133},{6,134},{7,135},{8... | collective-permute-start | bytes 196616 | tf_op jit(solution)/shard_map/ppermute | solution.py:30
  141.9 5.7 %collective-permute-start.23 = (bf16[8,16,256]{2,1,0:T(8,128)(2,1)S(1)}, bf16[8,16,256]{2,1,0:T(8,128)(2,1)S(1)}, u32[]{:S(2)}, u32[]{:S(2)}) collective-permute-start(bf16[8,16,256]{2,1,0:T(8,128)(2,1)S(1)} %get-tuple-element.34), channel_id=1, source_target_pairs={{0,192},{1,193},{2,194},{3,195},{4,196},{5,197},{6,198},{7,199},{8... | collective-permute-start | bytes 196616 | tf_op jit(solution)/shard_map/ppermute | solution.py:30
  143.4 17.2 %collective-permute-start.12 = (bf16[2,256,256]{2,1,0:T(8,128)(2,1)S(1)}, bf16[2,256,256]{2,1,0:T(8,128)(2,1)S(1)}, u32[]{:S(2)}, u32[]{:S(2)}) collective-permute-start(bf16[2,256,256]{2,1,0:T(8,128)(2,1)S(1)} %add_convert_fusion), channel_id=1, source_target_pairs={{0,8},{1,9},{2,10},{3,11},{4,12},{5,13},{6,14},{7,15},{8,0},{9,1},... | collective-permute-start | bytes 786440 | tf_op jit(solution)/shard_map/ppermute | solution.py:30
  147.6 4.8 %collective-permute-start.24 = (f32[2,16,256]{2,1,0:T(8,128)S(1)}, f32[2,16,256]{2,1,0:T(8,128)S(1)}, u32[]{:S(2)}, u32[]{:S(2)}) collective-permute-start(f32[2,16,256]{2,1,0:T(8,128)S(1)} %get-tuple-element.36), channel_id=1, source_target_pairs={{0,16},{1,17},{2,18},{3,19},{4,20},{5,21},{6,22},{7,23},{8,24},{9,... | collective-permute-start | bytes 98312 | tf_op jit(solution)/shard_map/ppermute | solution.py:30
  148.5 5.7 %collective-permute-start.25 = (f32[2,16,256]{2,1,0:T(8,128)S(1)}, f32[2,16,256]{2,1,0:T(8,128)S(1)}, u32[]{:S(2)}, u32[]{:S(2)}) collective-permute-start(f32[2,16,256]{2,1,0:T(8,128)S(1)} %get-tuple-element.38), channel_id=1, source_target_pairs={{0,32},{1,33},{2,34},{3,35},{4,36},{5,37},{6,38},{7,39},{8,40},{9,... | collective-permute-start | bytes 98312 | tf_op jit(solution)/shard_map/ppermute | solution.py:30
  151.9 5.1 %collective-permute-start.26 = (f32[2,16,256]{2,1,0:T(8,128)S(1)}, f32[2,16,256]{2,1,0:T(8,128)S(1)}, u32[]{:S(2)}, u32[]{:S(2)}) collective-permute-start(f32[2,16,256]{2,1,0:T(8,128)S(1)} %get-tuple-element.37), channel_id=1, source_target_pairs={{0,48},{1,49},{2,50},{3,51},{4,52},{5,53},{6,54},{7,55},{8,56},{9,... | collective-permute-start | bytes 98312 | tf_op jit(solution)/shard_map/ppermute | solution.py:30
  160.7 28.9 %collective-permute-start.14 = (bf16[2,256,256]{2,1,0:T(8,128)(2,1)S(1)}, bf16[2,256,256]{2,1,0:T(8,128)(2,1)S(1)}, u32[]{:S(2)}, u32[]{:S(2)}) collective-permute-start(bf16[2,256,256]{2,1,0:T(8,128)(2,1)S(1)} %multiply_convert_fusion.p0), channel_id=1, source_target_pairs={{0,1},{1,0},{2,3},{3,2},{4,5},{5,4},{6,7},{7,6},{8,9},{9,8},{10,11... | collective-permute-start | bytes 786440 | tf_op jit(solution)/shard_map/ppermute | solution.py:30
  160.8 28.8 %collective-permute-start.15 = (bf16[2,256,256]{2,1,0:T(8,128)(2,1)S(1)}, bf16[2,256,256]{2,1,0:T(8,128)(2,1)S(1)}, u32[]{:S(2)}, u32[]{:S(2)}) collective-permute-start(bf16[2,256,256]{2,1,0:T(8,128)(2,1)S(1)} %multiply_convert_fusion.p0), channel_id=1, source_target_pairs={{0,2},{1,3},{2,0},{3,1},{4,6},{5,7},{6,4},{7,5},{8,10},{9,11},{10,... | collective-permute-start | bytes 786440 | tf_op jit(solution)/shard_map/ppermute | solution.py:30
  163.2 26.4 %collective-permute-start.16 = (bf16[2,256,256]{2,1,0:T(8,128)(2,1)S(1)}, bf16[2,256,256]{2,1,0:T(8,128)(2,1)S(1)}, u32[]{:S(2)}, u32[]{:S(2)}) collective-permute-start(bf16[2,256,256]{2,1,0:T(8,128)(2,1)S(1)} %multiply_convert_fusion.p0), channel_id=1, source_target_pairs={{0,3},{1,2},{2,1},{3,0},{4,7},{5,6},{6,5},{7,4},{8,11},{9,10},{10,... | collective-permute-start | bytes 786440 | tf_op jit(solution)/shard_map/ppermute | solution.py:30
  165.2 23.8 %collective-permute-start.27 = (f32[16,256]{1,0:T(8,128)S(1)}, f32[16,256]{1,0:T(8,128)S(1)}, u32[]{:S(2)}, u32[]{:S(2)}) collective-permute-start(f32[16,256]{1,0:T(8,128)S(1)} %get-tuple-element.40), channel_id=1, source_target_pairs={{0,0},{1,1},{2,128},{3,129},{4,4},{5,5},{6,132},{7,133},{8,8},{9,9... | collective-permute-start | bytes 49160 | tf_op jit(solution)/shard_map/ppermute | solution.py:30
  167.7 21.3 %collective-permute-start.28 = (f32[16,256]{1,0:T(8,128)S(1)}, f32[16,256]{1,0:T(8,128)S(1)}, u32[]{:S(2)}, u32[]{:S(2)}) collective-permute-start(f32[16,256]{1,0:T(8,128)S(1)} %get-tuple-element.39), channel_id=1, source_target_pairs={{0,8},{1,9},{2,136},{3,137},{4,12},{5,13},{6,140},{7,141},{8,0},{9... | collective-permute-start | bytes 49160 | tf_op jit(solution)/shard_map/ppermute | solution.py:30
  (27 other events, 239.9 us)

commit v8 on v7

--- a/solution.py
+++ b/solution.py
@@ -275,7 +275,8 @@
 
     half = decoded_saved.shape[0] // 2
     dec_first = go(decoded_saved[:half], lambda b, c: (b, c ^ 2))
-    cot_pair = go(out_cotangent, lambda b, c: (b, c ^ 1))
+    cot_first = go(lax.optimization_barrier(out_cotangent)[:half], lambda b, c: (b, c ^ 1))
+    cot_second = go(lax.optimization_barrier(out_cotangent)[half:], lambda b, c: (b, c ^ 1))
     dec_second = go(lax.optimization_barrier(decoded_saved)[half:], lambda b, c: (b, c ^ 2))
 
     near = near_step(band)
@@ -311,7 +312,7 @@
     pieces = over_chan(aggregates)
     hidden_nodes, node_grad = project(chan, pieces, enc_mix, dec_proj, node_embed)
 
-    w_dec_grad = projection_gradient(go, out_cotangent, decoded_saved, cot_pair, (dec_first, dec_second), bands)
+    w_dec_grad = projection_gradient(go, out_cotangent, decoded_saved, (cot_first, cot_second), (dec_first, dec_second), bands)
     return (hidden_nodes, node_grad, w_dec_grad)
 
 
@@ -332,11 +333,12 @@
 
     half = cot.shape[0] // 2
     first = outer(cot, dec)
-    third = lax.optimization_barrier(outer(cot[:half], dec_pair[0]))
-    second = outer(cot_pair, dec)
-    fourth = lax.optimization_barrier(outer(cot_pair[:half], dec_pair[0]))
-    third = third + outer(cot[half:], dec_pair[1])
-    fourth = fourth + outer(cot_pair[half:], dec_pair[1])
+    early = lax.optimization_barrier(
+        (outer(cot_pair[0], dec[:half]), outer(cot[:half], dec_pair[0]), outer(cot_pair[0], dec_pair[0]))
+    )
+    second = early[0] + outer(cot_pair[1], dec[half:])
+    third = early[1] + outer(cot[half:], dec_pair[1])
+    fourth = early[2] + outer(cot_pair[1], dec_pair[1])
     whole = jnp.stack([first, second, third, fourth])
     halves = whole.reshape(4, 8, 2, rows, channels)
     own = lax.dynamic_index_in_dim(halves, core, 2, keepdims=False)

time: 192 us -> 175 us (0.911)
  the two profiles are of different devices: /device:TPU:4 before, /device:TPU:15 now
where the time goes in v8:
time: 175 us
  starting transfers between devices  73.1 us (42%)
  waiting for transfers between devices  54.1 us (31%)
  Pallas kernels  24.8 us (14%)
  matrix products  9.04 us (5%)
  local copies, waits for them, and re-layouts  6.63 us (4%)
  other arithmetic  5.61 us (3%)
    ppermute x30, starting transfers between devices, permute(): return lax.ppermute(x, ('band', 'chan'), pairs)  73.1 us
    ppermute x30, waiting for transfers between devices, permute(): return lax.ppermute(x, ('band', 'chan'), pairs)  54.1 us
    pallas_call x3, Pallas kernels, tile_products(): pl.pallas_call(functools.partial(products_kernel, groups, len(codes)), ou...  17.4 us
    dot_general x7, matrix products, outer(): lax.dot_general(left, right, (((0,), (0,)), ((), ())), preferred_element_...  9.04 us
    pallas_call x2, Pallas kernels, pick_tiles(): pl.pallas_call(functools.partial(pick_kernel, picks), out_shape=[jax.Shap...  6.33 us
  transfers between devices with their start and end apart: 30, of which 8 were waited for; matrix products, arithmetic and copies ran while one was open for 10% of the time, Pallas kernels for 14%

profile of v8, /device:TPU:15, one launch (start us, length us, event | category | flops | bytes accessed | tf_op | source)
XLA Modules:
  0.0 174.6 jit_solution(4252449874331097475)
XLA Ops:
  0.7 2.4 %fusion.33 = (bf16[1024,256]{1,0:T(8,128)(2,1)}, bf16[1024,256]{1,0:T(8,128)(2,1)}) fusion(bf16[2048,256]{1,0:T(8,128)(2,1)} %param.15), kind=kLoop, calls=%fused_computation.128 | loop fusion | bytes 2097152 | tf_op jit(solution)/shard_map/slice | solution.py:279
  3.1 1.7 collective-permute-start.17
  5.6 3.0 %collective-permute-start.18 = (bf16[1024,256]{1,0:T(8,128)(2,1)}, bf16[1024,256]{1,0:T(8,128)(2,1)}, u32[]{:S(2)}, u32[]{:S(2)}) collective-permute-start(bf16[1024,256]{1,0:T(8,128)(2,1)} %slice.68), channel_id=1, source_target_pairs={{0,2},{1,3},{2,0},{3,1},{4,6},{5,7},{6,4},{7,5},{8,10},{9,11},{10,... | collective-permute-start | bytes 1572872 | tf_op jit(solution)/shard_map/ppermute | solution.py:30
  9.6 3.2 %pick_tiles.3 = (s32[4,128,128]{2,1,0:T(8,128)}, s32[4,128,128]{2,1,0:T(8,128)}) custom-call(s32[2]{0:T(128)S(1)} %pad_add_fusion.1.place, s32[16,128]{1,0:T(8,128)S(1)} %bitcast.61, s32[32,128,128]{2,1,0:T(8,128)S(1)} %bitcast.58), custom_call_target="tpu_custom_call" | custom-call | flops 100000000 | bytes 1048576 | tf_op jit(solution)/shard_map/pick_tiles/pallas_call | solution.py:89
  12.7 6.5 %collective-permute-start.7 = (s32[4,128,128]{2,1,0:T(8,128)}, s32[4,128,128]{2,1,0:T(8,128)S(1)}, u32[]{:S(2)}, u32[]{:S(2)}) collective-permute-start(s32[4,128,128]{2,1,0:T(8,128)} %get-tuple-element.19), channel_id=1, source_target_pairs={{8,19},{9,18},{10,17},{11,16},{12,23},{13,22},{14,21},{15,20},{16,... | collective-permute-start | bytes 786440 | tf_op jit(solution)/shard_map/ppermute | solution.py:30
  20.8 3.2 %pick_tiles.2 = (s32[4,128,128]{2,1,0:T(8,128)S(1)}, s32[4,128,128]{2,1,0:T(8,128)S(1)}, s32[8,128,128]{2,1,0:T(8,128)S(1)}) custom-call(s32[2]{0:T(128)S(1)} %pad_add_fusion.1.place, s32[16,128]{1,0:T(8,128)S(1)} %bitcast.62, s32[32,128,128]{2,1,0:T(8,128)S(1)} %bitcast.59), custom_call_target="tpu_custom_call" | custom-call | flops 100000000 | bytes 2097152 | tf_op jit(solution)/shard_map/pick_tiles/pallas_call | solution.py:89
  24.5 2.3 %collective-permute-done.17 = bf16[1024,256]{1,0:T(8,128)(2,1)} collective-permute-done((bf16[1024,256]{1,0:T(8,128)(2,1)}, bf16[1024,256]{1,0:T(8,128)(2,1)}, u32[]{:S(2)}, u32[]{:S(2)}) %collective-permute-start.17) | collective-permute-done | bytes 524320 | tf_op jit(solution)/shard_map/ppermute | solution.py:30
  26.8 2.3 %collective-permute-start.1 = (bf16[16,128,256]{2,1,0:T(8,128)(2,1)}, bf16[16,128,256]{2,1,0:T(8,128)(2,1)}, u32[]{:S(2)}, u32[]{:S(2)}) collective-permute-start(bf16[16,128,256]{2,1,0:T(8,128)(2,1)} %bitcast.4.refs_3_.refs_5_), channel_id=1, source_target_pairs={{0,4},{1,5},{2,6},{3,7},{4,0},{5,1},{6,2},{7,3},{8,12},{9,13},{10,... | collective-permute-start | bytes 3145736 | tf_op jit(solution)/shard_map/ppermute | solution.py:30
  30.5 3.8 %collective-permute-start.2 = (bf16[16,128,256]{2,1,0:T(8,128)(2,1)S(1)}, bf16[16,128,256]{2,1,0:T(8,128)(2,1)}, u32[]{:S(2)}, u32[]{:S(2)}) collective-permute-start(bf16[16,128,256]{2,1,0:T(8,128)(2,1)S(1)} %bitcast.54), channel_id=1, source_target_pairs={{0,4},{1,5},{2,6},{3,7},{4,0},{5,1},{6,2},{7,3},{8,12},{9,13},{10,... | collective-permute-start | bytes 3145736 | tf_op jit(solution)/shard_map/ppermute | solution.py:30
  37.2 12.0 %collective-permute-done.19 = bf16[1024,256]{1,0:T(8,128)(2,1)} collective-permute-done((bf16[1024,256]{1,0:T(8,128)(2,1)}, bf16[1024,256]{1,0:T(8,128)(2,1)}, u32[]{:S(2)}, u32[]{:S(2)}) %collective-permute-start.19) | collective-permute-done | bytes 524320 | tf_op jit(solution)/shard_map/ppermute | solution.py:30
  49.3 4.9 %collective-permute-start.3 = (s32[4,128,128]{2,1,0:T(8,128)}, s32[4,128,128]{2,1,0:T(8,128)}, u32[]{:S(2)}, u32[]{:S(2)}) collective-permute-start(s32[4,128,128]{2,1,0:T(8,128)} %get-tuple-element.17), channel_id=1, source_target_pairs={{0,11},{1,10},{2,9},{3,8},{4,15},{5,14},{6,13},{7,12},{8,3},{9,2},... | collective-permute-start | bytes 786440 | tf_op jit(solution)/shard_map/ppermute | solution.py:30
  55.5 1.5 fusion.36
  59.5 4.4 %collective-permute-start.21 = (bf16[4,8,16,256]{3,2,1,0:T(8,128)(2,1)}, bf16[4,8,16,256]{3,2,1,0:T(8,128)(2,1)}, u32[]{:S(2)}, u32[]{:S(2)}) collective-permute-start(bf16[4,8,16,256]{3,2,1,0:T(8,128)(2,1)} %fusion.6), channel_id=1, source_target_pairs={{0,4},{1,5},{2,6},{3,7},{4,0},{5,1},{6,2},{7,3},{8,12},{9,13},{10,... | collective-permute-start | bytes 786440 | tf_op jit(solution)/shard_map/ppermute | solution.py:30
  64.6 8.8 %collective-permute-start.10 = (s32[4,128,128]{2,1,0:T(8,128)}, s32[4,128,128]{2,1,0:T(8,128)}, u32[]{:S(2)}, u32[]{:S(2)}) collective-permute-start(s32[4,128,128]{2,1,0:T(8,128)} %broadcast_select_fusion), channel_id=1, source_target_pairs={{1,2},{2,1},{5,6},{6,5},{8,19},{9,10},{10,9},{11,16},{12,23},{13,1... | collective-permute-start | bytes 786440 | tf_op jit(solution)/shard_map/ppermute | solution.py:30
  75.2 5.2 %collective-permute-done.10.refs_4_ = s32[4,128,128]{2,1,0:T(8,128)} collective-permute-done((s32[4,128,128]{2,1,0:T(8,128)}, s32[4,128,128]{2,1,0:T(8,128)}, u32[]{:S(2)}, u32[]{:S(2)}) %collective-permute-start.10) | collective-permute-done | bytes 262176 | tf_op jit(solution)/shard_map/ppermute | solution.py:30
  80.4 3.2 %collective-permute-start = (s32[8,128,128]{2,1,0:T(8,128)}, s32[8,128,128]{2,1,0:T(8,128)S(1)}, u32[]{:S(2)}, u32[]{:S(2)}) collective-permute-start(s32[8,128,128]{2,1,0:T(8,128)} %copy-done.9), channel_id=1, source_target_pairs={{4,20},{5,21},{6,22},{7,23},{12,28},{13,29},{14,30},{15,31},{16,0}... | collective-permute-start | bytes 1572872 | tf_op jit(solution)/shard_map/ppermute | solution.py:30
  85.0 2.9 %collective-permute-done.9.refs_3_ = s32[4,128,128]{2,1,0:T(8,128)S(1)} collective-permute-done((s32[4,128,128]{2,1,0:T(8,128)S(1)}, s32[4,128,128]{2,1,0:T(8,128)S(1)}, u32[]{:S(2)}, u32[]{:S(2)}) %collective-permute-start.9) | collective-permute-done | bytes 262176 | tf_op jit(solution)/shard_map/ppermute | solution.py:30
  89.1 1.8 %collective-permute-start.24 = (bf16[8,16,256]{2,1,0:T(8,128)(2,1)S(1)}, bf16[8,16,256]{2,1,0:T(8,128)(2,1)S(1)}, u32[]{:S(2)}, u32[]{:S(2)}) collective-permute-start(bf16[8,16,256]{2,1,0:T(8,128)(2,1)S(1)} %get-tuple-element.42), channel_id=1, source_target_pairs={{0,192},{1,193},{2,194},{3,195},{4,196},{5,197},{6,198},{7,199},{8... | collective-permute-start | bytes 196616 | tf_op jit(solution)/shard_map/ppermute | solution.py:30
  91.9 7.1 %collective-permute-start.6 = (s32[4,128,128]{2,1,0:T(8,128)S(1)}, s32[4,128,128]{2,1,0:T(8,128)S(1)}, u32[]{:S(2)}, u32[]{:S(2)}) collective-permute-start(s32[4,128,128]{2,1,0:T(8,128)S(1)} %broadcast_select_fusion.1), channel_id=1, source_target_pairs={{0,11},{1,2},{2,1},{3,8},{4,15},{5,6},{6,5},{7,12},{8,3},{9,10},{1... | collective-permute-start | bytes 786440 | tf_op jit(solution)/shard_map/ppermute | solution.py:30
  99.0 4.9 %tile_products.5 = bf16[2,256,256]{2,1,0:T(8,128)(2,1)S(1)} custom-call(s32[5,16]{1,0:T(8,128)S(1)} %stack.27.refs_0_, s32[4,128,128]{2,1,0:T(8,128)S(1)} %collective-permute-done.7.refs_1_, s32[4,128,128]{2,1,0:T(8,128)S(1)} %collective-permute-done.8.refs_2_, s32[4,128,128]{2,1,0:T(8,128)S(1)} %collective-permute-done.9.refs_3_, ...), custom_call_target="tpu_custom_call" | custom-call | flops 268435456 | bytes 3145728 | tf_op jit(solution)/shard_map/tile_products/pallas_call | solution.py:175
  104.0 2.3 %collective-permute-start.5 = (s32[4,128,128]{2,1,0:T(8,128)}, s32[4,128,128]{2,1,0:T(8,128)S(1)}, u32[]{:S(2)}, u32[]{:S(2)}) collective-permute-start(s32[4,128,128]{2,1,0:T(8,128)} %collective-permute-done.3.refs_1_), channel_id=1, source_target_pairs={{0,2},{1,3},{2,0},{3,1},{4,6},{5,7},{6,4},{7,5},{8,10},{9,11},{10,... | collective-permute-start | bytes 786440 | tf_op jit(solution)/shard_map/ppermute | solution.py:30
  106.4 2.2 %collective-permute-start.11 = (bf16[2,256,256]{2,1,0:T(8,128)(2,1)S(1)}, bf16[2,256,256]{2,1,0:T(8,128)(2,1)S(1)}, u32[]{:S(2)}, u32[]{:S(2)}) collective-permute-start(bf16[2,256,256]{2,1,0:T(8,128)(2,1)S(1)} %tile_products.5), channel_id=1, source_target_pairs={{8,24},{9,25},{10,26},{11,27},{12,28},{13,29},{14,30},{15,31},{16,... | collective-permute-start | bytes 786440 | tf_op jit(solution)/shard_map/ppermute | solution.py:30
  108.7 7.5 %tile_products.3 = (bf16[2,256,256]{2,1,0:T(8,128)(2,1)}, f32[2,256,256]{2,1,0:T(8,128)S(1)}) custom-call(s32[5,24]{1,0:T(8,128)S(1)} %pad_add_fusion.refs_0_, s32[8,128,128]{2,1,0:T(8,128)S(1)} %collective-permute-done.refs_1_, s32[32,128,128]{2,1,0:T(8,128)S(1)} %bitcast.60, bf16[16,128,256]{2,1,0:T(8,128)(2,1)} %bitcast.4.refs_3_.refs_5_, ...), custom_call_target="tpu_custom_call" | custom-call | flops 402653184 | bytes 4718592 | tf_op jit(solution)/shard_map/tile_products/pallas_call | solution.py:175
  117.0 3.9 %collective-permute-start.13 = (bf16[2,256,256]{2,1,0:T(8,128)(2,1)}, bf16[2,256,256]{2,1,0:T(8,128)(2,1)}, u32[]{:S(2)}, u32[]{:S(2)}) collective-permute-start(bf16[2,256,256]{2,1,0:T(8,128)(2,1)} %get-tuple-element.21), channel_id=1, source_target_pairs={{0,16},{1,17},{2,18},{3,19},{8,24},{9,25},{10,26},{11,27},{16,32},... | collective-permute-start | bytes 786440 | tf_op jit(solution)/shard_map/ppermute | solution.py:30
  120.9 4.9 %tile_products.4 = f32[2,256,256]{2,1,0:T(8,128)S(1)} custom-call(s32[5,16]{1,0:T(8,128)S(1)} %stack.26.refs_0_, s32[4,128,128]{2,1,0:T(8,128)} %collective-permute-done.3.refs_1_, s32[4,128,128]{2,1,0:T(8,128)S(1)} %collective-permute-done.4.refs_2_, s32[4,128,128]{2,1,0:T(8,128)S(1)} %collective-permute-done.5.refs_3_, ...), custom_call_target="tpu_custom_call" | custom-call | flops 268435456 | bytes 3145728 | tf_op jit(solution)/shard_map/tile_products/pallas_call | solution.py:175
  126.1 2.2 %collective-permute-start.25 = (f32[2,16,256]{2,1,0:T(8,128)S(1)}, f32[2,16,256]{2,1,0:T(8,128)S(1)}, u32[]{:S(2)}, u32[]{:S(2)}) collective-permute-start(f32[2,16,256]{2,1,0:T(8,128)S(1)} %get-tuple-element.44), channel_id=1, source_target_pairs={{0,16},{1,17},{2,18},{3,19},{4,20},{5,21},{6,22},{7,23},{8,24},{9,... | collective-permute-start | bytes 98312 | tf_op jit(solution)/shard_map/ppermute | solution.py:30
  129.7 3.0 %collective-permute-done.26 = f32[2,16,256]{2,1,0:T(8,128)S(1)} collective-permute-done((f32[2,16,256]{2,1,0:T(8,128)S(1)}, f32[2,16,256]{2,1,0:T(8,128)S(1)}, u32[]{:S(2)}, u32[]{:S(2)}) %collective-permute-start.26) | collective-permute-done | bytes 32800 | tf_op jit(solution)/shard_map/ppermute | solution.py:30
  132.6 5.3 %collective-permute-done.12 = bf16[2,256,256]{2,1,0:T(8,128)(2,1)S(1)} collective-permute-done((bf16[2,256,256]{2,1,0:T(8,128)(2,1)S(1)}, bf16[2,256,256]{2,1,0:T(8,128)(2,1)S(1)}, u32[]{:S(2)}, u32[]{:S(2)}) %collective-permute-start.12) | collective-permute-done | bytes 262176 | tf_op jit(solution)/shard_map/ppermute | solution.py:30
  139.0 1.6 collective-permute-start.14
  140.6 2.2 %collective-permute-start.16 = (bf16[2,256,256]{2,1,0:T(8,128)(2,1)S(1)}, bf16[2,256,256]{2,1,0:T(8,128)(2,1)S(1)}, u32[]{:S(2)}, u32[]{:S(2)}) collective-permute-start(bf16[2,256,256]{2,1,0:T(8,128)(2,1)S(1)} %multiply_convert_fusion.p0), channel_id=1, source_target_pairs={{0,3},{1,2},{2,1},{3,0},{4,7},{5,6},{6,5},{7,4},{8,11},{9,10},{10,... | collective-permute-start | bytes 786440 | tf_op jit(solution)/shard_map/ppermute | solution.py:30
  142.8 7.4 %collective-permute-start.28 = (f32[16,256]{1,0:T(8,128)S(1)}, f32[16,256]{1,0:T(8,128)S(1)}, u32[]{:S(2)}, u32[]{:S(2)}) collective-permute-start(f32[16,256]{1,0:T(8,128)S(1)} %get-tuple-element.48), channel_id=1, source_target_pairs={{0,0},{1,1},{2,128},{3,129},{4,4},{5,5},{6,132},{7,133},{8,8},{9,9... | collective-permute-start | bytes 49160 | tf_op jit(solution)/shard_map/ppermute | solution.py:30
  150.3 22.5 %collective-permute-done.28 = f32[16,256]{1,0:T(8,128)S(1)} collective-permute-done((f32[16,256]{1,0:T(8,128)S(1)}, f32[16,256]{1,0:T(8,128)S(1)}, u32[]{:S(2)}, u32[]{:S(2)}) %collective-permute-start.28) | collective-permute-done | bytes 16416 | tf_op jit(solution)/shard_map/ppermute | solution.py:30
  (119 shorter events, 23.1 us)
Async XLA Ops:
  3.1 23.7 %collective-permute-start.17 = (bf16[1024,256]{1,0:T(8,128)(2,1)}, bf16[1024,256]{1,0:T(8,128)(2,1)}, u32[]{:S(2)}, u32[]{:S(2)}) collective-permute-start(bf16[1024,256]{1,0:T(8,128)(2,1)} %get-tuple-element.40), channel_id=1, source_target_pairs={{0,1},{1,0},{2,3},{3,2},{4,5},{5,4},{6,7},{7,6},{8,9},{9,8},{10,11... | collective-permute-start | bytes 1572872 | tf_op jit(solution)/shard_map/ppermute | solution.py:30
  5.6 24.9 %collective-permute-start.18 = (bf16[1024,256]{1,0:T(8,128)(2,1)}, bf16[1024,256]{1,0:T(8,128)(2,1)}, u32[]{:S(2)}, u32[]{:S(2)}) collective-permute-start(bf16[1024,256]{1,0:T(8,128)(2,1)} %slice.68), channel_id=1, source_target_pairs={{0,2},{1,3},{2,0},{3,1},{4,6},{5,7},{6,4},{7,5},{8,10},{9,11},{10,... | collective-permute-start | bytes 1572872 | tf_op jit(solution)/shard_map/ppermute | solution.py:30
  8.6 40.6 %collective-permute-start.19 = (bf16[1024,256]{1,0:T(8,128)(2,1)}, bf16[1024,256]{1,0:T(8,128)(2,1)}, u32[]{:S(2)}, u32[]{:S(2)}) collective-permute-start(bf16[1024,256]{1,0:T(8,128)(2,1)} %get-tuple-element.39), channel_id=1, source_target_pairs={{0,1},{1,0},{2,3},{3,2},{4,5},{5,4},{6,7},{7,6},{8,9},{9,8},{10,11... | collective-permute-start | bytes 1572872 | tf_op jit(solution)/shard_map/ppermute | solution.py:30
  9.5 46.0 %collective-permute-start.20 = (bf16[1024,256]{1,0:T(8,128)(2,1)}, bf16[1024,256]{1,0:T(8,128)(2,1)}, u32[]{:S(2)}, u32[]{:S(2)}) collective-permute-start(bf16[1024,256]{1,0:T(8,128)(2,1)} %slice.78), channel_id=1, source_target_pairs={{0,2},{1,3},{2,0},{3,1},{4,6},{5,7},{6,4},{7,5},{8,10},{9,11},{10,... | collective-permute-start | bytes 1572872 | tf_op jit(solution)/shard_map/ppermute | solution.py:30
  12.7 51.1 %collective-permute-start.7 = (s32[4,128,128]{2,1,0:T(8,128)}, s32[4,128,128]{2,1,0:T(8,128)S(1)}, u32[]{:S(2)}, u32[]{:S(2)}) collective-permute-start(s32[4,128,128]{2,1,0:T(8,128)} %get-tuple-element.19), channel_id=1, source_target_pairs={{8,19},{9,18},{10,17},{11,16},{12,23},{13,22},{14,21},{15,20},{16,... | collective-permute-start | bytes 786440 | tf_op jit(solution)/shard_map/ppermute | solution.py:30
  26.8 62.3 %collective-permute-start.1 = (bf16[16,128,256]{2,1,0:T(8,128)(2,1)}, bf16[16,128,256]{2,1,0:T(8,128)(2,1)}, u32[]{:S(2)}, u32[]{:S(2)}) collective-permute-start(bf16[16,128,256]{2,1,0:T(8,128)(2,1)} %bitcast.4.refs_3_.refs_5_), channel_id=1, source_target_pairs={{0,4},{1,5},{2,6},{3,7},{4,0},{5,1},{6,2},{7,3},{8,12},{9,13},{10,... | collective-permute-start | bytes 3145736 | tf_op jit(solution)/shard_map/ppermute | solution.py:30
  30.5 61.4 %collective-permute-start.2 = (bf16[16,128,256]{2,1,0:T(8,128)(2,1)S(1)}, bf16[16,128,256]{2,1,0:T(8,128)(2,1)}, u32[]{:S(2)}, u32[]{:S(2)}) collective-permute-start(bf16[16,128,256]{2,1,0:T(8,128)(2,1)S(1)} %bitcast.54), channel_id=1, source_target_pairs={{0,4},{1,5},{2,6},{3,7},{4,0},{5,1},{6,2},{7,3},{8,12},{9,13},{10,... | collective-permute-start | bytes 3145736 | tf_op jit(solution)/shard_map/ppermute | solution.py:30
  49.3 24.4 %collective-permute-start.3 = (s32[4,128,128]{2,1,0:T(8,128)}, s32[4,128,128]{2,1,0:T(8,128)}, u32[]{:S(2)}, u32[]{:S(2)}) collective-permute-start(s32[4,128,128]{2,1,0:T(8,128)} %get-tuple-element.17), channel_id=1, source_target_pairs={{0,11},{1,10},{2,9},{3,8},{4,15},{5,14},{6,13},{7,12},{8,3},{9,2},... | collective-permute-start | bytes 786440 | tf_op jit(solution)/shard_map/ppermute | solution.py:30
  59.5 14.2 %collective-permute-start.21 = (bf16[4,8,16,256]{3,2,1,0:T(8,128)(2,1)}, bf16[4,8,16,256]{3,2,1,0:T(8,128)(2,1)}, u32[]{:S(2)}, u32[]{:S(2)}) collective-permute-start(bf16[4,8,16,256]{3,2,1,0:T(8,128)(2,1)} %fusion.6), channel_id=1, source_target_pairs={{0,4},{1,5},{2,6},{3,7},{4,0},{5,1},{6,2},{7,3},{8,12},{9,13},{10,... | collective-permute-start | bytes 786440 | tf_op jit(solution)/shard_map/ppermute | solution.py:30
  64.6 15.8 %collective-permute-start.10 = (s32[4,128,128]{2,1,0:T(8,128)}, s32[4,128,128]{2,1,0:T(8,128)}, u32[]{:S(2)}, u32[]{:S(2)}) collective-permute-start(s32[4,128,128]{2,1,0:T(8,128)} %broadcast_select_fusion), channel_id=1, source_target_pairs={{1,2},{2,1},{5,6},{6,5},{8,19},{9,10},{10,9},{11,16},{12,23},{13,1... | collective-permute-start | bytes 786440 | tf_op jit(solution)/shard_map/ppermute | solution.py:30
  73.6 10.9 %collective-permute-start.8 = (s32[4,128,128]{2,1,0:T(8,128)S(1)}, s32[4,128,128]{2,1,0:T(8,128)S(1)}, u32[]{:S(2)}, u32[]{:S(2)}) collective-permute-start(s32[4,128,128]{2,1,0:T(8,128)S(1)} %collective-permute-done.7.refs_1_), channel_id=1, source_target_pairs={{0,1},{1,0},{2,3},{3,2},{4,5},{5,4},{6,7},{7,6},{8,9},{9,8},{10,11... | collective-permute-start | bytes 786440 | tf_op jit(solution)/shard_map/ppermute | solution.py:30
  73.7 14.2 %collective-permute-start.9 = (s32[4,128,128]{2,1,0:T(8,128)S(1)}, s32[4,128,128]{2,1,0:T(8,128)S(1)}, u32[]{:S(2)}, u32[]{:S(2)}) collective-permute-start(s32[4,128,128]{2,1,0:T(8,128)S(1)} %collective-permute-done.7.refs_1_), channel_id=1, source_target_pairs={{0,2},{1,3},{2,0},{3,1},{4,6},{5,7},{6,4},{7,5},{8,10},{9,11},{10,... | collective-permute-start | bytes 786440 | tf_op jit(solution)/shard_map/ppermute | solution.py:30
  80.4 28.2 %collective-permute-start = (s32[8,128,128]{2,1,0:T(8,128)}, s32[8,128,128]{2,1,0:T(8,128)S(1)}, u32[]{:S(2)}, u32[]{:S(2)}) collective-permute-start(s32[8,128,128]{2,1,0:T(8,128)} %copy-done.9), channel_id=1, source_target_pairs={{4,20},{5,21},{6,22},{7,23},{12,28},{13,29},{14,30},{15,31},{16,0}... | collective-permute-start | bytes 1572872 | tf_op jit(solution)/shard_map/ppermute | solution.py:30
  84.5 19.4 %collective-permute-start.22 = (bf16[8,16,256]{2,1,0:T(8,128)(2,1)S(1)}, bf16[8,16,256]{2,1,0:T(8,128)(2,1)S(1)}, u32[]{:S(2)}, u32[]{:S(2)}) collective-permute-start(bf16[8,16,256]{2,1,0:T(8,128)(2,1)S(1)} %get-tuple-element.41), channel_id=1, source_target_pairs={{0,64},{1,65},{2,66},{3,67},{4,68},{5,69},{6,70},{7,71},{8,72},{9,... | collective-permute-start | bytes 196616 | tf_op jit(solution)/shard_map/ppermute | solution.py:30
  88.0 16.1 %collective-permute-start.23 = (bf16[8,16,256]{2,1,0:T(8,128)(2,1)S(1)}, bf16[8,16,256]{2,1,0:T(8,128)(2,1)S(1)}, u32[]{:S(2)}, u32[]{:S(2)}) collective-permute-start(bf16[8,16,256]{2,1,0:T(8,128)(2,1)S(1)} %get-tuple-element.43), channel_id=1, source_target_pairs={{0,128},{1,129},{2,130},{3,131},{4,132},{5,133},{6,134},{7,135},{8... | collective-permute-start | bytes 196616 | tf_op jit(solution)/shard_map/ppermute | solution.py:30
  89.1 17.3 %collective-permute-start.24 = (bf16[8,16,256]{2,1,0:T(8,128)(2,1)S(1)}, bf16[8,16,256]{2,1,0:T(8,128)(2,1)S(1)}, u32[]{:S(2)}, u32[]{:S(2)}) collective-permute-start(bf16[8,16,256]{2,1,0:T(8,128)(2,1)S(1)} %get-tuple-element.42), channel_id=1, source_target_pairs={{0,192},{1,193},{2,194},{3,195},{4,196},{5,197},{6,198},{7,199},{8... | collective-permute-start | bytes 196616 | tf_op jit(solution)/shard_map/ppermute | solution.py:30
  91.9 29.0 %collective-permute-start.6 = (s32[4,128,128]{2,1,0:T(8,128)S(1)}, s32[4,128,128]{2,1,0:T(8,128)S(1)}, u32[]{:S(2)}, u32[]{:S(2)}) collective-permute-start(s32[4,128,128]{2,1,0:T(8,128)S(1)} %broadcast_select_fusion.1), channel_id=1, source_target_pairs={{0,11},{1,2},{2,1},{3,8},{4,15},{5,6},{6,5},{7,12},{8,3},{9,10},{1... | collective-permute-start | bytes 786440 | tf_op jit(solution)/shard_map/ppermute | solution.py:30
  103.9 17.0 %collective-permute-start.4 = (s32[4,128,128]{2,1,0:T(8,128)}, s32[4,128,128]{2,1,0:T(8,128)S(1)}, u32[]{:S(2)}, u32[]{:S(2)}) collective-permute-start(s32[4,128,128]{2,1,0:T(8,128)} %collective-permute-done.3.refs_1_), channel_id=1, source_target_pairs={{0,1},{1,0},{2,3},{3,2},{4,5},{5,4},{6,7},{7,6},{8,9},{9,8},{10,11... | collective-permute-start | bytes 786440 | tf_op jit(solution)/shard_map/ppermute | solution.py:30
  104.0 16.9 %collective-permute-start.5 = (s32[4,128,128]{2,1,0:T(8,128)}, s32[4,128,128]{2,1,0:T(8,128)S(1)}, u32[]{:S(2)}, u32[]{:S(2)}) collective-permute-start(s32[4,128,128]{2,1,0:T(8,128)} %collective-permute-done.3.refs_1_), channel_id=1, source_target_pairs={{0,2},{1,3},{2,0},{3,1},{4,6},{5,7},{6,4},{7,5},{8,10},{9,11},{10,... | collective-permute-start | bytes 786440 | tf_op jit(solution)/shard_map/ppermute | solution.py:30
  106.4 19.5 %collective-permute-start.11 = (bf16[2,256,256]{2,1,0:T(8,128)(2,1)S(1)}, bf16[2,256,256]{2,1,0:T(8,128)(2,1)S(1)}, u32[]{:S(2)}, u32[]{:S(2)}) collective-permute-start(bf16[2,256,256]{2,1,0:T(8,128)(2,1)S(1)} %tile_products.5), channel_id=1, source_target_pairs={{8,24},{9,25},{10,26},{11,27},{12,28},{13,29},{14,30},{15,31},{16,... | collective-permute-start | bytes 786440 | tf_op jit(solution)/shard_map/ppermute | solution.py:30
  117.0 15.7 %collective-permute-start.13 = (bf16[2,256,256]{2,1,0:T(8,128)(2,1)}, bf16[2,256,256]{2,1,0:T(8,128)(2,1)}, u32[]{:S(2)}, u32[]{:S(2)}) collective-permute-start(bf16[2,256,256]{2,1,0:T(8,128)(2,1)} %get-tuple-element.21), channel_id=1, source_target_pairs={{0,16},{1,17},{2,18},{3,19},{8,24},{9,25},{10,26},{11,27},{16,32},... | collective-permute-start | bytes 786440 | tf_op jit(solution)/shard_map/ppermute | solution.py:30
  125.9 47.6 %copy-start.2 = (bf16[1024,256]{1,0:T(8,128)(2,1)S(1)}, bf16[1024,256]{1,0:T(8,128)(2,1)}, u32[]{:S(2)}) copy-start(bf16[1024,256]{1,0:T(8,128)(2,1)} %enc_mix.1) | copy-start | bytes 1572868
  125.9 47.6 %copy-start.3 = (bf16[1024,256]{1,0:T(8,128)(2,1)S(1)}, bf16[1024,256]{1,0:T(8,128)(2,1)}, u32[]{:S(2)}) copy-start(bf16[1024,256]{1,0:T(8,128)(2,1)} %dec_proj.1) | copy-start | bytes 1572868
  126.0 12.0 %collective-permute-start.12 = (bf16[2,256,256]{2,1,0:T(8,128)(2,1)S(1)}, bf16[2,256,256]{2,1,0:T(8,128)(2,1)S(1)}, u32[]{:S(2)}, u32[]{:S(2)}) collective-permute-start(bf16[2,256,256]{2,1,0:T(8,128)(2,1)S(1)} %add_convert_fusion), channel_id=1, source_target_pairs={{0,8},{1,9},{2,10},{3,11},{4,12},{5,13},{6,14},{7,15},{8,0},{9,1},... | collective-permute-start | bytes 786440 | tf_op jit(solution)/shard_map/ppermute | solution.py:30
  126.1 3.5 %collective-permute-start.25 = (f32[2,16,256]{2,1,0:T(8,128)S(1)}, f32[2,16,256]{2,1,0:T(8,128)S(1)}, u32[]{:S(2)}, u32[]{:S(2)}) collective-permute-start(f32[2,16,256]{2,1,0:T(8,128)S(1)} %get-tuple-element.44), channel_id=1, source_target_pairs={{0,16},{1,17},{2,18},{3,19},{4,20},{5,21},{6,22},{7,23},{8,24},{9,... | collective-permute-start | bytes 98312 | tf_op jit(solution)/shard_map/ppermute | solution.py:30
  128.3 4.3 %collective-permute-start.26 = (f32[2,16,256]{2,1,0:T(8,128)S(1)}, f32[2,16,256]{2,1,0:T(8,128)S(1)}, u32[]{:S(2)}, u32[]{:S(2)}) collective-permute-start(f32[2,16,256]{2,1,0:T(8,128)S(1)} %get-tuple-element.46), channel_id=1, source_target_pairs={{0,32},{1,33},{2,34},{3,35},{4,36},{5,37},{6,38},{7,39},{8,40},{9,... | collective-permute-start | bytes 98312 | tf_op jit(solution)/shard_map/ppermute | solution.py:30
  129.3 3.4 %collective-permute-start.27 = (f32[2,16,256]{2,1,0:T(8,128)S(1)}, f32[2,16,256]{2,1,0:T(8,128)S(1)}, u32[]{:S(2)}, u32[]{:S(2)}) collective-permute-start(f32[2,16,256]{2,1,0:T(8,128)S(1)} %get-tuple-element.45), channel_id=1, source_target_pairs={{0,48},{1,49},{2,50},{3,51},{4,52},{5,53},{6,54},{7,55},{8,56},{9,... | collective-permute-start | bytes 98312 | tf_op jit(solution)/shard_map/ppermute | solution.py:30
  139.0 34.4 %collective-permute-start.14 = (bf16[2,256,256]{2,1,0:T(8,128)(2,1)S(1)}, bf16[2,256,256]{2,1,0:T(8,128)(2,1)S(1)}, u32[]{:S(2)}, u32[]{:S(2)}) collective-permute-start(bf16[2,256,256]{2,1,0:T(8,128)(2,1)S(1)} %multiply_convert_fusion.p0), channel_id=1, source_target_pairs={{0,1},{1,0},{2,3},{3,2},{4,5},{5,4},{6,7},{7,6},{8,9},{9,8},{10,11... | collective-permute-start | bytes 786440 | tf_op jit(solution)/shard_map/ppermute | solution.py:30
  140.6 32.8 %collective-permute-start.15 = (bf16[2,256,256]{2,1,0:T(8,128)(2,1)S(1)}, bf16[2,256,256]{2,1,0:T(8,128)(2,1)S(1)}, u32[]{:S(2)}, u32[]{:S(2)}) collective-permute-start(bf16[2,256,256]{2,1,0:T(8,128)(2,1)S(1)} %multiply_convert_fusion.p0), channel_id=1, source_target_pairs={{0,2},{1,3},{2,0},{3,1},{4,6},{5,7},{6,4},{7,5},{8,10},{9,11},{10,... | collective-permute-start | bytes 786440 | tf_op jit(solution)/shard_map/ppermute | solution.py:30
  140.6 32.8 %collective-permute-start.16 = (bf16[2,256,256]{2,1,0:T(8,128)(2,1)S(1)}, bf16[2,256,256]{2,1,0:T(8,128)(2,1)S(1)}, u32[]{:S(2)}, u32[]{:S(2)}) collective-permute-start(bf16[2,256,256]{2,1,0:T(8,128)(2,1)S(1)} %multiply_convert_fusion.p0), channel_id=1, source_target_pairs={{0,3},{1,2},{2,1},{3,0},{4,7},{5,6},{6,5},{7,4},{8,11},{9,10},{10,... | collective-permute-start | bytes 786440 | tf_op jit(solution)/shard_map/ppermute | solution.py:30
  142.8 30.0 %collective-permute-start.28 = (f32[16,256]{1,0:T(8,128)S(1)}, f32[16,256]{1,0:T(8,128)S(1)}, u32[]{:S(2)}, u32[]{:S(2)}) collective-permute-start(f32[16,256]{1,0:T(8,128)S(1)} %get-tuple-element.48), channel_id=1, source_target_pairs={{0,0},{1,1},{2,128},{3,129},{4,4},{5,5},{6,132},{7,133},{8,8},{9,9... | collective-permute-start | bytes 49160 | tf_op jit(solution)/shard_map/ppermute | solution.py:30
  150.2 22.6 %collective-permute-start.29 = (f32[16,256]{1,0:T(8,128)S(1)}, f32[16,256]{1,0:T(8,128)S(1)}, u32[]{:S(2)}, u32[]{:S(2)}) collective-permute-start(f32[16,256]{1,0:T(8,128)S(1)} %get-tuple-element.47), channel_id=1, source_target_pairs={{0,8},{1,9},{2,136},{3,137},{4,12},{5,13},{6,140},{7,141},{8,0},{9... | collective-permute-start | bytes 49160 | tf_op jit(solution)/shard_map/ppermute | solution.py:30
  (15 other events, 213.5 us)
